TPU v7x, 256 devices: a whole 4x4x8 slice. The times are simulated.
256 devices in a mesh: seg: 64 (over z, x, core), bin: 4 (over y).
Axes of the slice: x: 4, y: 4, z: 8, core: 2. Of those that a mesh axis runs over, the one named last changes fastest.
Arguments:
- magnet_real: bfloat16 [512, 8, 32768], P('seg', None, 'bin'), may hold values from -8 to 8
- magnet_imag: bfloat16 [512, 8, 32768], P('seg', None, 'bin'), may hold values from -8 to 8
- detector_real: bfloat16 [512, 2, 32768], P('seg', None, 'bin'), may hold values from -8 to 8
- detector_imag: bfloat16 [512, 2, 32768], P('seg', None, 'bin'), may hold values from -8 to 8
- valid: int32 [512], P('seg'), may hold values 0 or 1
- intersection: float32 [32768], P('bin'), may hold values from 0.1 to 1
Outputs:
- cleaned_real: float32 [512, 32768], P('seg', 'bin')
- cleaned_imag: float32 [512, 32768], P('seg', 'bin')
- estimate: float32 [512], P('seg')
Inputs may be any that keep to these rules, and one draw needn't show every extreme that they name: `valid`: 1 keeps a segment in the spectral sums, 0 vetoes it.
All inputs are finite; a program needn't handle non-finite values. No bound on the sum of `valid` on one device may be relied on, other than what follows from the above.
Results may differ from a plain program's by a relative error of at most 0.0005.
Values sent between devices are 32-bit elements; how exact they have to be, the bound alone decides.
No kernel may reach another device: no remote copies, remote signals or barrier semaphores. Data moves between devices by JAX's collectives and lax.ppermute only.
A program may use at most 64 MiB of HBM per device.

v0:
```python
import jax
import jax.numpy as jnp
from jax import lax
from jax.sharding import Mesh
from jax.sharding import PartitionSpec as P

SEG = ("seg_0", "seg_1", "seg_2")


def summed_rows(shard, axes, dim):
    for axis in axes:
        shard = lax.psum_scatter(shard, axis, scatter_dimension=dim, tiled=True)
    return shard


def sent_together(arrays, axis, dim, along):
    both = jnp.concatenate(arrays, axis=along)
    whole, at, gathered = (lax.all_gather(both, axis, axis=dim, tiled=True), 0, [])
    for a in arrays:
        gathered.append(lax.slice_in_dim(whole, at, at + a.shape[along], axis=along))
        at += a.shape[along]
    return tuple(gathered)


def wiener_solve(s_real, s_imag, p_real, p_imag):
    channels = s_real.shape[0]
    matrix_size = 2 * channels

    def matrix_entry(i, j):
        if i < channels and j < channels:
            value = s_real[i, j]
        elif j < channels:
            value = s_imag[i - channels, j]
        else:
            value = s_real[i - channels, j - channels]
        if i == j:
            value = value + 1.0
        return value

    def right_entry(i):
        if i < channels:
            return p_real[i]
        return p_imag[i - channels]

    factor = [[None] * matrix_size for i in range(matrix_size)]
    for j in range(matrix_size):
        running = matrix_entry(j, j)
        for k in range(j):
            running = running - factor[j][k] * factor[j][k]
        factor[j][j] = jnp.sqrt(running)
        inverse = 1.0 / factor[j][j]
        for i in range(j + 1, matrix_size):
            running = matrix_entry(i, j)
            for k in range(j):
                running = running - factor[i][k] * factor[j][k]
            factor[i][j] = running * inverse
    forward = []
    for i in range(matrix_size):
        running = right_entry(i)
        for k in range(i):
            running = running - factor[i][k] * forward[k]
        forward.append(running / factor[i][i])
    backward = [None] * matrix_size
    for i in reversed(range(matrix_size)):
        running = forward[i]
        for k in range(i + 1, matrix_size):
            running = running - factor[k][i] * backward[k]
        backward[i] = running / factor[i][i]
    return (jnp.stack(backward[:channels]), jnp.stack(backward[channels:]))


def cross_spectra(magnet_real, magnet_imag, detector_real, detector_imag, valid):
    keep = valid.astype(jnp.float32)[:, None]
    channels = magnet_real.shape[1]
    s_real_rows = []
    s_imag_rows = []
    p_real_rows = []
    p_imag_rows = []
    for chan in range(channels):
        left_real = (magnet_real[:, chan].astype(jnp.float32) * keep)[:, None, :]
        left_imag = (magnet_imag[:, chan].astype(jnp.float32) * keep)[:, None, :]
        s_real_rows.append(
            jnp.sum(
                left_real * magnet_real.astype(jnp.float32)
                + left_imag * magnet_imag.astype(jnp.float32),
                axis=0,
            )
        )
        s_imag_rows.append(
            jnp.sum(
                left_imag * magnet_real.astype(jnp.float32)
                - left_real * magnet_imag.astype(jnp.float32),
                axis=0,
            )
        )
        p_real_rows.append(
            jnp.sum(
                left_real * detector_real.astype(jnp.float32)
                + left_imag * detector_imag.astype(jnp.float32),
                axis=0,
            )
        )
        p_imag_rows.append(
            jnp.sum(
                left_imag * detector_real.astype(jnp.float32)
                - left_real * detector_imag.astype(jnp.float32),
                axis=0,
            )
        )
    return (
        jnp.stack(s_real_rows),
        jnp.stack(s_imag_rows),
        jnp.stack(p_real_rows),
        jnp.stack(p_imag_rows),
    )


def pack_spectra(s_real, s_imag, p_real, p_imag):
    bin_count = s_real.shape[2]
    pieces = [s_real.reshape(-1, bin_count), s_imag.reshape(-1, bin_count)]
    pieces = pieces + [p_real.reshape(-1, bin_count), p_imag.reshape(-1, bin_count)]
    return jnp.concatenate(pieces, axis=0)


def unpack_spectra(packed, channels, detectors):
    bin_count = packed.shape[1]
    square_count = channels * channels
    s_real = packed[:square_count].reshape(channels, channels, bin_count)
    s_imag = packed[square_count : 2 * square_count].reshape(channels, channels, bin_count)
    cross_rows = packed[2 * square_count :]
    cross_count = channels * detectors
    p_real = cross_rows[:cross_count].reshape(channels, detectors, bin_count)
    p_imag = cross_rows[cross_count:].reshape(channels, detectors, bin_count)
    return (s_real, s_imag, p_real, p_imag)


def on_device(magnet_real, magnet_imag, detector_real, detector_imag, valid, intersection):
    s_real, s_imag, p_real, p_imag = cross_spectra(
        magnet_real, magnet_imag, detector_real, detector_imag, valid
    )
    channels = s_real.shape[0]
    detectors = p_real.shape[1]
    packed = pack_spectra(s_real, s_imag, p_real, p_imag)
    shared_spectra = summed_rows(packed, SEG, 1)
    share_real, share_imag = wiener_solve(*unpack_spectra(shared_spectra, channels, detectors))
    filt_real, filt_imag = sent_together((share_real, share_imag), SEG, 2, 0)
    clean_real = detector_real.astype(jnp.float32)
    clean_imag = detector_imag.astype(jnp.float32)
    for chan in range(channels):
        field_real = magnet_real[:, chan].astype(jnp.float32)[:, None, :]
        field_imag = magnet_imag[:, chan].astype(jnp.float32)[:, None, :]
        weight_real = filt_real[chan][None, :, :]
        weight_imag = filt_imag[chan][None, :, :]
        clean_real = clean_real - weight_real * field_real - weight_imag * field_imag
        clean_imag = clean_imag - weight_real * field_imag + weight_imag * field_real
    cleaned_real = clean_real[:, 0] * clean_real[:, 1] + clean_imag[:, 0] * clean_imag[:, 1]
    cleaned_imag = clean_imag[:, 0] * clean_real[:, 1] - clean_real[:, 0] * clean_imag[:, 1]
    numerator = jnp.sum(cleaned_real * intersection[None, :], axis=1)
    weight_square = jnp.sum(intersection * intersection)
    summed, norm_square = lax.psum((numerator, weight_square), "bin")
    estimate = summed / jnp.sqrt(norm_square)
    return (cleaned_real, cleaned_imag, estimate)


def solution(mesh):
    torus = Mesh(
        mesh.devices.reshape(8, 4, 2, mesh.shape["bin"]), ("seg_0", "seg_1", "seg_2", "bin")
    )
    in_specs = (
        P(SEG, None, "bin"),
        P(SEG, None, "bin"),
        P(SEG, None, "bin"),
        P(SEG, None, "bin"),
        P(SEG),
        P("bin"),
    )
    out_specs = (P(SEG, "bin"), P(SEG, "bin"), P(SEG))
    return jax.shard_map(
        on_device, mesh=torus, in_specs=in_specs, out_specs=out_specs, check_vma=False
    )
```

profile of v0, /device:TPU:2, one launch (start us, length us, event | category | flops | bytes accessed | tf_op | source)
XLA Modules:
  0.0 242.7 jit_solution(8950154593771467322)
XLA Ops:
  7.2 6.6 %fusion.416 = (bf16[8,1,8192]{2,1,0:T(2,128)(2,1)S(1)}, bf16[8,1,8192]{2,1,0:T(2,128)(2,1)S(1)}, bf16[8,1,8192]{2,1,0:T(2,128)(2,1)S(1)}, bf16[8,1,8192]{2,1,0:T...) fusion(bf16[8,8,8192]{2,1,0:T(8,128)(2,1)} %param.7), kind=kLoop, calls=%fused_computation.776 | loop fusion | bytes 2097152 | tf_op jit(solution)/shard_map/slice | solution.py:81
  13.9 2.2 fusion.417
  16.1 3.4 %fusion.95 = (f32[8,8192]{1,0:T(8,128)S(1)}, f32[8,8192]{1,0:T(8,128)S(1)}, f32[8,8192]{1,0:T(8,128)S(1)}, f32[8,8192]{1,0:T(8,128)S(1)}, f32[8,8192]{1,0:T(8,12...) fusion(f32[8]{0:T(128)S(1)} %convert_element_type.76, ...), kind=kLoop, calls=%fused_computation.194 | loop fusion | flops 2097152 | bytes 6291488 | tf_op jit(solution)/shard_map/mul | solution.py:85
  19.6 7.1 %fusion.15 = (f32[8,8192]{1,0:T(8,128)}, f32[8,8192]{1,0:T(8,128)}, f32[8,8192]{1,0:T(8,128)}, f32[8,8192]{1,0:T(8,128)}, f32[8,8192]{1,0:T(8,128)}, /*index=5*/...) fusion(bf16[8,8,8192]{2,1,0:T(8,128)(2,1)S(1)} %copy-done.1, ...), kind=kLoop, calls=%fused_computation.82 | loop fusion | flops 33554432 | bytes 10485760 | tf_op jit(solution)/shard_map/reduce_sum | solution.py:83
  26.7 3.7 %fusion.47 = (f32[2,8192]{1,0:T(2,128)S(1)}, f32[2,8192]{1,0:T(2,128)S(1)}, f32[2,8192]{1,0:T(2,128)S(1)}, f32[2,8192]{1,0:T(2,128)S(1)}, f32[2,8192]{1,0:T(2,12...) fusion(f32[8,8192]{1,0:T(8,128)S(1)} %get-tuple-element.282, ...), kind=kLoop, calls=%fused_computation.114 | loop fusion | flops 8388608 | bytes 5767168 | tf_op jit(solution)/shard_map/reduce_sum | solution.py:97
  31.8 1.4 reshape.28780
  33.3 1.1 bitcast_dynamic-update-slice_fusion.7
  34.4 1.0 bitcast_dynamic-update-slice_fusion.15
  35.4 1.0 bitcast_dynamic-update-slice_fusion.6
  36.4 1.0 bitcast_dynamic-update-slice_fusion.5
  38.7 2.5 %pad_maximum_fusion = f32[160,8192]{1,0:T(8,128)} fusion(f32[16,8192]{1,0:T(8,128)S(1)} %reshape.28781, f32[16,8192]{1,0:T(8,128)S(1)} %reshape.28780, f32[64,8192]{1,0:T(8,128)S(1)} %bitcast.1228, f32[64,8192]{1,0:T(8,128)S(1)} %bitcast.1227), kind=kLoop, calls=%fused_computation.32 | loop fusion | flops 3932160 | bytes 10485760 | tf_op jit(solution)/shard_map/concatenate | solution.py:122
  41.6 1.3 convert_bitcast_fusion.1
  43.6 66.0 %reduce-scatter.4.cloned.1.call-done = f32[160,1024]{1,0:T(8,128)} async-done(((f32[160,8192]{1,0:T(8,128)}), f32[160,1024]{1,0:T(8,128)}) %reduce-scatter.4.cloned.1.call-update) | async-done | bytes 655376 | tf_op jit(solution)/shard_map/reduce_scatter | solution.py:12
  109.7 2.0 convert_bitcast_fusion.8
  111.7 21.5 %reduce-scatter.6.cloned.1.call-done = f32[160,256]{1,0:T(8,128)} async-done(((f32[160,1024]{1,0:T(8,128)}), f32[160,256]{1,0:T(8,128)}) %reduce-scatter.6.cloned.1.call-update) | async-done | bytes 163856 | tf_op jit(solution)/shard_map/reduce_scatter | solution.py:12
  133.3 2.1 convert_bitcast_fusion.9
  135.5 15.1 %reduce-scatter.8.cloned.1.call-done = f32[160,128]{1,0:T(8,128)} async-done(((f32[160,256]{1,0:T(8,128)}), f32[160,128]{1,0:T(8,128)}) %reduce-scatter.8.cloned.1.call-update) | async-done | bytes 81936 | tf_op jit(solution)/shard_map/reduce_scatter | solution.py:12
  151.8 1.2 subtract_divide_fusion.15
  152.9 1.1 constant_dynamic-update-slice_fusion.31
  154.9 1.1 convert_bitcast_fusion.12
  156.6 1.1 convert_bitcast_fusion.13
  157.7 61.1 %all-gather.2.cloned.1.call-done = f32[16,2,8192]{2,1,0:T(2,128)} async-done(((f32[16,2,128]{2,1,0:T(2,128)}), f32[16,2,8192]{2,1,0:T(2,128)}) %all-gather.2.cloned.1.call-update) | async-done | bytes 1048592 | tf_op jit(solution)/shard_map/all_gather | solution.py:18
  218.8 1.4 slice_bitcast_fusion.15
  223.8 11.1 %all-reduce = (f32[8]{0:T(128)S(1)}, f32[]{:T(128)}) all-reduce(f32[8]{0:T(128)S(1)} %get-tuple-element.65, f32[]{:T(128)} %multiply_reduce_fusion.1), channel_id=1, replica_groups=mesh['seg_0'=8,'seg_1'=4,'seg_2'=2,'bin'=4] {'bin'}, use_global_device_ids=true, to_apply=%region_36.0 | all-reduce | flops 9 | bytes 72 | tf_op jit(solution)/shard_map/psum | solution.py:160
  (149 shorter events, 10.3 us)
Async XLA Ops:
  7.2 6.7 %copy-start.36 = (s32[8]{0:T(128)S(1)}, s32[8]{0:T(128)}, u32[]{:S(2)}) copy-start(s32[8]{0:T(128)} %param.10) | copy-start | bytes 100
  7.2 6.7 %copy-start.1 = (bf16[8,8,8192]{2,1,0:T(8,128)(2,1)S(1)}, bf16[8,8,8192]{2,1,0:T(8,128)(2,1)}, u32[]{:S(2)}) copy-start(bf16[8,8,8192]{2,1,0:T(8,128)(2,1)} %param.6) | copy-start | bytes 3145732
  7.2 102.4 %reduce-scatter.4.cloned.1.call-start = ((), (), s32[]{:S(2)}) async-start(), calls=%async_computation.3 | async-start | bytes 5898240 | tf_op jit(solution)/shard_map/reduce_scatter | solution.py:12
  16.1 3.5 %copy-start.5 = (bf16[8,1,8192]{2,1,0:T(2,128)(2,1)}, bf16[8,1,8192]{2,1,0:T(2,128)(2,1)S(1)}, u32[]{:S(2)}) copy-start(bf16[8,1,8192]{2,1,0:T(2,128)(2,1)S(1)} %get-tuple-element.259) | copy-start | bytes 393220
  16.1 3.5 %copy-start.6 = (bf16[8,1,8192]{2,1,0:T(2,128)(2,1)}, bf16[8,1,8192]{2,1,0:T(2,128)(2,1)S(1)}, u32[]{:S(2)}) copy-start(bf16[8,1,8192]{2,1,0:T(2,128)(2,1)S(1)} %get-tuple-element.260) | copy-start | bytes 393220
  16.1 3.5 %copy-start.9 = (bf16[8,1,8192]{2,1,0:T(2,128)(2,1)}, bf16[8,1,8192]{2,1,0:T(2,128)(2,1)S(1)}, u32[]{:S(2)}) copy-start(bf16[8,1,8192]{2,1,0:T(2,128)(2,1)S(1)} %get-tuple-element.258) | copy-start | bytes 393220
  16.1 3.5 %copy-start.11 = (bf16[8,1,8192]{2,1,0:T(2,128)(2,1)}, bf16[8,1,8192]{2,1,0:T(2,128)(2,1)S(1)}, u32[]{:S(2)}) copy-start(bf16[8,1,8192]{2,1,0:T(2,128)(2,1)S(1)} %get-tuple-element.256) | copy-start | bytes 393220
  16.1 3.5 %copy-start.12 = (bf16[8,1,8192]{2,1,0:T(2,128)(2,1)}, bf16[8,1,8192]{2,1,0:T(2,128)(2,1)S(1)}, u32[]{:S(2)}) copy-start(bf16[8,1,8192]{2,1,0:T(2,128)(2,1)S(1)} %get-tuple-element.262) | copy-start | bytes 393220
  16.1 3.4 %copy-start = (bf16[8,8,8192]{2,1,0:T(8,128)(2,1)S(1)}, bf16[8,8,8192]{2,1,0:T(8,128)(2,1)}, u32[]{:S(2)}) copy-start(bf16[8,8,8192]{2,1,0:T(8,128)(2,1)} %param.7) | copy-start | bytes 3145732
  19.6 7.2 %copy-start.17 = (bf16[8,2,8192]{2,1,0:T(2,128)(2,1)S(1)}, bf16[8,2,8192]{2,1,0:T(2,128)(2,1)}, u32[]{:S(2)}) copy-start(bf16[8,2,8192]{2,1,0:T(2,128)(2,1)} %param.9) | copy-start | bytes 786436
  19.6 7.2 %copy-start.19 = (bf16[8,2,8192]{2,1,0:T(2,128)(2,1)S(1)}, bf16[8,2,8192]{2,1,0:T(2,128)(2,1)}, u32[]{:S(2)}) copy-start(bf16[8,2,8192]{2,1,0:T(2,128)(2,1)} %param.8) | copy-start | bytes 786436
  33.2 4.2 %copy-start.30 = (f32[8,8192]{1,0:T(8,128)S(1)}, f32[8,8192]{1,0:T(8,128)}, u32[]{:S(2)}) copy-start(f32[8,8192]{1,0:T(8,128)} %get-tuple-element.23) | copy-start | bytes 786436
  33.3 4.2 %copy-start.29 = (f32[8,8192]{1,0:T(8,128)S(1)}, f32[8,8192]{1,0:T(8,128)}, u32[]{:S(2)}) copy-start(f32[8,8192]{1,0:T(8,128)} %get-tuple-element.25) | copy-start | bytes 786436
  33.3 4.3 %copy-start.28 = (f32[8,8192]{1,0:T(8,128)S(1)}, f32[8,8192]{1,0:T(8,128)}, u32[]{:S(2)}) copy-start(f32[8,8192]{1,0:T(8,128)} %get-tuple-element.27) | copy-start | bytes 786436
  33.3 4.3 %copy-start.27 = (f32[8,8192]{1,0:T(8,128)S(1)}, f32[8,8192]{1,0:T(8,128)}, u32[]{:S(2)}) copy-start(f32[8,8192]{1,0:T(8,128)} %get-tuple-element.29) | copy-start | bytes 786436
  33.3 4.3 %copy-start.26 = (f32[8,8192]{1,0:T(8,128)S(1)}, f32[8,8192]{1,0:T(8,128)}, u32[]{:S(2)}) copy-start(f32[8,8192]{1,0:T(8,128)} %get-tuple-element.20) | copy-start | bytes 786436
  41.3 92.0 %reduce-scatter.6.cloned.1.call-start = ((), (), s32[]{:S(2)}) async-start(), calls=%async_computation.4 | async-start | bytes 819200 | tf_op jit(solution)/shard_map/reduce_scatter | solution.py:12
  109.6 46.4 %copy-start.34 = (f32[8192]{0:T(1024)S(1)}, f32[8192]{0:T(1024)}, u32[]{:S(2)}) copy-start(f32[8192]{0:T(1024)} %param.11) | copy-start | bytes 98308
  109.6 40.9 %reduce-scatter.8.cloned.1.call-start = ((), (), s32[]{:S(2)}) async-start(), calls=%async_computation.5 | async-start | bytes 245760 | tf_op jit(solution)/shard_map/reduce_scatter | solution.py:12
  133.3 85.5 %all-gather.2.cloned.1.call-start = ((), (), s32[]{:S(2)}) async-start(), calls=%async_computation.6 | async-start | bytes 1064960 | tf_op jit(solution)/shard_map/all_gather | solution.py:18
  156.0 64.2 %copy-start.2 = (f32[8,8192]{1,0:T(8,128)S(1)}, f32[8,8192]{1,0:T(8,128)}, u32[]{:S(2)}) copy-start(f32[8,8192]{1,0:T(8,128)} %get-tuple-element.289) | copy-start | bytes 786436
  156.0 64.2 %copy-start.3 = (f32[8,8192]{1,0:T(8,128)S(1)}, f32[8,8192]{1,0:T(8,128)}, u32[]{:S(2)}) copy-start(f32[8,8192]{1,0:T(8,128)} %get-tuple-element.296) | copy-start | bytes 786436
  157.7 62.5 %copy-start.4 = (f32[8,8192]{1,0:T(8,128)S(1)}, f32[8,8192]{1,0:T(8,128)}, u32[]{:S(2)}) copy-start(f32[8,8192]{1,0:T(8,128)} %get-tuple-element.297) | copy-start | bytes 786436
  157.7 62.5 %copy-start.13 = (f32[8,8192]{1,0:T(8,128)S(1)}, f32[8,8192]{1,0:T(8,128)}, u32[]{:S(2)}) copy-start(f32[8,8192]{1,0:T(8,128)} %get-tuple-element.290) | copy-start | bytes 786436
  (17 other events, 25.9 us)
Sparse Core Ops, SparseCore 0:
  41.4 68.1 reduce-scatter.3
  112.1 21.0 reduce-scatter.5
  135.7 14.7 reduce-scatter.7
  155.0 63.7 all-gather.1
where the time goes:
time: 243 us
  waiting for transfers between devices  164 us (67%)
  other arithmetic  32.5 us (13%)
  local copies, waits for them, and re-layouts  20 us (8%)
  between operations  15.3 us (6%)
  blocking collectives  11.1 us (5%)
    reduce_scatter x3, waiting for transfers between devices, summed_rows(): shard = lax.psum_scatter(shard, axis, scatter_dimension=dim, tiled=True)  103 us
    all_gather x1, waiting for transfers between devices, sent_together(): lax.all_gather(both, axis, axis=dim, tiled=True)  61.1 us
    psum x1, blocking collectives, on_device(): summed, norm_square = lax.psum((numerator, weight_square), 'bin')  11.1 us
    unnamed x116, local copies, waits for them, and re-layouts  7.14 us
    reduce_sum x1, other arithmetic, cross_spectra(): jnp.sum(left_real * magnet_real.astype(jnp.float32) + left_imag * magnet_...  7.14 us
    slice x1, local copies, waits for them, and re-layouts, cross_spectra(): left_imag = (magnet_imag[:, chan].astype(jnp.float32) * keep)[:, None, :]  6.59 us
    mul x4, other arithmetic, on_device(): weight_real * field_real  4.91 us
  transfers between devices with their start and end apart: 4, of which 4 were waited for; matrix products, arithmetic and copies ran while one was open for 4% of the time, Pallas kernels for 0%

commit v1 on v0

v1 whole, which is shorter than its diff:
```python
import jax
import jax.numpy as jnp
from jax import lax
from jax.experimental import pallas as pl
from jax.experimental.pallas import tpu as pltpu
from jax.sharding import Mesh
from jax.sharding import PartitionSpec as P


SEG = ("z", "x", "c")
LANES = 128
CH = 8
DET = 2
ROWS = 96
WROWS = 32
VMEM = pltpu.VMEM
SMEM = pltpu.SMEM
F32 = jnp.float32


def gray(i):
    return i ^ (i >> 1)


def flip_pairs(size, shift, bit):
    where = {gray((i - shift) % size): i for i in range(size)}
    return [(i, where[gray((i - shift) % size) ^ (1 << bit)]) for i in range(size)]


STEPS = (
    (("x", 0, 0), ("x", 0, 1), ("z", 0, 0), ("z", 0, 1), ("z", 0, 2)),
    (("x", 0, 1), ("x", 0, 0), ("z", 1, 0), ("z", 1, 2), ("z", 1, 1)),
)
SUB = 2


def swap_step(value, at, sizes):
    nz, nx, nc = sizes["z"], sizes["x"], sizes["c"]
    pairs = []
    for z in range(nz):
        for x in range(nx):
            for c in range(nc):
                axis, shift, bit = STEPS[c][at]
                where = {"z": z, "x": x}
                where[axis] = dict(flip_pairs(sizes[axis], shift, bit))[where[axis]]
                pairs.append(((z * nx + x) * nc + c, (where["z"] * nx + where["x"]) * nc + c))
    return lax.ppermute(value, SEG, pairs)


def swap_core(value):
    return lax.ppermute(value, "c", [(0, 1), (1, 0)])


def step_code(core, sizes):
    code = jnp.int32(0)
    for axis, shift, bit in STEPS[core][:-1]:
        ring = (lax.axis_index(axis) - shift + sizes[axis]) % sizes[axis]
        code = code * 2 + ((gray(ring) >> bit) & 1)
    return code * SUB


def sublane(shape=(CH, LANES)):
    return lax.broadcasted_iota(jnp.int32, shape, 0)


def down(v, k):
    return v if k == 0 else pltpu.roll(v, CH - k, 0)


def params():
    return pltpu.CompilerParams(vmem_limit_bytes=16 << 20)


def cost(blocks, flops):
    return pl.CostEstimate(flops=blocks * flops, bytes_accessed=0, transcendentals=0)


def block_of(code_ref, which, p):
    return code_ref[2 * which] + (p ^ code_ref[2 * which + 1])


def lanes_of(block):
    return pl.ds(pl.multiple_of(block * LANES, LANES), LANES)


def spectra_body(which, first, count, code_ref, valid_ref, mr_ref, mi_ref, hr_ref, hi_ref, out_ref):
    low = sublane() < 4
    keep = [valid_ref[s].astype(F32) for s in range(CH)]

    def step(p, carry):
        at = lanes_of(block_of(code_ref, which, first + p))
        acc = [jnp.zeros((CH, LANES), F32) for _ in range(12)]
        for s in range(CH):
            mr = mr_ref[s, :, at].astype(F32)
            mi = mi_ref[s, :, at].astype(F32)
            kr = mr * keep[s]
            ki = mi * keep[s]
            acc[0] = acc[0] + (kr * mr + ki * mi)
            for k in range(1, 4):
                rr = down(mr, k)
                ri = down(mi, k)
                acc[2 * k - 1] = acc[2 * k - 1] + (kr * rr + ki * ri)
                acc[2 * k] = acc[2 * k] + (ki * rr - kr * ri)
            rr = down(mr, 4)
            ri = down(mi, 4)
            acc[7] = acc[7] + (jnp.where(low, kr, ki) * rr + jnp.where(low, ki, -kr) * ri)
            hr = hr_ref[s, :, at].astype(F32)
            hi = hi_ref[s, :, at].astype(F32)
            for k in range(DET):
                br = jnp.broadcast_to(hr[k : k + 1], (CH, LANES))
                bi = jnp.broadcast_to(hi[k : k + 1], (CH, LANES))
                acc[8 + 2 * k] = acc[8 + 2 * k] + (kr * br + ki * bi)
                acc[9 + 2 * k] = acc[9 + 2 * k] + (ki * br - kr * bi)
        for r in range(12):
            out_ref[p, CH * r : CH * (r + 1), :] = acc[r]
        return carry

    lax.fori_loop(0, count, step, 0)


def spectra(codes, valid, mr, mi, hr, hi, which, first, count):
    return pl.pallas_call(
        lambda *refs: spectra_body(which, first, count, *refs),
        out_shape=jax.ShapeDtypeStruct((count, ROWS, LANES), F32),
        in_specs=[pl.BlockSpec(memory_space=SMEM)] * 2 + [pl.BlockSpec(memory_space=VMEM)] * 4,
        out_specs=pl.BlockSpec(memory_space=VMEM),
        compiler_params=params(),
        cost_estimate=cost(count, 500000),
        name="spectra",
    )(codes, valid, mr, mi, hr, hi)


def solve_block(rows):
    sub = sublane()
    low = sub < 4
    dr = [None] * CH
    di = [None] * CH
    dr[0] = rows[0] + 1.0
    di[0] = jnp.zeros_like(rows[0])
    for k in range(1, 4):
        dr[k], di[k] = rows[2 * k - 1], rows[2 * k]
        dr[CH - k] = pltpu.roll(rows[2 * k - 1], k, 0)
        di[CH - k] = -pltpu.roll(rows[2 * k], k, 0)
    half = rows[7]
    turned = pltpu.roll(half, 4, 0)
    dr[4] = jnp.where(low, half, turned)
    di[4] = jnp.where(low, -turned, half)
    cols_r, cols_i = [], []
    for j in range(CH):
        cr, ci = dr[j], di[j]
        for c in range(1, CH):
            cr = jnp.where(sub == c, dr[(j - c) % CH], cr)
            ci = jnp.where(sub == c, di[(j - c) % CH], ci)
        cols_r.append(cr)
        cols_i.append(ci)
    cols_r += [rows[8], rows[10]]
    cols_i += [rows[9], rows[11]]

    def row(v, j):
        return jnp.broadcast_to(v[j : j + 1], (CH, LANES))

    diag = jnp.ones((CH, LANES), F32)
    for j in range(CH):
        pivot = row(cols_r[j], j)
        diag = jnp.where(sub == j, pivot, diag)
        inv = 1.0 / pivot
        fr = jnp.where(sub == j, 0.0, cols_r[j] * inv)
        fi = jnp.where(sub == j, 0.0, cols_i[j] * inv)
        for k in range(j + 1, CH + DET):
            ar, ai = row(cols_r[k], j), row(cols_i[k], j)
            cols_r[k] = cols_r[k] - (fr * ar - fi * ai)
            cols_i[k] = cols_i[k] - (fr * ai + fi * ar)
    inv = 1.0 / diag
    return [cols_r[8] * inv, cols_i[8] * inv, cols_r[9] * inv, cols_i[9] * inv]


def solve_body(a_ref, b_ref, out_ref):
    for u in range(SUB):
        rows = [
            a_ref[u, CH * r : CH * (r + 1), :] + b_ref[u, CH * r : CH * (r + 1), :]
            for r in range(12)
        ]
        for q, tile in enumerate(solve_block(rows)):
            out_ref[u, CH * q : CH * (q + 1), :] = tile


def solve(a, b):
    return pl.pallas_call(
        solve_body,
        out_shape=jax.ShapeDtypeStruct((SUB, WROWS, LANES), F32),
        in_specs=[pl.BlockSpec(memory_space=VMEM)] * 2,
        out_specs=pl.BlockSpec(memory_space=VMEM),
        compiler_params=params(),
        cost_estimate=cost(SUB, 5000000),
        name="solve",
    )(a, b)


def channel_sums(tiles):
    sub = sublane()
    half = sub < 4
    level = []
    for s in range(4):
        a, b = tiles[s], tiles[s + 4]
        level.append(jnp.where(half, a, b) + pltpu.roll(jnp.where(half, b, a), 4, 0))
    for bit in (2, 1):
        mask = (sub & bit) == 0
        nxt = []
        for s in range(bit):
            a, b = level[s], level[s + bit]
            nxt.append(jnp.where(mask, a + pltpu.roll(a, CH - bit, 0), b + pltpu.roll(b, bit, 0)))
        level = nxt
    return level[0]


def clean_block(block, w, mr_ref, mi_ref, h_ref, inter_ref):
    at = lanes_of(block)
    parts = [[] for _ in range(4)]
    for s in range(CH):
        mr = mr_ref[s, :, at].astype(F32)
        mi = mi_ref[s, :, at].astype(F32)
        for k in range(DET):
            wr, wi = w[2 * k], w[2 * k + 1]
            parts[2 * k].append(wr * mr + wi * mi)
            parts[2 * k + 1].append(wr * mi - wi * mr)
    g = [h_ref[q, :, at] - channel_sums(parts[q]) for q in range(4)]
    real = g[0] * g[2] + g[1] * g[3]
    imag = g[1] * g[2] - g[0] * g[3]
    weight = jnp.broadcast_to(inter_ref[pl.ds(block, 1), :], (CH, LANES))
    return real, imag, real * weight


def filter_tiles(w_ref, p):
    return [w_ref[p, CH * q : CH * (q + 1), :] for q in range(4)]


def clean_body(which, first, count, code_ref, w_ref, mr_ref, mi_ref, h_ref, inter_ref, out_ref, num_ref):
    def step(p, num):
        block = block_of(code_ref, which, first + p)
        real, imag, part = clean_block(block, filter_tiles(w_ref, p), mr_ref, mi_ref, h_ref, inter_ref)
        out_ref[p, 0:CH, :] = real
        out_ref[p, CH : 2 * CH, :] = imag
        return num + part

    num_ref[...] = lax.fori_loop(0, count, step, jnp.zeros((CH, LANES), F32))


def clean(codes, filters, rest, which, first):
    count = filters.shape[0]
    return pl.pallas_call(
        lambda *refs: clean_body(which, first, count, *refs),
        out_shape=[
            jax.ShapeDtypeStruct((count, 2 * CH, LANES), F32),
            jax.ShapeDtypeStruct((CH, LANES), F32),
        ],
        in_specs=[pl.BlockSpec(memory_space=SMEM)] + [pl.BlockSpec(memory_space=VMEM)] * 5,
        out_specs=[pl.BlockSpec(memory_space=VMEM)] * 2,
        compiler_params=params(),
        cost_estimate=cost(count, 300000),
        name="clean",
    )(codes, filters, *rest)


def finish_body(which, first, count, places, code_ref, w_ref, mr_ref, mi_ref, h_ref, inter_ref, *refs):
    real_ref, imag_ref, num_ref = refs[-3:]
    done = refs[: len(places)]
    sums = refs[len(places) : 2 * len(places)]

    def step(p, num):
        block = block_of(code_ref, which, first + p)
        real, imag, part = clean_block(block, filter_tiles(w_ref, p), mr_ref, mi_ref, h_ref, inter_ref)
        at = lanes_of(block)
        real_ref[:, at] = real
        imag_ref[:, at] = imag
        return num + part

    num = lax.fori_loop(0, count, step, jnp.zeros((CH, LANES), F32))
    for (from_which, from_first), done_ref, sum_ref in zip(places, done, sums):
        num = num + sum_ref[...]

        def move(p, carry, from_which=from_which, from_first=from_first, done_ref=done_ref):
            at = lanes_of(block_of(code_ref, from_which, from_first + p))
            real_ref[:, at] = done_ref[p, 0:CH, :]
            imag_ref[:, at] = done_ref[p, CH : 2 * CH, :]
            return carry

        lax.fori_loop(0, done_ref.shape[0], move, 0, unroll=4)
    weight = inter_ref[...]
    square = jnp.sum(weight * weight)
    lane = lax.broadcasted_iota(jnp.int32, (CH, LANES), 1)
    total = jnp.broadcast_to(jnp.sum(num, axis=1, keepdims=True), (CH, LANES))
    num_ref[...] = jnp.where(lane == 0, total, square)


def finish(codes, filters, rest, which, first, places, pieces, sums):
    count = filters.shape[0]
    mr = rest[0]
    args = (codes, filters, *rest, *pieces, *sums)
    return pl.pallas_call(
        lambda *refs: finish_body(which, first, count, places, *refs),
        out_shape=[jax.ShapeDtypeStruct((mr.shape[0], mr.shape[2]), F32)] * 2
        + [jax.ShapeDtypeStruct((CH, LANES), F32)],
        in_specs=[pl.BlockSpec(memory_space=SMEM)]
        + [pl.BlockSpec(memory_space=VMEM)] * (len(args) - 1),
        out_specs=[pl.BlockSpec(memory_space=VMEM)] * 3,
        compiler_params=params(),
        cost_estimate=cost(count, 400000),
        name="finish",
    )(*args)


def summed_over_bin(value, sizes):
    for bit in range(sizes["y"].bit_length() - 1):
        value = value + lax.ppermute(value, "y", flip_pairs(sizes["y"], 0, bit))
    return value


def on_device(sizes, magnet_real, magnet_imag, detector_real, detector_imag, valid, intersection):
    bins = magnet_real.shape[2]
    half = bins // (LANES * sizes["c"])
    top = half // 2
    core = lax.axis_index("c")
    code_a, code_b = step_code(0, sizes), step_code(1, sizes)
    own = jnp.where(core == 0, code_a, code_b)
    other = jnp.where(core == 0, code_b, code_a)
    codes = jnp.stack([core * half, own, (1 - core) * half, other])
    data = (magnet_real, magnet_imag, detector_real, detector_imag)

    def reduced_over_core(first):
        away = spectra(codes, valid, *data, 1, first, top)
        away = swap_core(away)
        return [spectra(codes, valid, *data, 0, first, top), away]

    def summed(pieces, lo, hi):
        total = pieces[0][lo:hi]
        for piece in pieces[1:]:
            total = total + piece[lo:hi]
        return total

    pieces = reduced_over_core(top)
    got = swap_step(summed(pieces, 0, top), 0, sizes)
    pieces = reduced_over_core(0) + [got]
    h = jnp.stack([detector_real, detector_imag]).astype(F32)
    h = h.transpose(2, 0, 1, 3).reshape(2 * DET, CH, bins)
    size = top
    for at in range(1, len(STEPS[0]) - 1):
        size //= 2
        got = swap_step(summed(pieces, size, 2 * size), at, sizes)
        pieces = [p[:size] for p in pieces] + [got]
    last = summed(pieces, 0, size)
    got = swap_step(last, len(STEPS[0]) - 1, sizes)
    filters = solve(last, got)

    rest = (magnet_real, magnet_imag, h, intersection.reshape(bins // LANES, LANES))
    for at in range(len(STEPS[0]) - 2, 0, -1):
        filters = jnp.concatenate([filters, swap_step(filters, at, sizes)], axis=0)
    upper = swap_step(filters, 0, sizes)
    other = swap_core(filters)
    last = swap_core(upper)
    pieces, sums = [], []
    places = ((0, 0), (1, 0), (0, top))
    for f, place in zip((filters, other, upper), places):
        piece, num = clean(codes, f, rest, *place)
        pieces.append(piece)
        sums.append(num)
    real, imag, num = finish(codes, last, rest, 1, top, places, pieces, sums)
    totals = summed_over_bin(num, sizes)
    estimate = totals[:, 0] / jnp.sqrt(totals[:, 1])
    return (real, imag, estimate)


def solution(mesh):
    sizes = {"z": 8, "x": 4, "c": 2, "y": mesh.shape["bin"]}
    torus = Mesh(mesh.devices.reshape(*sizes.values()), tuple(sizes))
    in_specs = (
        P(SEG, None, "y"),
        P(SEG, None, "y"),
        P(SEG, None, "y"),
        P(SEG, None, "y"),
        P(SEG),
        P("y"),
    )
    out_specs = (P(SEG, "y"), P(SEG, "y"), P(SEG))

    def body(*args):
        return on_device(sizes, *args)

    return jax.shard_map(
        body, mesh=torus, in_specs=in_specs, out_specs=out_specs, check_vma=False
    )
```

time: 243 us -> 97.1 us (0.40)
  waiting for transfers between devices: 164 us -> 44.1 us
  other arithmetic: 32.5 us -> 1.74 us
  starting transfers between devices: 0.16 us -> 28 us
  between operations: 15.3 us -> 0.87 us
  Pallas kernels: 0 us -> 14.1 us
  local copies, waits for them, and re-layouts: 20 us -> 6.44 us
  blocking collectives: 11.1 us -> 0 us
    reduce_scatter x3 -> x0, waiting for transfers between devices: 103 us -> none  [summed_rows(): shard = lax.psum_scatter(shard, axis, scatter_dimension=dim, tiled=True)]
    all_gather x1 -> x0, waiting for transfers between devices: 61.1 us -> none  [sent_together(): lax.all_gather(both, axis, axis=dim, tiled=True)]
    ppermute x0 -> x15, waiting for transfers between devices: none -> 44.1 us  [the longest x9 40.6 us: swap_step(): return lax.ppermute(value, SEG, pairs)]
    ppermute x0 -> x15, starting transfers between devices: none -> 28 us  [the longest x9 22.4 us: swap_step(): return lax.ppermute(value, SEG, pairs)]
    pallas_call x0 -> x9, Pallas kernels: none -> 14.1 us  [the longest x4 7.79 us: spectra(): pl.pallas_call(lambda *refs: spectra_body(which, first, count, *refs), ou...]
    reduce_sum x4 -> x0, other arithmetic: 12.3 us -> none  [the longest x1 7.14 us: cross_spectra(): jnp.sum(left_real * magnet_real.astype(jnp.float32) + left_imag * magnet_...]
    mul x9 -> x0, other arithmetic: 12.1 us -> none  [the longest x4 4.91 us: on_device(): weight_real * field_real]
    psum x1 -> x0, blocking collectives: 11.1 us -> none  [on_device(): summed, norm_square = lax.psum((numerator, weight_square), 'bin')]
  transfers between devices with their start and end apart: 4 -> 15, of which waited for: 4 -> 11; matrix products, arithmetic and copies ran while one was open for 4% -> 1% of each run, Pallas kernels for 0% -> 10%
where the time goes in v1:
time: 97.1 us; the launch traced here: 95.2 us
  waiting for transfers between devices  44.1 us (45%)
  starting transfers between devices  28 us (29%)
  Pallas kernels  14.1 us (15%)
  local copies, waits for them, and re-layouts  6.44 us (7%)
  other arithmetic  1.74 us (2%)
    ppermute x9, waiting for transfers between devices, swap_step(): return lax.ppermute(value, SEG, pairs)  40.6 us
    ppermute x9, starting transfers between devices, swap_step(): return lax.ppermute(value, SEG, pairs)  22.4 us
    pallas_call x4, Pallas kernels, spectra(): pl.pallas_call(lambda *refs: spectra_body(which, first, count, *refs), ou...  7.79 us
    unnamed x16, local copies, waits for them, and re-layouts  5.83 us
    ppermute x2, starting transfers between devices, summed_over_bin(): value = value + lax.ppermute(value, 'y', flip_pairs(sizes['y'], 0, bit))  4.91 us
    pallas_call x3, Pallas kernels, clean(): pl.pallas_call(lambda *refs: clean_body(which, first, count, *refs), out_...  3.83 us
    ppermute x2, waiting for transfers between devices, summed_over_bin(): value = value + lax.ppermute(value, 'y', flip_pairs(sizes['y'], 0, bit))  3.52 us
    pallas_call x1, Pallas kernels, finish(): pl.pallas_call(lambda *refs: finish_body(which, first, count, places, *re...  2.25 us
  transfers between devices with their start and end apart: 15, of which 11 were waited for; matrix products, arithmetic and copies ran while one was open for 1% of the time, Pallas kernels for 10%

profile of v1, /device:TPU:2, one launch (start us, length us, event | category | flops | bytes accessed | tf_op | source)
XLA Modules:
  0.0 95.2 jit_solution(8063504272152887544)
XLA Ops:
  5.7 1.9 %spectra.7 = f32[16,96,128]{2,1,0:T(8,128)S(1)} custom-call(s32[4]{0:T(128)S(1)} %pad_add_fusion.refs_0_, s32[8]{0:T(128)S(1)} %copy-done.7, bf16[8,8,8192]{2,1,0:T(8,128)(2,1)S(1)} %copy-done, bf16[8,8,8192]{2,1,0:T(8,128)(2,1)S(1)} %copy-done.2, bf16[8,2,8192]{2,1,0:T(2,128)(2,1)S(1)} %copy-done.4, bf16[8,2,8192]{2,1,0:T(2,128)(2,1)S(1)} %copy-done.5), custom_call_target="tpu_custom_call" | custom-call | flops 8000000 | tf_op jit(solution)/shard_map/spectra/pallas_call | solution.py:122
  7.7 1.9 %spectra.5 = f32[16,96,128]{2,1,0:T(8,128)S(1)} custom-call(s32[4]{0:T(128)S(1)} %pad_add_fusion.refs_0_, s32[8]{0:T(128)S(1)} %copy-done.7, bf16[8,8,8192]{2,1,0:T(8,128)(2,1)S(1)} %copy-done, bf16[8,8,8192]{2,1,0:T(8,128)(2,1)S(1)} %copy-done.2, bf16[8,2,8192]{2,1,0:T(2,128)(2,1)S(1)} %copy-done.4, bf16[8,2,8192]{2,1,0:T(2,128)(2,1)S(1)} %copy-done.5), custom_call_target="tpu_custom_call" | custom-call | flops 8000000 | tf_op jit(solution)/shard_map/spectra/pallas_call | solution.py:122
  10.3 1.9 %spectra.6 = f32[16,96,128]{2,1,0:T(8,128)S(1)} custom-call(s32[4]{0:T(128)S(1)} %pad_add_fusion.refs_0_, s32[8]{0:T(128)S(1)} %copy-done.7, bf16[8,8,8192]{2,1,0:T(8,128)(2,1)S(1)} %copy-done, bf16[8,8,8192]{2,1,0:T(8,128)(2,1)S(1)} %copy-done.2, bf16[8,2,8192]{2,1,0:T(2,128)(2,1)S(1)} %copy-done.4, bf16[8,2,8192]{2,1,0:T(2,128)(2,1)S(1)} %copy-done.5), custom_call_target="tpu_custom_call" | custom-call | flops 8000000 | tf_op jit(solution)/shard_map/spectra/pallas_call | solution.py:122
  12.3 2.3 %collective-permute-start.2 = (f32[16,96,128]{2,1,0:T(8,128)S(1)}, f32[16,96,128]{2,1,0:T(8,128)S(1)}, u32[]{:S(2)}, u32[]{:S(2)}) collective-permute-start(f32[16,96,128]{2,1,0:T(8,128)S(1)} %add.114), channel_id=1, source_target_pairs={{0,8},{4,28},{8,0},{12,20},{16,24},{20,12},{24,16},{28,4},{32,40},... | collective-permute-start | bytes 2359304 | tf_op jit(solution)/shard_map/ppermute | solution.py:47
  14.7 1.9 %spectra.4 = f32[16,96,128]{2,1,0:T(8,128)S(1)} custom-call(s32[4]{0:T(128)S(1)} %pad_add_fusion.refs_0_, s32[8]{0:T(128)S(1)} %copy-done.7, bf16[8,8,8192]{2,1,0:T(8,128)(2,1)S(1)} %copy-done, bf16[8,8,8192]{2,1,0:T(8,128)(2,1)S(1)} %copy-done.2, bf16[8,2,8192]{2,1,0:T(2,128)(2,1)S(1)} %copy-done.4, bf16[8,2,8192]{2,1,0:T(2,128)(2,1)S(1)} %copy-done.5), custom_call_target="tpu_custom_call" | custom-call | flops 8000000 | tf_op jit(solution)/shard_map/spectra/pallas_call | solution.py:122
  16.6 8.0 %collective-permute-done.2 = f32[16,96,128]{2,1,0:T(8,128)S(1)} collective-permute-done((f32[16,96,128]{2,1,0:T(8,128)S(1)}, f32[16,96,128]{2,1,0:T(8,128)S(1)}, u32[]{:S(2)}, u32[]{:S(2)}) %collective-permute-start.2) | collective-permute-done | bytes 786464 | tf_op jit(solution)/shard_map/ppermute | solution.py:47
  26.1 6.5 %collective-permute-done.3 = f32[8,96,128]{2,1,0:T(8,128)S(1)} collective-permute-done((f32[8,96,128]{2,1,0:T(8,128)S(1)}, f32[8,96,128]{2,1,0:T(8,128)S(1)}, u32[]{:S(2)}, u32[]{:S(2)}) %collective-permute-start.3) | collective-permute-done | bytes 393248 | tf_op jit(solution)/shard_map/ppermute | solution.py:47
  32.6 1.8 %collective-permute-start.4 = (f32[4,96,128]{2,1,0:T(8,128)S(1)}, f32[4,96,128]{2,1,0:T(8,128)S(1)}, u32[]{:S(2)}, u32[]{:S(2)}) collective-permute-start(f32[4,96,128]{2,1,0:T(8,128)S(1)} %slice_add_fusion.2), channel_id=1, source_target_pairs={{0,32},{4,228},{8,40},{12,236},{16,48},{20,244},{24,56},{28,252},{... | collective-permute-start | bytes 589832 | tf_op jit(solution)/shard_map/ppermute | solution.py:47
  34.4 4.0 %collective-permute-done.4 = f32[4,96,128]{2,1,0:T(8,128)S(1)} collective-permute-done((f32[4,96,128]{2,1,0:T(8,128)S(1)}, f32[4,96,128]{2,1,0:T(8,128)S(1)}, u32[]{:S(2)}, u32[]{:S(2)}) %collective-permute-start.4) | collective-permute-done | bytes 196640 | tf_op jit(solution)/shard_map/ppermute | solution.py:47
  38.4 4.5 %collective-permute-start.5 = (f32[2,96,128]{2,1,0:T(8,128)S(1)}, f32[2,96,128]{2,1,0:T(8,128)S(1)}, u32[]{:S(2)}, u32[]{:S(2)}) collective-permute-start(f32[2,96,128]{2,1,0:T(8,128)S(1)} %slice_add_fusion.5), channel_id=1, source_target_pairs={{0,96},{4,36},{8,104},{12,44},{16,112},{20,52},{24,120},{28,60},{3... | collective-permute-start | bytes 294920 | tf_op jit(solution)/shard_map/ppermute | solution.py:47
  42.9 2.6 %collective-permute-done.5 = f32[2,96,128]{2,1,0:T(8,128)S(1)} collective-permute-done((f32[2,96,128]{2,1,0:T(8,128)S(1)}, f32[2,96,128]{2,1,0:T(8,128)S(1)}, u32[]{:S(2)}, u32[]{:S(2)}) %collective-permute-start.5) | collective-permute-done | bytes 98336 | tf_op jit(solution)/shard_map/ppermute | solution.py:47
  45.5 5.2 %collective-permute-start.6 = (f32[2,96,128]{2,1,0:T(8,128)S(1)}, f32[2,96,128]{2,1,0:T(8,128)S(1)}, u32[]{:S(2)}, u32[]{:S(2)}) collective-permute-start(f32[2,96,128]{2,1,0:T(8,128)S(1)} %fusion.a_ref), channel_id=1, source_target_pairs={{0,224},{4,164},{8,232},{12,172},{16,240},{20,180},{24,248},{28,18... | collective-permute-start | bytes 294920 | tf_op jit(solution)/shard_map/ppermute | solution.py:47
  50.8 3.1 %collective-permute-done.6.b_ref = f32[2,96,128]{2,1,0:T(8,128)S(1)} collective-permute-done((f32[2,96,128]{2,1,0:T(8,128)S(1)}, f32[2,96,128]{2,1,0:T(8,128)S(1)}, u32[]{:S(2)}, u32[]{:S(2)}) %collective-permute-start.6) | collective-permute-done | bytes 98336 | tf_op jit(solution)/shard_map/ppermute | solution.py:47
  54.1 2.2 %collective-permute-start.7 = (f32[2,32,128]{2,1,0:T(8,128)S(1)}, f32[2,32,128]{2,1,0:T(8,128)S(1)}, u32[]{:S(2)}, u32[]{:S(2)}) collective-permute-start(f32[2,32,128]{2,1,0:T(8,128)S(1)} %solve.1), channel_id=1, source_target_pairs={{0,96},{4,36},{8,104},{12,44},{16,112},{20,52},{24,120},{28,60},{3... | collective-permute-start | bytes 98312 | tf_op jit(solution)/shard_map/ppermute | solution.py:47
  56.3 3.6 %collective-permute-done.7 = f32[2,32,128]{2,1,0:T(8,128)S(1)} collective-permute-done((f32[2,32,128]{2,1,0:T(8,128)S(1)}, f32[2,32,128]{2,1,0:T(8,128)S(1)}, u32[]{:S(2)}, u32[]{:S(2)}) %collective-permute-start.7) | collective-permute-done | bytes 32800 | tf_op jit(solution)/shard_map/ppermute | solution.py:47
  59.9 4.3 %collective-permute-done.8 = f32[4,32,128]{2,1,0:T(8,128)S(1)} collective-permute-done((f32[4,32,128]{2,1,0:T(8,128)S(1)}, f32[4,32,128]{2,1,0:T(8,128)S(1)}, u32[]{:S(2)}, u32[]{:S(2)}) %collective-permute-start.8) | collective-permute-done | bytes 65568 | tf_op jit(solution)/shard_map/ppermute | solution.py:47
  64.2 2.1 %collective-permute-start.9 = (f32[8,32,128]{2,1,0:T(8,128)S(1)}, f32[8,32,128]{2,1,0:T(8,128)S(1)}, u32[]{:S(2)}, u32[]{:S(2)}) collective-permute-start(f32[8,32,128]{2,1,0:T(8,128)S(1)} %pad_maximum_fusion.1), channel_id=1, source_target_pairs={{0,24},{4,12},{8,16},{12,4},{16,8},{20,28},{24,0},{28,20},{32,56},... | collective-permute-start | bytes 393224 | tf_op jit(solution)/shard_map/ppermute | solution.py:47
  66.3 4.2 %collective-permute-done.9 = f32[8,32,128]{2,1,0:T(8,128)S(1)} collective-permute-done((f32[8,32,128]{2,1,0:T(8,128)S(1)}, f32[8,32,128]{2,1,0:T(8,128)S(1)}, u32[]{:S(2)}, u32[]{:S(2)}) %collective-permute-start.9) | collective-permute-done | bytes 131104 | tf_op jit(solution)/shard_map/ppermute | solution.py:47
  70.5 2.9 %collective-permute-start.10 = (f32[16,32,128]{2,1,0:T(8,128)S(1)}, f32[16,32,128]{2,1,0:T(8,128)S(1)}, u32[]{:S(2)}, u32[]{:S(2)}) collective-permute-start(f32[16,32,128]{2,1,0:T(8,128)S(1)} %pad_maximum_fusion.refs_1_), channel_id=1, source_target_pairs={{0,8},{4,28},{8,0},{12,20},{16,24},{20,12},{24,16},{28,4},{32,40},... | collective-permute-start | bytes 786440 | tf_op jit(solution)/shard_map/ppermute | solution.py:47
  73.4 4.3 %collective-permute-done.10.refs_1_ = f32[16,32,128]{2,1,0:T(8,128)S(1)} collective-permute-done((f32[16,32,128]{2,1,0:T(8,128)S(1)}, f32[16,32,128]{2,1,0:T(8,128)S(1)}, u32[]{:S(2)}, u32[]{:S(2)}) %collective-permute-start.10) | collective-permute-done | bytes 262176 | tf_op jit(solution)/shard_map/ppermute | solution.py:47
  83.8 2.3 %finish.1 = (f32[8,8192]{1,0:T(8,128)}, f32[8,8192]{1,0:T(8,128)}, f32[8,128]{1,0:T(8,128)S(1)}) custom-call(s32[4]{0:T(128)S(1)} %pad_add_fusion.refs_0_, f32[16,32,128]{2,1,0:T(8,128)S(1)} %collective-permute-done.11.refs_1_, bf16[8,8,8192]{2,1,0:T(8,128)(2,1)S(1)} %copy-done.1, bf16[8,8,8192]{2,1,0:T(8,128)(2,1)S(1)} %copy-done.3, ...), custom_call_target="tpu_custom_call" | custom-call | flops 6400000 | tf_op jit(solution)/shard_map/finish/pallas_call | solution.py:299
  86.0 1.7 %collective-permute-start.13 = (f32[8,128]{1,0:T(8,128)S(1)}, f32[8,128]{1,0:T(8,128)S(1)}, u32[]{:S(2)}, u32[]{:S(2)}) collective-permute-start(f32[8,128]{1,0:T(8,128)S(1)} %get-tuple-element.20), channel_id=1, source_target_pairs={{0,1},{1,0},{2,3},{3,2},{4,5},{5,4},{6,7},{7,6},{8,9},{9,8},{10,11... | collective-permute-start | bytes 12296 | tf_op jit(solution)/shard_map/ppermute | solution.py:314
  87.8 1.9 %collective-permute-done.13 = f32[8,128]{1,0:T(8,128)S(1)} collective-permute-done((f32[8,128]{1,0:T(8,128)S(1)}, f32[8,128]{1,0:T(8,128)S(1)}, u32[]{:S(2)}, u32[]{:S(2)}) %collective-permute-start.13) | collective-permute-done | bytes 4128 | tf_op jit(solution)/shard_map/ppermute | solution.py:314
  89.7 3.2 %collective-permute-start.14 = (f32[8,128]{1,0:T(8,128)S(1)}, f32[8,128]{1,0:T(8,128)S(1)}, u32[]{:S(2)}, u32[]{:S(2)}) collective-permute-start(f32[8,128]{1,0:T(8,128)S(1)} %add.128), channel_id=1, source_target_pairs={{0,3},{1,2},{2,1},{3,0},{4,7},{5,6},{6,5},{7,4},{8,11},{9,10},{10,... | collective-permute-start | bytes 12296 | tf_op jit(solution)/shard_map/ppermute | solution.py:314
  (45 shorter events, 15.9 us)
Async XLA Ops:
  0.7 0.7 copy-start.7
  1.3 1.2 %copy-start = (bf16[8,8,8192]{2,1,0:T(8,128)(2,1)S(1)}, bf16[8,8,8192]{2,1,0:T(8,128)(2,1)}, u32[]{:S(2)}) copy-start(bf16[8,8,8192]{2,1,0:T(8,128)(2,1)} %refs_2_.15) | copy-start | bytes 3145732
  2.6 1.2 %copy-start.2 = (bf16[8,8,8192]{2,1,0:T(8,128)(2,1)S(1)}, bf16[8,8,8192]{2,1,0:T(8,128)(2,1)}, u32[]{:S(2)}) copy-start(bf16[8,8,8192]{2,1,0:T(8,128)(2,1)} %refs_3_.15) | copy-start | bytes 3145732
  3.8 0.9 copy-start.4
  4.7 0.9 copy-start.5
  7.6 4.6 %collective-permute-start.1 = (f32[16,96,128]{2,1,0:T(8,128)S(1)}, f32[16,96,128]{2,1,0:T(8,128)S(1)}, u32[]{:S(2)}, u32[]{:S(2)}) collective-permute-start(f32[16,96,128]{2,1,0:T(8,128)S(1)} %spectra.7), channel_id=1, source_target_pairs={{0,4},{4,0},{1,5},{5,1},{2,6},{6,2},{3,7},{7,3},{8,12},{12,8},{9,1... | collective-permute-start | bytes 2359304 | tf_op jit(solution)/shard_map/ppermute | solution.py:51
  9.7 6.9 %collective-permute-start = (f32[16,96,128]{2,1,0:T(8,128)S(1)}, f32[16,96,128]{2,1,0:T(8,128)S(1)}, u32[]{:S(2)}, u32[]{:S(2)}) collective-permute-start(f32[16,96,128]{2,1,0:T(8,128)S(1)} %spectra.5), channel_id=1, source_target_pairs={{0,4},{4,0},{1,5},{5,1},{2,6},{6,2},{3,7},{7,3},{8,12},{12,8},{9,1... | collective-permute-start | bytes 2359304 | tf_op jit(solution)/shard_map/ppermute | solution.py:51
  12.3 12.3 %collective-permute-start.2 = (f32[16,96,128]{2,1,0:T(8,128)S(1)}, f32[16,96,128]{2,1,0:T(8,128)S(1)}, u32[]{:S(2)}, u32[]{:S(2)}) collective-permute-start(f32[16,96,128]{2,1,0:T(8,128)S(1)} %add.114), channel_id=1, source_target_pairs={{0,8},{4,28},{8,0},{12,20},{16,24},{20,12},{24,16},{28,4},{32,40},... | collective-permute-start | bytes 2359304 | tf_op jit(solution)/shard_map/ppermute | solution.py:47
  24.7 7.9 %collective-permute-start.3 = (f32[8,96,128]{2,1,0:T(8,128)S(1)}, f32[8,96,128]{2,1,0:T(8,128)S(1)}, u32[]{:S(2)}, u32[]{:S(2)}) collective-permute-start(f32[8,96,128]{2,1,0:T(8,128)S(1)} %slice_add_fusion), channel_id=1, source_target_pairs={{0,24},{4,12},{8,16},{12,4},{16,8},{20,28},{24,0},{28,20},{32,56},... | collective-permute-start | bytes 1179656 | tf_op jit(solution)/shard_map/ppermute | solution.py:47
  32.6 5.8 %collective-permute-start.4 = (f32[4,96,128]{2,1,0:T(8,128)S(1)}, f32[4,96,128]{2,1,0:T(8,128)S(1)}, u32[]{:S(2)}, u32[]{:S(2)}) collective-permute-start(f32[4,96,128]{2,1,0:T(8,128)S(1)} %slice_add_fusion.2), channel_id=1, source_target_pairs={{0,32},{4,228},{8,40},{12,236},{16,48},{20,244},{24,56},{28,252},{... | collective-permute-start | bytes 589832 | tf_op jit(solution)/shard_map/ppermute | solution.py:47
  38.4 7.1 %collective-permute-start.5 = (f32[2,96,128]{2,1,0:T(8,128)S(1)}, f32[2,96,128]{2,1,0:T(8,128)S(1)}, u32[]{:S(2)}, u32[]{:S(2)}) collective-permute-start(f32[2,96,128]{2,1,0:T(8,128)S(1)} %slice_add_fusion.5), channel_id=1, source_target_pairs={{0,96},{4,36},{8,104},{12,44},{16,112},{20,52},{24,120},{28,60},{3... | collective-permute-start | bytes 294920 | tf_op jit(solution)/shard_map/ppermute | solution.py:47
  45.5 8.4 %collective-permute-start.6 = (f32[2,96,128]{2,1,0:T(8,128)S(1)}, f32[2,96,128]{2,1,0:T(8,128)S(1)}, u32[]{:S(2)}, u32[]{:S(2)}) collective-permute-start(f32[2,96,128]{2,1,0:T(8,128)S(1)} %fusion.a_ref), channel_id=1, source_target_pairs={{0,224},{4,164},{8,232},{12,172},{16,240},{20,180},{24,248},{28,18... | collective-permute-start | bytes 294920 | tf_op jit(solution)/shard_map/ppermute | solution.py:47
  54.1 5.8 %collective-permute-start.7 = (f32[2,32,128]{2,1,0:T(8,128)S(1)}, f32[2,32,128]{2,1,0:T(8,128)S(1)}, u32[]{:S(2)}, u32[]{:S(2)}) collective-permute-start(f32[2,32,128]{2,1,0:T(8,128)S(1)} %solve.1), channel_id=1, source_target_pairs={{0,96},{4,36},{8,104},{12,44},{16,112},{20,52},{24,120},{28,60},{3... | collective-permute-start | bytes 98312 | tf_op jit(solution)/shard_map/ppermute | solution.py:47
  59.9 4.3 %collective-permute-start.8 = (f32[4,32,128]{2,1,0:T(8,128)S(1)}, f32[4,32,128]{2,1,0:T(8,128)S(1)}, u32[]{:S(2)}, u32[]{:S(2)}) collective-permute-start(f32[4,32,128]{2,1,0:T(8,128)S(1)} %pad_maximum_fusion.2), channel_id=1, source_target_pairs={{0,32},{4,228},{8,40},{12,236},{16,48},{20,244},{24,56},{28,252},{... | collective-permute-start | bytes 196616 | tf_op jit(solution)/shard_map/ppermute | solution.py:47
  64.2 6.3 %collective-permute-start.9 = (f32[8,32,128]{2,1,0:T(8,128)S(1)}, f32[8,32,128]{2,1,0:T(8,128)S(1)}, u32[]{:S(2)}, u32[]{:S(2)}) collective-permute-start(f32[8,32,128]{2,1,0:T(8,128)S(1)} %pad_maximum_fusion.1), channel_id=1, source_target_pairs={{0,24},{4,12},{8,16},{12,4},{16,8},{20,28},{24,0},{28,20},{32,56},... | collective-permute-start | bytes 393224 | tf_op jit(solution)/shard_map/ppermute | solution.py:47
  70.5 7.2 %collective-permute-start.10 = (f32[16,32,128]{2,1,0:T(8,128)S(1)}, f32[16,32,128]{2,1,0:T(8,128)S(1)}, u32[]{:S(2)}, u32[]{:S(2)}) collective-permute-start(f32[16,32,128]{2,1,0:T(8,128)S(1)} %pad_maximum_fusion.refs_1_), channel_id=1, source_target_pairs={{0,8},{4,28},{8,0},{12,20},{16,24},{20,12},{24,16},{28,4},{32,40},... | collective-permute-start | bytes 786440 | tf_op jit(solution)/shard_map/ppermute | solution.py:47
  73.3 9.1 %collective-permute-start.12 = (f32[16,32,128]{2,1,0:T(8,128)S(1)}, f32[16,32,128]{2,1,0:T(8,128)S(1)}, u32[]{:S(2)}, u32[]{:S(2)}) collective-permute-start(f32[16,32,128]{2,1,0:T(8,128)S(1)} %pad_maximum_fusion.refs_1_), channel_id=1, source_target_pairs={{0,4},{4,0},{1,5},{5,1},{2,6},{6,2},{3,7},{7,3},{8,12},{12,8},{9,1... | collective-permute-start | bytes 786440 | tf_op jit(solution)/shard_map/ppermute | solution.py:51
  77.7 6.1 %collective-permute-start.11 = (f32[16,32,128]{2,1,0:T(8,128)S(1)}, f32[16,32,128]{2,1,0:T(8,128)S(1)}, u32[]{:S(2)}, u32[]{:S(2)}) collective-permute-start(f32[16,32,128]{2,1,0:T(8,128)S(1)} %collective-permute-done.10.refs_1_), channel_id=1, source_target_pairs={{0,4},{4,0},{1,5},{5,1},{2,6},{6,2},{3,7},{7,3},{8,12},{12,8},{9,1... | collective-permute-start | bytes 786440 | tf_op jit(solution)/shard_map/ppermute | solution.py:51
  77.7 1.3 %copy-start.6 = (f32[8192]{0:T(1024)S(1)}, f32[8192]{0:T(1024)}, u32[]{:S(2)}) copy-start(f32[8192]{0:T(1024)} %param.11) | copy-start | bytes 98308
  78.4 1.2 %copy-start.1 = (bf16[8,8,8192]{2,1,0:T(8,128)(2,1)S(1)}, bf16[8,8,8192]{2,1,0:T(8,128)(2,1)}, u32[]{:S(2)}) copy-start(bf16[8,8,8192]{2,1,0:T(8,128)(2,1)} %refs_2_.15) | copy-start | bytes 3145732
  78.4 1.5 %copy-start.3 = (bf16[8,8,8192]{2,1,0:T(8,128)(2,1)S(1)}, bf16[8,8,8192]{2,1,0:T(8,128)(2,1)}, u32[]{:S(2)}) copy-start(bf16[8,8,8192]{2,1,0:T(8,128)(2,1)} %refs_3_.15) | copy-start | bytes 3145732
  86.0 3.6 %collective-permute-start.13 = (f32[8,128]{1,0:T(8,128)S(1)}, f32[8,128]{1,0:T(8,128)S(1)}, u32[]{:S(2)}, u32[]{:S(2)}) collective-permute-start(f32[8,128]{1,0:T(8,128)S(1)} %get-tuple-element.20), channel_id=1, source_target_pairs={{0,1},{1,0},{2,3},{3,2},{4,5},{5,4},{6,7},{7,6},{8,9},{9,8},{10,11... | collective-permute-start | bytes 12296 | tf_op jit(solution)/shard_map/ppermute | solution.py:314
  89.7 4.8 %collective-permute-start.14 = (f32[8,128]{1,0:T(8,128)S(1)}, f32[8,128]{1,0:T(8,128)S(1)}, u32[]{:S(2)}, u32[]{:S(2)}) collective-permute-start(f32[8,128]{1,0:T(8,128)S(1)} %add.128), channel_id=1, source_target_pairs={{0,3},{1,2},{2,1},{3,0},{4,7},{5,6},{6,5},{7,4},{8,11},{9,10},{10,... | collective-permute-start | bytes 12296 | tf_op jit(solution)/shard_map/ppermute | solution.py:314

commit v2 on v1

v2 whole, which is shorter than its diff:
```python
import jax
import jax.numpy as jnp
from jax import lax
from jax.experimental import pallas as pl
from jax.experimental.pallas import tpu as pltpu
from jax.sharding import Mesh
from jax.sharding import PartitionSpec as P


SEG = ("z", "x", "c")
LANES = 128
CH = 8
DET = 2
ROWS = 96
WROWS = 32
VMEM = pltpu.VMEM
F32 = jnp.float32


def gray(i):
    return i ^ (i >> 1)


def flip_pairs(size, shift, bit):
    where = {gray((i - shift) % size): i for i in range(size)}
    return [(i, where[gray((i - shift) % size) ^ (1 << bit)]) for i in range(size)]


STEPS = (
    (("x", 0, 0), ("x", 0, 1), ("z", 0, 0), ("z", 0, 1), ("z", 0, 2)),
    (("x", 0, 1), ("x", 0, 0), ("z", 1, 0), ("z", 1, 2), ("z", 1, 1)),
)
SUB = 2


def swap_steps(value, steps, sizes):
    nz, nx, nc = sizes["z"], sizes["x"], sizes["c"]
    pairs = []
    for z in range(nz):
        for x in range(nx):
            for c in range(nc):
                where = {"z": z, "x": x}
                for at in steps:
                    axis, shift, bit = STEPS[c][at]
                    where[axis] = dict(flip_pairs(sizes[axis], shift, bit))[where[axis]]
                pairs.append(((z * nx + x) * nc + c, (where["z"] * nx + where["x"]) * nc + c))
    return lax.ppermute(value, SEG, pairs)


def swap_core(value):
    return lax.ppermute(value, "c", [(0, 1), (1, 0)])


def step_code(core, sizes):
    code = jnp.int32(0)
    for axis, shift, bit in STEPS[core][:-1]:
        ring = (lax.axis_index(axis) + (sizes[axis] - shift)) & (sizes[axis] - 1)
        code = code * 2 + ((gray(ring) >> bit) & 1)
    return code * SUB


def half_codes(sizes, half):
    core = lax.axis_index("c")
    code_a, code_b = step_code(0, sizes), step_code(1, sizes)
    own = jnp.where(core == 0, code_a, code_b)
    other = jnp.where(core == 0, code_b, code_a)
    return ((core * half, own), ((1 - core) * half, other))


def sublane(shape=(CH, LANES)):
    return lax.broadcasted_iota(jnp.int32, shape, 0)


def down(v, k):
    return v if k == 0 else pltpu.roll(v, CH - k, 0)


def params():
    return pltpu.CompilerParams(vmem_limit_bytes=16 << 20)


def cost(blocks, flops):
    return pl.CostEstimate(flops=blocks * flops, bytes_accessed=0, transcendentals=0)


def block_of(codes, which, p):
    base, code = codes[which]
    return base + (p ^ code)


def lanes_of(block):
    return pl.ds(pl.multiple_of(block * LANES, LANES), LANES)


def spectra_block(at, keep, mr_ref, mi_ref, hr_ref, hi_ref, store):
    low = sublane() < 4
    acc = [jnp.zeros((CH, LANES), F32) for _ in range(12)]
    for s in range(CH):
        mr = mr_ref[s, :, at].astype(F32)
        mi = mi_ref[s, :, at].astype(F32)
        kr = mr * keep[s]
        ki = mi * keep[s]
        acc[0] = acc[0] + (kr * mr + ki * mi)
        for k in range(1, 4):
            rr = down(mr, k)
            ri = down(mi, k)
            acc[2 * k - 1] = acc[2 * k - 1] + (kr * rr + ki * ri)
            acc[2 * k] = acc[2 * k] + (ki * rr - kr * ri)
        rr = down(mr, 4)
        ri = down(mi, 4)
        acc[7] = acc[7] + (jnp.where(low, kr, ki) * rr + jnp.where(low, ki, -kr) * ri)
        hr = hr_ref[s, :, at].astype(F32)
        hi = hi_ref[s, :, at].astype(F32)
        for k in range(DET):
            br = jnp.broadcast_to(hr[k : k + 1], (CH, LANES))
            bi = jnp.broadcast_to(hi[k : k + 1], (CH, LANES))
            acc[8 + 2 * k] = acc[8 + 2 * k] + (kr * br + ki * bi)
            acc[9 + 2 * k] = acc[9 + 2 * k] + (ki * br - kr * bi)
    for r in range(12):
        store(r, acc[r])


def spectra_loop(codes, which, first, count, keep, data, out_ref):
    def step(p, carry):
        def store(r, tile):
            out_ref[p, CH * r : CH * (r + 1), :] = tile

        spectra_block(lanes_of(block_of(codes, which, first + p)), keep, *data, store)
        return carry

    lax.fori_loop(0, count, step, 0)


def front_body(sizes, half, first, count, valid_hbm, *refs):
    hbm, (out_ref, keep_ref, *local) = refs[:4], refs[4:10]
    keep_smem, keep_sem, sems = refs[10:]
    codes = half_codes(sizes, half)
    width = count * LANES
    npiece = hbm[0].shape[2] // width
    lead = block_of(codes, 1, first) // count
    keep_copy = pltpu.make_async_copy(valid_hbm, keep_smem, keep_sem)
    keep_copy.start()
    copies = []
    for n in range(npiece):
        at = pl.ds(pl.multiple_of((n ^ lead) * width, width), width)
        copies.append(
            [
                pltpu.make_async_copy(src.at[:, :, at], dst.at[:, :, at], sems.at[n, i])
                for i, (src, dst) in enumerate(zip(hbm, local))
            ]
        )
        for copy in copies[-1]:
            copy.start()
    keep_copy.wait()
    for copy in copies[0]:
        copy.wait()
    for s in range(CH):
        keep_ref[s] = jnp.full((CH, LANES), keep_smem[s].astype(F32))
    spectra_loop(codes, 1, first, count, keep_ref, local, out_ref)
    for piece in copies[1:]:
        for copy in piece:
            copy.wait()


def front(sizes, half, valid, data, first, count):
    npiece = data[0].shape[2] // (count * LANES)
    return pl.pallas_call(
        lambda *refs: front_body(sizes, half, first, count, *refs),
        out_shape=[
            jax.ShapeDtypeStruct((count, ROWS, LANES), F32),
            jax.ShapeDtypeStruct((CH, CH, LANES), F32),
        ]
        + [jax.ShapeDtypeStruct(d.shape, d.dtype) for d in data],
        in_specs=[pl.BlockSpec(memory_space=pltpu.MemorySpace.HBM)] * 5,
        out_specs=[pl.BlockSpec(memory_space=VMEM)] * 6,
        scratch_shapes=[
            pltpu.SMEM(valid.shape, valid.dtype),
            pltpu.SemaphoreType.DMA,
            pltpu.SemaphoreType.DMA((npiece, 4)),
        ],
        compiler_params=params(),
        cost_estimate=cost(count, 500000),
        name="front",
    )(*(pltpu.with_memory_space_constraint(a, pltpu.MemorySpace.HBM) for a in (valid, *data)))


def spectra_body(sizes, half, which, first, count, keep_ref, *refs):
    spectra_loop(half_codes(sizes, half), which, first, count, keep_ref, refs[:4], refs[4])


def spectra(sizes, half, keep, data, which, first, count):
    return pl.pallas_call(
        lambda *refs: spectra_body(sizes, half, which, first, count, *refs),
        out_shape=jax.ShapeDtypeStruct((count, ROWS, LANES), F32),
        in_specs=[pl.BlockSpec(memory_space=VMEM)] * 5,
        out_specs=pl.BlockSpec(memory_space=VMEM),
        compiler_params=params(),
        cost_estimate=cost(count, 500000),
        name="spectra",
    )(keep, *data)


def solve_block(rows):
    sub = sublane()
    low = sub < 4
    dr = [None] * CH
    di = [None] * CH
    dr[0] = rows[0] + 1.0
    di[0] = jnp.zeros_like(rows[0])
    for k in range(1, 4):
        dr[k], di[k] = rows[2 * k - 1], rows[2 * k]
        dr[CH - k] = pltpu.roll(rows[2 * k - 1], k, 0)
        di[CH - k] = -pltpu.roll(rows[2 * k], k, 0)
    half = rows[7]
    turned = pltpu.roll(half, 4, 0)
    dr[4] = jnp.where(low, half, turned)
    di[4] = jnp.where(low, -turned, half)
    cols_r, cols_i = [], []
    for j in range(CH):
        cr, ci = dr[j], di[j]
        for c in range(1, CH):
            cr = jnp.where(sub == c, dr[(j - c) % CH], cr)
            ci = jnp.where(sub == c, di[(j - c) % CH], ci)
        cols_r.append(cr)
        cols_i.append(ci)
    cols_r += [rows[8], rows[10]]
    cols_i += [rows[9], rows[11]]

    def row(v, j):
        return jnp.broadcast_to(v[j : j + 1], (CH, LANES))

    diag = jnp.ones((CH, LANES), F32)
    for j in range(CH):
        pivot = row(cols_r[j], j)
        diag = jnp.where(sub == j, pivot, diag)
        inv = 1.0 / pivot
        fr = jnp.where(sub == j, 0.0, cols_r[j] * inv)
        fi = jnp.where(sub == j, 0.0, cols_i[j] * inv)
        for k in range(j + 1, CH + DET):
            ar, ai = row(cols_r[k], j), row(cols_i[k], j)
            cols_r[k] = cols_r[k] - (fr * ar - fi * ai)
            cols_i[k] = cols_i[k] - (fr * ai + fi * ar)
    inv = 1.0 / diag
    return [cols_r[8] * inv, cols_i[8] * inv, cols_r[9] * inv, cols_i[9] * inv]


def solve_body(a_ref, b_ref, out_ref):
    for u in range(SUB):
        rows = [
            a_ref[u, CH * r : CH * (r + 1), :] + b_ref[u, CH * r : CH * (r + 1), :]
            for r in range(12)
        ]
        for q, tile in enumerate(solve_block(rows)):
            out_ref[u, CH * q : CH * (q + 1), :] = tile


def solve(a, b):
    return pl.pallas_call(
        solve_body,
        out_shape=jax.ShapeDtypeStruct((SUB, WROWS, LANES), F32),
        in_specs=[pl.BlockSpec(memory_space=VMEM)] * 2,
        out_specs=pl.BlockSpec(memory_space=VMEM),
        compiler_params=params(),
        cost_estimate=cost(SUB, 5000000),
        name="solve",
    )(a, b)


def channel_sums(tiles):
    sub = sublane()
    half = sub < 4
    level = []
    for s in range(4):
        a, b = tiles[s], tiles[s + 4]
        level.append(jnp.where(half, a, b) + pltpu.roll(jnp.where(half, b, a), 4, 0))
    for bit in (2, 1):
        mask = (sub & bit) == 0
        nxt = []
        for s in range(bit):
            a, b = level[s], level[s + bit]
            nxt.append(jnp.where(mask, a + pltpu.roll(a, CH - bit, 0), b + pltpu.roll(b, bit, 0)))
        level = nxt
    return level[0]


def clean_block(block, w, mr_ref, mi_ref, h_ref, inter_ref):
    at = lanes_of(block)
    parts = [[] for _ in range(4)]
    for s in range(CH):
        mr = mr_ref[s, :, at].astype(F32)
        mi = mi_ref[s, :, at].astype(F32)
        for k in range(DET):
            wr, wi = w[2 * k], w[2 * k + 1]
            parts[2 * k].append(wr * mr + wi * mi)
            parts[2 * k + 1].append(wr * mi - wi * mr)
    g = [h_ref[q, :, at] - channel_sums(parts[q]) for q in range(4)]
    real = g[0] * g[2] + g[1] * g[3]
    imag = g[1] * g[2] - g[0] * g[3]
    weight = jnp.broadcast_to(inter_ref[pl.ds(block, 1), :], (CH, LANES))
    return real, imag, real * weight


def filter_tiles(w_ref, p):
    return [w_ref[p, CH * q : CH * (q + 1), :] for q in range(4)]


def clean_body(sizes, half, which, first, count, w_ref, *refs):
    data, (out_ref, num_ref) = refs[:4], refs[4:]
    codes = half_codes(sizes, half)

    def step(p, num):
        block = block_of(codes, which, first + p)
        real, imag, part = clean_block(block, filter_tiles(w_ref, p), *data)
        out_ref[p, 0:CH, :] = real
        out_ref[p, CH : 2 * CH, :] = imag
        return num + part

    num_ref[...] = lax.fori_loop(0, count, step, jnp.zeros((CH, LANES), F32))


def clean(sizes, half, filters, rest, which, first):
    count = filters.shape[0]
    return pl.pallas_call(
        lambda *refs: clean_body(sizes, half, which, first, count, *refs),
        out_shape=[
            jax.ShapeDtypeStruct((count, 2 * CH, LANES), F32),
            jax.ShapeDtypeStruct((CH, LANES), F32),
        ],
        in_specs=[pl.BlockSpec(memory_space=VMEM)] * 5,
        out_specs=[pl.BlockSpec(memory_space=VMEM)] * 2,
        compiler_params=params(),
        cost_estimate=cost(count, 300000),
        name="clean",
    )(filters, *rest)


def finish_body(sizes, half, which, first, count, places, w_ref, *refs):
    data, refs = refs[:4], refs[4:]
    real_ref, imag_ref, num_ref = refs[-3:]
    done = refs[: len(places)]
    sums = refs[len(places) : 2 * len(places)]
    codes = half_codes(sizes, half)

    def step(p, num):
        block = block_of(codes, which, first + p)
        real, imag, part = clean_block(block, filter_tiles(w_ref, p), *data)
        at = lanes_of(block)
        real_ref[:, at] = real
        imag_ref[:, at] = imag
        return num + part

    num = lax.fori_loop(0, count, step, jnp.zeros((CH, LANES), F32))
    for (from_which, from_first), done_ref, sum_ref in zip(places, done, sums):
        num = num + sum_ref[...]
        for p in range(done_ref.shape[0]):
            at = lanes_of(block_of(codes, from_which, from_first + p))
            real_ref[:, at] = done_ref[p, 0:CH, :]
            imag_ref[:, at] = done_ref[p, CH : 2 * CH, :]
    weight = data[3][...]
    square = jnp.sum(weight * weight)
    lane = lax.broadcasted_iota(jnp.int32, (CH, LANES), 1)
    total = jnp.broadcast_to(jnp.sum(num, axis=1, keepdims=True), (CH, LANES))
    num_ref[...] = jnp.where(lane == 0, total, square)


def finish(sizes, half, filters, rest, which, first, places, pieces, sums):
    count = filters.shape[0]
    mr = rest[0]
    args = (filters, *rest, *pieces, *sums)
    return pl.pallas_call(
        lambda *refs: finish_body(sizes, half, which, first, count, places, *refs),
        out_shape=[jax.ShapeDtypeStruct((mr.shape[0], mr.shape[2]), F32)] * 2
        + [jax.ShapeDtypeStruct((CH, LANES), F32)],
        in_specs=[pl.BlockSpec(memory_space=VMEM)] * len(args),
        out_specs=[pl.BlockSpec(memory_space=VMEM)] * 3,
        compiler_params=params(),
        cost_estimate=cost(count, 400000),
        name="finish",
    )(*args)


def summed_over_bin(value, sizes):
    for bit in range(sizes["y"].bit_length() - 1):
        value = value + lax.ppermute(value, "y", flip_pairs(sizes["y"], 0, bit))
    return value


def on_device(sizes, magnet_real, magnet_imag, detector_real, detector_imag, valid, intersection):
    bins = magnet_real.shape[2]
    half = bins // (LANES * sizes["c"])
    q = half // 4
    e = half // 8
    data = (magnet_real, magnet_imag, detector_real, detector_imag)

    away, keep, *data = front(sizes, half, valid, data, 3 * q, q)
    received = []

    def local(first, count, away=None):
        if away is None:
            away = spectra(sizes, half, keep, data, 1, first, count)
        away = swap_core(away)
        own = spectra(sizes, half, keep, data, 0, first, count)
        received.extend([(first, first + count, own), (first, first + count, away)])

    def summed(lo, hi):
        parts = [a[lo - f : hi - f] for f, t, a in received if f <= lo and hi <= t]
        total = parts[0]
        for part in parts[1:]:
            total = total + part
        return total

    def halve(at, lo, hi, to):
        got = swap_steps(summed(lo, hi), (at,), sizes)
        received.append((to, to + hi - lo, got))

    local(3 * q, q, away)
    halve(0, 3 * q, 4 * q, q)
    local(2 * q, q)
    halve(0, 2 * q, 3 * q, 0)
    local(0, 2 * q)
    h = jnp.stack([data[2], data[3]]).astype(F32)
    h = h.transpose(2, 0, 1, 3).reshape(2 * DET, CH, bins)
    halve(1, 3 * e, 4 * e, e)
    halve(1, 2 * e, 3 * e, 0)
    halve(2, e, 2 * e, 0)
    halve(3, e // 2, e, 0)
    last = summed(0, SUB)
    got = swap_steps(last, (4,), sizes)
    filters = solve(last, got)

    rest = (data[0], data[1], h, intersection.reshape(bins // LANES, LANES))
    near = [filters]
    for steps in ((3,), (2,), (2, 3)):
        near.append(swap_steps(filters, steps, sizes))
    near = jnp.concatenate(near, axis=0)
    quarters = [near]
    quarters.append(swap_steps(near, (1,), sizes))
    quarters.append(swap_steps(near, (0,), sizes))
    quarters.append(swap_steps(quarters[1], (0,), sizes))
    pieces, sums, places = [], [], []
    for n, mine in enumerate(quarters):
        other = swap_core(mine)
        for which, filt in enumerate((mine, other)):
            if (n, which) == (3, 1):
                real, imag, num = finish(
                    sizes, half, filt, rest, which, n * q, places, pieces, sums
                )
            else:
                piece, num = clean(sizes, half, filt, rest, which, n * q)
                pieces.append(piece)
                sums.append(num)
                places.append((which, n * q))
    totals = summed_over_bin(num, sizes)
    estimate = totals[:, 0] / jnp.sqrt(totals[:, 1])
    return (real, imag, estimate)


def solution(mesh):
    sizes = {"z": 8, "x": 4, "c": 2, "y": mesh.shape["bin"]}
    torus = Mesh(mesh.devices.reshape(*sizes.values()), tuple(sizes))
    in_specs = (
        P(SEG, None, "y"),
        P(SEG, None, "y"),
        P(SEG, None, "y"),
        P(SEG, None, "y"),
        P(SEG),
        P("y"),
    )
    out_specs = (P(SEG, "y"), P(SEG, "y"), P(SEG))

    def body(*args):
        return on_device(sizes, *args)

    return jax.shard_map(
        body, mesh=torus, in_specs=in_specs, out_specs=out_specs, check_vma=False
    )
```

time: 97.1 us -> 78.5 us (0.81)
  the two profiles are of different devices: /device:TPU:2 before, /device:TPU:24 now
where the time goes in v2:
time: 78.5 us; the launch traced here: 78.3 us
  waiting for transfers between devices  36.4 us (46%)
  starting transfers between devices  27.5 us (35%)
  Pallas kernels  11.2 us (14%)
  other arithmetic  1.69 us (2%)
  between operations  0.79 us (1%)
    ppermute x13, waiting for transfers between devices, swap_steps(): return lax.ppermute(value, SEG, pairs)  28.9 us
    ppermute x13, starting transfers between devices, swap_steps(): return lax.ppermute(value, SEG, pairs)  25.2 us
    ppermute x2, waiting for transfers between devices, summed_over_bin(): value = value + lax.ppermute(value, 'y', flip_pairs(sizes['y'], 0, bit))  7.46 us
    pallas_call x5, Pallas kernels, spectra(): pl.pallas_call(lambda *refs: spectra_body(sizes, half, which, first, coun...  4.86 us
    pallas_call x7, Pallas kernels, clean(): pl.pallas_call(lambda *refs: clean_body(sizes, half, which, first, count,...  2.69 us
    pallas_call x1, Pallas kernels, front(): pl.pallas_call(lambda *refs: front_body(sizes, half, first, count, *refs)...  2.11 us
  transfers between devices with their start and end apart: 22, of which 12 were waited for; matrix products, arithmetic and copies ran while one was open for 2% of the time, Pallas kernels for 10%

profile of v2, /device:TPU:24, one launch (start us, length us, event | category | flops | bytes accessed | tf_op | source)
XLA Modules:
  0.0 78.3 jit_solution(6999621196163561757)
XLA Ops:
  0.6 2.1 %front.1 = (f32[8,96,128]{2,1,0:T(8,128)S(1)}, f32[8,8,128]{2,1,0:T(8,128)S(1)}, bf16[8,8,8192]{2,1,0:T(8,128)(2,1)S(1)}, bf16[8,8,8192]{2,1,0:T(8,128)(2,1)S(1)...) custom-call(s32[8]{0:T(128)} %refs_0_.1, bf16[8,8,8192]{2,1,0:T(8,128)(2,1)} %refs_1_.1, ...), custom_call_target="tpu_custom_call" | custom-call | flops 4000000 | tf_op jit(solution)/shard_map/front/pallas_call | solution.py:167
  2.9 1.4 %spectra.8 = f32[16,96,128]{2,1,0:T(8,128)S(1)} custom-call(f32[8,8,128]{2,1,0:T(8,128)S(1)} %get-tuple-element.26.refs_0_, bf16[8,8,8192]{2,1,0:T(8,128)(2,1)S(1)} %get-tuple-element.27.refs_1_, bf16[8,8,8192]{2,1,0:T(8,128)(2,1)S(1)} %get-tuple-element.28.refs_2_, bf16[8,2,8192]{2,1,0:T(2,128)(2,1)S(1)} %get-tuple-element.29.refs_3_, ...), custom_call_target="tpu_custom_call" | custom-call | flops 8000000 | tf_op jit(solution)/shard_map/spectra/pallas_call | solution.py:192
  6.4 1.6 %collective-permute-start.4 = (f32[8,96,128]{2,1,0:T(8,128)S(1)}, f32[8,96,128]{2,1,0:T(8,128)S(1)}, u32[]{:S(2)}, u32[]{:S(2)}) collective-permute-start(f32[8,96,128]{2,1,0:T(8,128)S(1)} %add.63), channel_id=1, source_target_pairs={{0,8},{4,28},{8,0},{12,20},{16,24},{20,12},{24,16},{28,4},{32,40},... | collective-permute-start | bytes 1179656 | tf_op jit(solution)/shard_map/ppermute | solution.py:47
  8.7 1.4 %spectra.7 = f32[16,96,128]{2,1,0:T(8,128)S(1)} custom-call(f32[8,8,128]{2,1,0:T(8,128)S(1)} %get-tuple-element.26.refs_0_, bf16[8,8,8192]{2,1,0:T(8,128)(2,1)S(1)} %get-tuple-element.27.refs_1_, bf16[8,8,8192]{2,1,0:T(8,128)(2,1)S(1)} %get-tuple-element.28.refs_2_, bf16[8,2,8192]{2,1,0:T(2,128)(2,1)S(1)} %get-tuple-element.29.refs_3_, ...), custom_call_target="tpu_custom_call" | custom-call | flops 8000000 | tf_op jit(solution)/shard_map/spectra/pallas_call | solution.py:192
  10.8 3.5 %collective-permute-done.4 = f32[8,96,128]{2,1,0:T(8,128)S(1)} collective-permute-done((f32[8,96,128]{2,1,0:T(8,128)S(1)}, f32[8,96,128]{2,1,0:T(8,128)S(1)}, u32[]{:S(2)}, u32[]{:S(2)}) %collective-permute-start.4) | collective-permute-done | bytes 393248 | tf_op jit(solution)/shard_map/ppermute | solution.py:47
  14.3 2.9 %collective-permute-start.6 = (f32[4,96,128]{2,1,0:T(8,128)S(1)}, f32[4,96,128]{2,1,0:T(8,128)S(1)}, u32[]{:S(2)}, u32[]{:S(2)}) collective-permute-start(f32[4,96,128]{2,1,0:T(8,128)S(1)} %get-tuple-element.50), channel_id=1, source_target_pairs={{0,24},{4,12},{8,16},{12,4},{16,8},{20,28},{24,0},{28,20},{32,56},... | collective-permute-start | bytes 589832 | tf_op jit(solution)/shard_map/ppermute | solution.py:47
  17.7 1.7 %collective-permute-done.1 = f32[8,96,128]{2,1,0:T(8,128)S(1)} collective-permute-done((f32[8,96,128]{2,1,0:T(8,128)S(1)}, f32[8,96,128]{2,1,0:T(8,128)S(1)}, u32[]{:S(2)}, u32[]{:S(2)}) %collective-permute-start.1) | collective-permute-done | bytes 393248 | tf_op jit(solution)/shard_map/ppermute | solution.py:47
  19.4 2.4 %collective-permute-done.6 = f32[4,96,128]{2,1,0:T(8,128)S(1)} collective-permute-done((f32[4,96,128]{2,1,0:T(8,128)S(1)}, f32[4,96,128]{2,1,0:T(8,128)S(1)}, u32[]{:S(2)}, u32[]{:S(2)}) %collective-permute-start.6) | collective-permute-done | bytes 196640 | tf_op jit(solution)/shard_map/ppermute | solution.py:47
  21.8 2.0 %collective-permute-start.7 = (f32[4,96,128]{2,1,0:T(8,128)S(1)}, f32[4,96,128]{2,1,0:T(8,128)S(1)}, u32[]{:S(2)}, u32[]{:S(2)}) collective-permute-start(f32[4,96,128]{2,1,0:T(8,128)S(1)} %fusion), channel_id=1, source_target_pairs={{0,32},{4,228},{8,40},{12,236},{16,48},{20,244},{24,56},{28,252},{... | collective-permute-start | bytes 589832 | tf_op jit(solution)/shard_map/ppermute | solution.py:47
  24.1 3.5 %collective-permute-done.7 = f32[4,96,128]{2,1,0:T(8,128)S(1)} collective-permute-done((f32[4,96,128]{2,1,0:T(8,128)S(1)}, f32[4,96,128]{2,1,0:T(8,128)S(1)}, u32[]{:S(2)}, u32[]{:S(2)}) %collective-permute-start.7) | collective-permute-done | bytes 196640 | tf_op jit(solution)/shard_map/ppermute | solution.py:47
  27.6 4.7 %collective-permute-start.8 = (f32[2,96,128]{2,1,0:T(8,128)S(1)}, f32[2,96,128]{2,1,0:T(8,128)S(1)}, u32[]{:S(2)}, u32[]{:S(2)}) collective-permute-start(f32[2,96,128]{2,1,0:T(8,128)S(1)} %slice_add_fusion.6), channel_id=1, source_target_pairs={{0,96},{4,36},{8,104},{12,44},{16,112},{20,52},{24,120},{28,60},{3... | collective-permute-start | bytes 294920 | tf_op jit(solution)/shard_map/ppermute | solution.py:47
  32.3 2.6 %collective-permute-done.8 = f32[2,96,128]{2,1,0:T(8,128)S(1)} collective-permute-done((f32[2,96,128]{2,1,0:T(8,128)S(1)}, f32[2,96,128]{2,1,0:T(8,128)S(1)}, u32[]{:S(2)}, u32[]{:S(2)}) %collective-permute-start.8) | collective-permute-done | bytes 98336 | tf_op jit(solution)/shard_map/ppermute | solution.py:47
  35.0 5.1 %collective-permute-start.9 = (f32[2,96,128]{2,1,0:T(8,128)S(1)}, f32[2,96,128]{2,1,0:T(8,128)S(1)}, u32[]{:S(2)}, u32[]{:S(2)}) collective-permute-start(f32[2,96,128]{2,1,0:T(8,128)S(1)} %fusion.1.a_ref), channel_id=1, source_target_pairs={{0,224},{4,164},{8,232},{12,172},{16,240},{20,180},{24,248},{28,18... | collective-permute-start | bytes 294920 | tf_op jit(solution)/shard_map/ppermute | solution.py:47
  40.1 2.6 %collective-permute-done.9.b_ref = f32[2,96,128]{2,1,0:T(8,128)S(1)} collective-permute-done((f32[2,96,128]{2,1,0:T(8,128)S(1)}, f32[2,96,128]{2,1,0:T(8,128)S(1)}, u32[]{:S(2)}, u32[]{:S(2)}) %collective-permute-start.9) | collective-permute-done | bytes 98336 | tf_op jit(solution)/shard_map/ppermute | solution.py:47
  42.9 2.1 %collective-permute-start.12 = (f32[2,32,128]{2,1,0:T(8,128)S(1)}, f32[2,32,128]{2,1,0:T(8,128)S(1)}, u32[]{:S(2)}, u32[]{:S(2)}) collective-permute-start(f32[2,32,128]{2,1,0:T(8,128)S(1)} %solve.1), channel_id=1, source_target_pairs={{0,64},{4,68},{8,72},{12,76},{16,80},{20,84},{24,88},{28,92},{32,9... | collective-permute-start | bytes 98312 | tf_op jit(solution)/shard_map/ppermute | solution.py:47
  45.0 1.6 %collective-permute-start.11 = (f32[2,32,128]{2,1,0:T(8,128)S(1)}, f32[2,32,128]{2,1,0:T(8,128)S(1)}, u32[]{:S(2)}, u32[]{:S(2)}) collective-permute-start(f32[2,32,128]{2,1,0:T(8,128)S(1)} %solve.1), channel_id=1, source_target_pairs={{0,32},{4,228},{8,40},{12,236},{16,48},{20,244},{24,56},{28,252},{... | collective-permute-start | bytes 98312 | tf_op jit(solution)/shard_map/ppermute | solution.py:47
  46.7 2.3 %collective-permute-start.10 = (f32[2,32,128]{2,1,0:T(8,128)S(1)}, f32[2,32,128]{2,1,0:T(8,128)S(1)}, u32[]{:S(2)}, u32[]{:S(2)}) collective-permute-start(f32[2,32,128]{2,1,0:T(8,128)S(1)} %solve.1), channel_id=1, source_target_pairs={{0,96},{4,36},{8,104},{12,44},{16,112},{20,52},{24,120},{28,60},{3... | collective-permute-start | bytes 98312 | tf_op jit(solution)/shard_map/ppermute | solution.py:47
  49.0 3.4 %collective-permute-done.10 = f32[2,32,128]{2,1,0:T(8,128)S(1)} collective-permute-done((f32[2,32,128]{2,1,0:T(8,128)S(1)}, f32[2,32,128]{2,1,0:T(8,128)S(1)}, u32[]{:S(2)}, u32[]{:S(2)}) %collective-permute-start.10) | collective-permute-done | bytes 32800 | tf_op jit(solution)/shard_map/ppermute | solution.py:47
  52.4 1.8 %collective-permute-start.13 = (f32[8,32,128]{2,1,0:T(8,128)S(1)}, f32[8,32,128]{2,1,0:T(8,128)S(1)}, u32[]{:S(2)}, u32[]{:S(2)}) collective-permute-start(f32[8,32,128]{2,1,0:T(8,128)S(1)} %pad_maximum_fusion.refs_0_), channel_id=1, source_target_pairs={{0,24},{4,12},{8,16},{12,4},{16,8},{20,28},{24,0},{28,20},{32,56},... | collective-permute-start | bytes 393224 | tf_op jit(solution)/shard_map/ppermute | solution.py:47
  54.2 4.4 %collective-permute-done.13.refs_0_ = f32[8,32,128]{2,1,0:T(8,128)S(1)} collective-permute-done((f32[8,32,128]{2,1,0:T(8,128)S(1)}, f32[8,32,128]{2,1,0:T(8,128)S(1)}, u32[]{:S(2)}, u32[]{:S(2)}) %collective-permute-start.13) | collective-permute-done | bytes 131104 | tf_op jit(solution)/shard_map/ppermute | solution.py:47
  59.2 4.4 %collective-permute-done.14.refs_0_ = f32[8,32,128]{2,1,0:T(8,128)S(1)} collective-permute-done((f32[8,32,128]{2,1,0:T(8,128)S(1)}, f32[8,32,128]{2,1,0:T(8,128)S(1)}, u32[]{:S(2)}, u32[]{:S(2)}) %collective-permute-start.14) | collective-permute-done | bytes 131104 | tf_op jit(solution)/shard_map/ppermute | solution.py:47
  67.8 1.3 %finish.1 = (f32[8,8192]{1,0:T(8,128)}, f32[8,8192]{1,0:T(8,128)}, f32[8,128]{1,0:T(8,128)S(1)}) custom-call(f32[8,32,128]{2,1,0:T(8,128)S(1)} %collective-permute-done.15.refs_0_, bf16[8,8,8192]{2,1,0:T(8,128)(2,1)S(1)} %get-tuple-element.27.refs_1_, bf16[8,8,8192]{2,1,0:T(8,128)(2,1)S(1)} %get-tuple-element.28.refs_2_, f32[4,8,8192]{2,1,0:T(8,128)S(1)} %bitcast.13, ...), custom_call_target="tpu_custom_call" | custom-call | flops 3200000 | tf_op jit(solution)/shard_map/finish/pallas_call | solution.py:370
  69.9 2.9 %collective-permute-done.20 = f32[8,128]{1,0:T(8,128)S(1)} collective-permute-done((f32[8,128]{1,0:T(8,128)S(1)}, f32[8,128]{1,0:T(8,128)S(1)}, u32[]{:S(2)}, u32[]{:S(2)}) %collective-permute-start.20) | collective-permute-done | bytes 4128 | tf_op jit(solution)/shard_map/ppermute | solution.py:384
  73.0 4.6 %collective-permute-done.21 = f32[8,128]{1,0:T(8,128)S(1)} collective-permute-done((f32[8,128]{1,0:T(8,128)S(1)}, f32[8,128]{1,0:T(8,128)S(1)}, u32[]{:S(2)}, u32[]{:S(2)}) %collective-permute-start.21) | collective-permute-done | bytes 4128 | tf_op jit(solution)/shard_map/ppermute | solution.py:384
  (49 shorter events, 11.0 us)
Async XLA Ops:
  2.8 3.6 %collective-permute-start.3 = (f32[8,96,128]{2,1,0:T(8,128)S(1)}, f32[8,96,128]{2,1,0:T(8,128)S(1)}, u32[]{:S(2)}, u32[]{:S(2)}) collective-permute-start(f32[8,96,128]{2,1,0:T(8,128)S(1)} %get-tuple-element.31), channel_id=1, source_target_pairs={{0,4},{4,0},{1,5},{5,1},{2,6},{6,2},{3,7},{7,3},{8,12},{12,8},{9,1... | collective-permute-start | bytes 1179656 | tf_op jit(solution)/shard_map/ppermute | solution.py:51
  4.3 10.0 %collective-permute-start.2 = (f32[16,96,128]{2,1,0:T(8,128)S(1)}, f32[16,96,128]{2,1,0:T(8,128)S(1)}, u32[]{:S(2)}, u32[]{:S(2)}) collective-permute-start(f32[16,96,128]{2,1,0:T(8,128)S(1)} %spectra.8), channel_id=1, source_target_pairs={{0,4},{4,0},{1,5},{5,1},{2,6},{6,2},{3,7},{7,3},{8,12},{12,8},{9,1... | collective-permute-start | bytes 2359304 | tf_op jit(solution)/shard_map/ppermute | solution.py:51
  5.5 4.6 %collective-permute-start = (f32[8,96,128]{2,1,0:T(8,128)S(1)}, f32[8,96,128]{2,1,0:T(8,128)S(1)}, u32[]{:S(2)}, u32[]{:S(2)}) collective-permute-start(f32[8,96,128]{2,1,0:T(8,128)S(1)} %spectra.6), channel_id=1, source_target_pairs={{0,4},{4,0},{1,5},{5,1},{2,6},{6,2},{3,7},{7,3},{8,12},{12,8},{9,1... | collective-permute-start | bytes 1179656 | tf_op jit(solution)/shard_map/ppermute | solution.py:51
  6.4 7.9 %collective-permute-start.4 = (f32[8,96,128]{2,1,0:T(8,128)S(1)}, f32[8,96,128]{2,1,0:T(8,128)S(1)}, u32[]{:S(2)}, u32[]{:S(2)}) collective-permute-start(f32[8,96,128]{2,1,0:T(8,128)S(1)} %add.63), channel_id=1, source_target_pairs={{0,8},{4,28},{8,0},{12,20},{16,24},{20,12},{24,16},{28,4},{32,40},... | collective-permute-start | bytes 1179656 | tf_op jit(solution)/shard_map/ppermute | solution.py:47
  10.1 9.2 %collective-permute-start.1 = (f32[8,96,128]{2,1,0:T(8,128)S(1)}, f32[8,96,128]{2,1,0:T(8,128)S(1)}, u32[]{:S(2)}, u32[]{:S(2)}) collective-permute-start(f32[8,96,128]{2,1,0:T(8,128)S(1)} %add.60), channel_id=1, source_target_pairs={{0,8},{4,28},{8,0},{12,20},{16,24},{20,12},{24,16},{28,4},{32,40},... | collective-permute-start | bytes 1179656 | tf_op jit(solution)/shard_map/ppermute | solution.py:47
  14.3 7.4 %collective-permute-start.6 = (f32[4,96,128]{2,1,0:T(8,128)S(1)}, f32[4,96,128]{2,1,0:T(8,128)S(1)}, u32[]{:S(2)}, u32[]{:S(2)}) collective-permute-start(f32[4,96,128]{2,1,0:T(8,128)S(1)} %get-tuple-element.50), channel_id=1, source_target_pairs={{0,24},{4,12},{8,16},{12,4},{16,8},{20,28},{24,0},{28,20},{32,56},... | collective-permute-start | bytes 589832 | tf_op jit(solution)/shard_map/ppermute | solution.py:47
  17.2 6.9 %collective-permute-start.5 = (f32[4,96,128]{2,1,0:T(8,128)S(1)}, f32[4,96,128]{2,1,0:T(8,128)S(1)}, u32[]{:S(2)}, u32[]{:S(2)}) collective-permute-start(f32[4,96,128]{2,1,0:T(8,128)S(1)} %get-tuple-element.49), channel_id=1, source_target_pairs={{0,24},{4,12},{8,16},{12,4},{16,8},{20,28},{24,0},{28,20},{32,56},... | collective-permute-start | bytes 589832 | tf_op jit(solution)/shard_map/ppermute | solution.py:47
  21.8 5.8 %collective-permute-start.7 = (f32[4,96,128]{2,1,0:T(8,128)S(1)}, f32[4,96,128]{2,1,0:T(8,128)S(1)}, u32[]{:S(2)}, u32[]{:S(2)}) collective-permute-start(f32[4,96,128]{2,1,0:T(8,128)S(1)} %fusion), channel_id=1, source_target_pairs={{0,32},{4,228},{8,40},{12,236},{16,48},{20,244},{24,56},{28,252},{... | collective-permute-start | bytes 589832 | tf_op jit(solution)/shard_map/ppermute | solution.py:47
  27.6 7.3 %collective-permute-start.8 = (f32[2,96,128]{2,1,0:T(8,128)S(1)}, f32[2,96,128]{2,1,0:T(8,128)S(1)}, u32[]{:S(2)}, u32[]{:S(2)}) collective-permute-start(f32[2,96,128]{2,1,0:T(8,128)S(1)} %slice_add_fusion.6), channel_id=1, source_target_pairs={{0,96},{4,36},{8,104},{12,44},{16,112},{20,52},{24,120},{28,60},{3... | collective-permute-start | bytes 294920 | tf_op jit(solution)/shard_map/ppermute | solution.py:47
  35.0 7.7 %collective-permute-start.9 = (f32[2,96,128]{2,1,0:T(8,128)S(1)}, f32[2,96,128]{2,1,0:T(8,128)S(1)}, u32[]{:S(2)}, u32[]{:S(2)}) collective-permute-start(f32[2,96,128]{2,1,0:T(8,128)S(1)} %fusion.1.a_ref), channel_id=1, source_target_pairs={{0,224},{4,164},{8,232},{12,172},{16,240},{20,180},{24,248},{28,18... | collective-permute-start | bytes 294920 | tf_op jit(solution)/shard_map/ppermute | solution.py:47
  42.9 6.0 %collective-permute-start.12 = (f32[2,32,128]{2,1,0:T(8,128)S(1)}, f32[2,32,128]{2,1,0:T(8,128)S(1)}, u32[]{:S(2)}, u32[]{:S(2)}) collective-permute-start(f32[2,32,128]{2,1,0:T(8,128)S(1)} %solve.1), channel_id=1, source_target_pairs={{0,64},{4,68},{8,72},{12,76},{16,80},{20,84},{24,88},{28,92},{32,9... | collective-permute-start | bytes 98312 | tf_op jit(solution)/shard_map/ppermute | solution.py:47
  45.0 3.9 %collective-permute-start.11 = (f32[2,32,128]{2,1,0:T(8,128)S(1)}, f32[2,32,128]{2,1,0:T(8,128)S(1)}, u32[]{:S(2)}, u32[]{:S(2)}) collective-permute-start(f32[2,32,128]{2,1,0:T(8,128)S(1)} %solve.1), channel_id=1, source_target_pairs={{0,32},{4,228},{8,40},{12,236},{16,48},{20,244},{24,56},{28,252},{... | collective-permute-start | bytes 98312 | tf_op jit(solution)/shard_map/ppermute | solution.py:47
  46.7 5.7 %collective-permute-start.10 = (f32[2,32,128]{2,1,0:T(8,128)S(1)}, f32[2,32,128]{2,1,0:T(8,128)S(1)}, u32[]{:S(2)}, u32[]{:S(2)}) collective-permute-start(f32[2,32,128]{2,1,0:T(8,128)S(1)} %solve.1), channel_id=1, source_target_pairs={{0,96},{4,36},{8,104},{12,44},{16,112},{20,52},{24,120},{28,60},{3... | collective-permute-start | bytes 98312 | tf_op jit(solution)/shard_map/ppermute | solution.py:47
  52.4 6.3 %collective-permute-start.13 = (f32[8,32,128]{2,1,0:T(8,128)S(1)}, f32[8,32,128]{2,1,0:T(8,128)S(1)}, u32[]{:S(2)}, u32[]{:S(2)}) collective-permute-start(f32[8,32,128]{2,1,0:T(8,128)S(1)} %pad_maximum_fusion.refs_0_), channel_id=1, source_target_pairs={{0,24},{4,12},{8,16},{12,4},{16,8},{20,28},{24,0},{28,20},{32,56},... | collective-permute-start | bytes 393224 | tf_op jit(solution)/shard_map/ppermute | solution.py:47
  54.2 5.0 %collective-permute-start.18 = (f32[8,32,128]{2,1,0:T(8,128)S(1)}, f32[8,32,128]{2,1,0:T(8,128)S(1)}, u32[]{:S(2)}, u32[]{:S(2)}) collective-permute-start(f32[8,32,128]{2,1,0:T(8,128)S(1)} %pad_maximum_fusion.refs_0_), channel_id=1, source_target_pairs={{0,8},{4,28},{8,0},{12,20},{16,24},{20,12},{24,16},{28,4},{32,40},... | collective-permute-start | bytes 393224 | tf_op jit(solution)/shard_map/ppermute | solution.py:47
  58.7 5.0 %collective-permute-start.14 = (f32[8,32,128]{2,1,0:T(8,128)S(1)}, f32[8,32,128]{2,1,0:T(8,128)S(1)}, u32[]{:S(2)}, u32[]{:S(2)}) collective-permute-start(f32[8,32,128]{2,1,0:T(8,128)S(1)} %collective-permute-done.13.refs_0_), channel_id=1, source_target_pairs={{0,8},{4,28},{8,0},{12,20},{16,24},{20,12},{24,16},{28,4},{32,40},... | collective-permute-start | bytes 393224 | tf_op jit(solution)/shard_map/ppermute | solution.py:47
  58.7 7.6 %collective-permute-start.16 = (f32[8,32,128]{2,1,0:T(8,128)S(1)}, f32[8,32,128]{2,1,0:T(8,128)S(1)}, u32[]{:S(2)}, u32[]{:S(2)}) collective-permute-start(f32[8,32,128]{2,1,0:T(8,128)S(1)} %pad_maximum_fusion.refs_0_), channel_id=1, source_target_pairs={{0,4},{4,0},{1,5},{5,1},{2,6},{6,2},{3,7},{7,3},{8,12},{12,8},{9,1... | collective-permute-start | bytes 393224 | tf_op jit(solution)/shard_map/ppermute | solution.py:51
  58.7 8.7 %collective-permute-start.17 = (f32[8,32,128]{2,1,0:T(8,128)S(1)}, f32[8,32,128]{2,1,0:T(8,128)S(1)}, u32[]{:S(2)}, u32[]{:S(2)}) collective-permute-start(f32[8,32,128]{2,1,0:T(8,128)S(1)} %collective-permute-done.13.refs_0_), channel_id=1, source_target_pairs={{0,4},{4,0},{1,5},{5,1},{2,6},{6,2},{3,7},{7,3},{8,12},{12,8},{9,1... | collective-permute-start | bytes 393224 | tf_op jit(solution)/shard_map/ppermute | solution.py:51
  59.2 7.8 %collective-permute-start.19 = (f32[8,32,128]{2,1,0:T(8,128)S(1)}, f32[8,32,128]{2,1,0:T(8,128)S(1)}, u32[]{:S(2)}, u32[]{:S(2)}) collective-permute-start(f32[8,32,128]{2,1,0:T(8,128)S(1)} %collective-permute-done.18.refs_0_), channel_id=1, source_target_pairs={{0,4},{4,0},{1,5},{5,1},{2,6},{6,2},{3,7},{7,3},{8,12},{12,8},{9,1... | collective-permute-start | bytes 393224 | tf_op jit(solution)/shard_map/ppermute | solution.py:51
  63.7 4.2 %collective-permute-start.15 = (f32[8,32,128]{2,1,0:T(8,128)S(1)}, f32[8,32,128]{2,1,0:T(8,128)S(1)}, u32[]{:S(2)}, u32[]{:S(2)}) collective-permute-start(f32[8,32,128]{2,1,0:T(8,128)S(1)} %collective-permute-done.14.refs_0_), channel_id=1, source_target_pairs={{0,4},{4,0},{1,5},{5,1},{2,6},{6,2},{3,7},{7,3},{8,12},{12,8},{9,1... | collective-permute-start | bytes 393224 | tf_op jit(solution)/shard_map/ppermute | solution.py:51
  64.3 0.8 copy-start
  69.1 3.6 %collective-permute-start.20 = (f32[8,128]{1,0:T(8,128)S(1)}, f32[8,128]{1,0:T(8,128)S(1)}, u32[]{:S(2)}, u32[]{:S(2)}) collective-permute-start(f32[8,128]{1,0:T(8,128)S(1)} %get-tuple-element.48), channel_id=1, source_target_pairs={{0,1},{1,0},{2,3},{3,2},{4,5},{5,4},{6,7},{7,6},{8,9},{9,8},{10,11... | collective-permute-start | bytes 12296 | tf_op jit(solution)/shard_map/ppermute | solution.py:384
  72.8 4.8 %collective-permute-start.21 = (f32[8,128]{1,0:T(8,128)S(1)}, f32[8,128]{1,0:T(8,128)S(1)}, u32[]{:S(2)}, u32[]{:S(2)}) collective-permute-start(f32[8,128]{1,0:T(8,128)S(1)} %add.78), channel_id=1, source_target_pairs={{0,3},{1,2},{2,1},{3,0},{4,7},{5,6},{6,5},{7,4},{8,11},{9,10},{10,... | collective-permute-start | bytes 12296 | tf_op jit(solution)/shard_map/ppermute | solution.py:384

commit v3 on v2

--- a/solution.py
+++ b/solution.py
@@ -21,9 +21,13 @@
     return i ^ (i >> 1)
 
 
-def flip_pairs(size, shift, bit):
-    where = {gray((i - shift) % size): i for i in range(size)}
-    return [(i, where[gray((i - shift) % size) ^ (1 << bit)]) for i in range(size)]
+def label(axis, i):
+    return (gray(i >> 1) << 1) | (i & 1) if axis == "z" else gray(i)
+
+
+def flip_pairs(axis, size, shift, bits):
+    where = {label(axis, (i - shift) % size): i for i in range(size)}
+    return [(i, where[label(axis, (i - shift) % size) ^ bits]) for i in range(size)]
 
 
 STEPS = (
@@ -42,7 +46,7 @@
                 where = {"z": z, "x": x}
                 for at in steps:
                     axis, shift, bit = STEPS[c][at]
-                    where[axis] = dict(flip_pairs(sizes[axis], shift, bit))[where[axis]]
+                    where[axis] = dict(flip_pairs(axis, sizes[axis], shift, 1 << bit))[where[axis]]
                 pairs.append(((z * nx + x) * nc + c, (where["z"] * nx + where["x"]) * nc + c))
     return lax.ppermute(value, SEG, pairs)
 
@@ -55,7 +59,7 @@
     code = jnp.int32(0)
     for axis, shift, bit in STEPS[core][:-1]:
         ring = (lax.axis_index(axis) + (sizes[axis] - shift)) & (sizes[axis] - 1)
-        code = code * 2 + ((gray(ring) >> bit) & 1)
+        code = code * 2 + ((label(axis, ring) >> bit) & 1)
     return code * SUB
 
 
@@ -380,9 +384,12 @@
 
 
 def summed_over_bin(value, sizes):
-    for bit in range(sizes["y"].bit_length() - 1):
-        value = value + lax.ppermute(value, "y", flip_pairs(sizes["y"], 0, bit))
-    return value
+    got = [value]
+    for bits in range(1, sizes["y"]):
+        got.append(lax.ppermute(value, "y", flip_pairs("y", sizes["y"], 0, bits)))
+    while len(got) > 1:
+        got = [a + b for a, b in zip(got[::2], got[1::2])]
+    return got[0]
 
 
 def on_device(sizes, magnet_real, magnet_imag, detector_real, detector_imag, valid, intersection):
@@ -417,11 +424,12 @@
     halve(0, 3 * q, 4 * q, q)
     local(2 * q, q)
     halve(0, 2 * q, 3 * q, 0)
-    local(0, 2 * q)
+    local(q, q)
+    halve(1, 3 * e, 4 * e, e)
+    halve(1, 2 * e, 3 * e, 0)
+    local(0, q)
     h = jnp.stack([data[2], data[3]]).astype(F32)
     h = h.transpose(2, 0, 1, 3).reshape(2 * DET, CH, bins)
-    halve(1, 3 * e, 4 * e, e)
-    halve(1, 2 * e, 3 * e, 0)
     halve(2, e, 2 * e, 0)
     halve(3, e // 2, e, 0)
     last = summed(0, SUB)

time: 78.5 us -> 78 us (level)
  the two profiles are of different devices: /device:TPU:24 before, /device:TPU:2 now
where the time goes in v3:
time: 78 us; the launch traced here: 76.5 us
  starting transfers between devices  34.6 us (44%)
  waiting for transfers between devices  27.5 us (35%)
  Pallas kernels  11.2 us (14%)
  other arithmetic  1.63 us (2%)
  between operations  0.83 us (1%)
    ppermute x13, starting transfers between devices, swap_steps(): return lax.ppermute(value, SEG, pairs)  28.9 us
    ppermute x13, waiting for transfers between devices, swap_steps(): return lax.ppermute(value, SEG, pairs)  23.1 us
    pallas_call x7, Pallas kernels, spectra(): pl.pallas_call(lambda *refs: spectra_body(sizes, half, which, first, coun...  4.9 us
    ppermute x3, waiting for transfers between devices, summed_over_bin(): got.append(lax.ppermute(value, 'y', flip_pairs('y', sizes['y'], 0, bits)))  4.39 us
    ppermute x3, starting transfers between devices, summed_over_bin(): got.append(lax.ppermute(value, 'y', flip_pairs('y', sizes['y'], 0, bits)))  4.31 us
    pallas_call x7, Pallas kernels, clean(): pl.pallas_call(lambda *refs: clean_body(sizes, half, which, first, count,...  2.7 us
    pallas_call x1, Pallas kernels, front(): pl.pallas_call(lambda *refs: front_body(sizes, half, first, count, *refs)...  2.11 us
  transfers between devices with their start and end apart: 24, of which 14 were waited for; matrix products, arithmetic and copies ran while one was open for 2% of the time, Pallas kernels for 10%

profile of v3, /device:TPU:2, one launch (start us, length us, event | category | flops | bytes accessed | tf_op | source)
XLA Modules:
  0.0 76.5 jit_solution(9945692439674507044)
XLA Ops:
  0.6 2.1 %front.1 = (f32[8,96,128]{2,1,0:T(8,128)S(1)}, f32[8,8,128]{2,1,0:T(8,128)S(1)}, bf16[8,8,8192]{2,1,0:T(8,128)(2,1)S(1)}, bf16[8,8,8192]{2,1,0:T(8,128)(2,1)S(1)...) custom-call(s32[8]{0:T(128)} %refs_0_.1, bf16[8,8,8192]{2,1,0:T(8,128)(2,1)} %refs_1_.1, ...), custom_call_target="tpu_custom_call" | custom-call | flops 4000000 | tf_op jit(solution)/shard_map/front/pallas_call | solution.py:171
  5.7 2.3 %collective-permute-start.3 = (f32[8,96,128]{2,1,0:T(8,128)S(1)}, f32[8,96,128]{2,1,0:T(8,128)S(1)}, u32[]{:S(2)}, u32[]{:S(2)}) collective-permute-start(f32[8,96,128]{2,1,0:T(8,128)S(1)} %add.64), channel_id=1, source_target_pairs={{0,8},{4,28},{8,0},{12,20},{16,24},{20,12},{24,16},{28,4},{32,40},... | collective-permute-start | bytes 1179656 | tf_op jit(solution)/shard_map/ppermute | solution.py:51
  11.6 2.2 %collective-permute-done.3 = f32[8,96,128]{2,1,0:T(8,128)S(1)} collective-permute-done((f32[8,96,128]{2,1,0:T(8,128)S(1)}, f32[8,96,128]{2,1,0:T(8,128)S(1)}, u32[]{:S(2)}, u32[]{:S(2)}) %collective-permute-start.3) | collective-permute-done | bytes 393248 | tf_op jit(solution)/shard_map/ppermute | solution.py:51
  13.9 1.4 %collective-permute-start.7 = (f32[4,96,128]{2,1,0:T(8,128)S(1)}, f32[4,96,128]{2,1,0:T(8,128)S(1)}, u32[]{:S(2)}, u32[]{:S(2)}) collective-permute-start(f32[4,96,128]{2,1,0:T(8,128)S(1)} %get-tuple-element.50), channel_id=1, source_target_pairs={{0,24},{4,12},{8,16},{12,4},{16,8},{20,28},{24,0},{28,20},{32,56},... | collective-permute-start | bytes 589832 | tf_op jit(solution)/shard_map/ppermute | solution.py:51
  16.8 2.3 %collective-permute-done.1 = f32[8,96,128]{2,1,0:T(8,128)S(1)} collective-permute-done((f32[8,96,128]{2,1,0:T(8,128)S(1)}, f32[8,96,128]{2,1,0:T(8,128)S(1)}, u32[]{:S(2)}, u32[]{:S(2)}) %collective-permute-start.1) | collective-permute-done | bytes 393248 | tf_op jit(solution)/shard_map/ppermute | solution.py:51
  19.8 1.9 %collective-permute-start.8 = (f32[4,96,128]{2,1,0:T(8,128)S(1)}, f32[4,96,128]{2,1,0:T(8,128)S(1)}, u32[]{:S(2)}, u32[]{:S(2)}) collective-permute-start(f32[4,96,128]{2,1,0:T(8,128)S(1)} %slice_add_fusion), channel_id=1, source_target_pairs={{0,32},{4,228},{8,40},{12,236},{16,48},{20,244},{24,56},{28,252},{... | collective-permute-start | bytes 589832 | tf_op jit(solution)/shard_map/ppermute | solution.py:51
  21.9 3.7 %collective-permute-done.8 = f32[4,96,128]{2,1,0:T(8,128)S(1)} collective-permute-done((f32[4,96,128]{2,1,0:T(8,128)S(1)}, f32[4,96,128]{2,1,0:T(8,128)S(1)}, u32[]{:S(2)}, u32[]{:S(2)}) %collective-permute-start.8) | collective-permute-done | bytes 196640 | tf_op jit(solution)/shard_map/ppermute | solution.py:51
  25.6 3.2 %collective-permute-start.9 = (f32[2,96,128]{2,1,0:T(8,128)S(1)}, f32[2,96,128]{2,1,0:T(8,128)S(1)}, u32[]{:S(2)}, u32[]{:S(2)}) collective-permute-start(f32[2,96,128]{2,1,0:T(8,128)S(1)} %slice_add_fusion.7), channel_id=1, source_target_pairs={{0,64},{4,68},{8,72},{12,76},{16,80},{20,84},{24,88},{28,92},{32,9... | collective-permute-start | bytes 294920 | tf_op jit(solution)/shard_map/ppermute | solution.py:51
  28.8 2.6 %collective-permute-done.9 = f32[2,96,128]{2,1,0:T(8,128)S(1)} collective-permute-done((f32[2,96,128]{2,1,0:T(8,128)S(1)}, f32[2,96,128]{2,1,0:T(8,128)S(1)}, u32[]{:S(2)}, u32[]{:S(2)}) %collective-permute-start.9) | collective-permute-done | bytes 98336 | tf_op jit(solution)/shard_map/ppermute | solution.py:51
  31.5 7.1 %collective-permute-start.10 = (f32[2,96,128]{2,1,0:T(8,128)S(1)}, f32[2,96,128]{2,1,0:T(8,128)S(1)}, u32[]{:S(2)}, u32[]{:S(2)}) collective-permute-start(f32[2,96,128]{2,1,0:T(8,128)S(1)} %fusion.a_ref), channel_id=1, source_target_pairs={{0,192},{4,196},{8,200},{12,204},{16,208},{20,212},{24,216},{28,22... | collective-permute-start | bytes 294920 | tf_op jit(solution)/shard_map/ppermute | solution.py:51
  38.6 3.6 %collective-permute-done.10.b_ref = f32[2,96,128]{2,1,0:T(8,128)S(1)} collective-permute-done((f32[2,96,128]{2,1,0:T(8,128)S(1)}, f32[2,96,128]{2,1,0:T(8,128)S(1)}, u32[]{:S(2)}, u32[]{:S(2)}) %collective-permute-start.10) | collective-permute-done | bytes 98336 | tf_op jit(solution)/shard_map/ppermute | solution.py:51
  42.4 2.0 %collective-permute-start.11 = (f32[2,32,128]{2,1,0:T(8,128)S(1)}, f32[2,32,128]{2,1,0:T(8,128)S(1)}, u32[]{:S(2)}, u32[]{:S(2)}) collective-permute-start(f32[2,32,128]{2,1,0:T(8,128)S(1)} %solve.1), channel_id=1, source_target_pairs={{0,64},{4,68},{8,72},{12,76},{16,80},{20,84},{24,88},{28,92},{32,9... | collective-permute-start | bytes 98312 | tf_op jit(solution)/shard_map/ppermute | solution.py:51
  44.6 2.2 %collective-permute-start.13 = (f32[2,32,128]{2,1,0:T(8,128)S(1)}, f32[2,32,128]{2,1,0:T(8,128)S(1)}, u32[]{:S(2)}, u32[]{:S(2)}) collective-permute-start(f32[2,32,128]{2,1,0:T(8,128)S(1)} %solve.1), channel_id=1, source_target_pairs={{0,96},{4,36},{8,104},{12,44},{16,112},{20,52},{24,120},{28,60},{3... | collective-permute-start | bytes 98312 | tf_op jit(solution)/shard_map/ppermute | solution.py:51
  48.4 2.0 %collective-permute-done.13 = f32[2,32,128]{2,1,0:T(8,128)S(1)} collective-permute-done((f32[2,32,128]{2,1,0:T(8,128)S(1)}, f32[2,32,128]{2,1,0:T(8,128)S(1)}, u32[]{:S(2)}, u32[]{:S(2)}) %collective-permute-start.13) | collective-permute-done | bytes 32800 | tf_op jit(solution)/shard_map/ppermute | solution.py:51
  50.4 1.6 %collective-permute-start.14 = (f32[8,32,128]{2,1,0:T(8,128)S(1)}, f32[8,32,128]{2,1,0:T(8,128)S(1)}, u32[]{:S(2)}, u32[]{:S(2)}) collective-permute-start(f32[8,32,128]{2,1,0:T(8,128)S(1)} %pad_maximum_fusion.refs_0_), channel_id=1, source_target_pairs={{0,24},{4,12},{8,16},{12,4},{16,8},{20,28},{24,0},{28,20},{32,56},... | collective-permute-start | bytes 393224 | tf_op jit(solution)/shard_map/ppermute | solution.py:51
  52.0 2.1 %collective-permute-start.19 = (f32[8,32,128]{2,1,0:T(8,128)S(1)}, f32[8,32,128]{2,1,0:T(8,128)S(1)}, u32[]{:S(2)}, u32[]{:S(2)}) collective-permute-start(f32[8,32,128]{2,1,0:T(8,128)S(1)} %pad_maximum_fusion.refs_0_), channel_id=1, source_target_pairs={{0,8},{4,28},{8,0},{12,20},{16,24},{20,12},{24,16},{28,4},{32,40},... | collective-permute-start | bytes 393224 | tf_op jit(solution)/shard_map/ppermute | solution.py:51
  54.0 1.8 %collective-permute-done.14.refs_0_ = f32[8,32,128]{2,1,0:T(8,128)S(1)} collective-permute-done((f32[8,32,128]{2,1,0:T(8,128)S(1)}, f32[8,32,128]{2,1,0:T(8,128)S(1)}, u32[]{:S(2)}, u32[]{:S(2)}) %collective-permute-start.14) | collective-permute-done | bytes 131104 | tf_op jit(solution)/shard_map/ppermute | solution.py:51
  55.9 2.8 %collective-permute-start.15 = (f32[8,32,128]{2,1,0:T(8,128)S(1)}, f32[8,32,128]{2,1,0:T(8,128)S(1)}, u32[]{:S(2)}, u32[]{:S(2)}) collective-permute-start(f32[8,32,128]{2,1,0:T(8,128)S(1)} %collective-permute-done.14.refs_0_), channel_id=1, source_target_pairs={{0,8},{4,28},{8,0},{12,20},{16,24},{20,12},{24,16},{28,4},{32,40},... | collective-permute-start | bytes 393224 | tf_op jit(solution)/shard_map/ppermute | solution.py:51
  59.2 2.4 %collective-permute-done.15.refs_0_ = f32[8,32,128]{2,1,0:T(8,128)S(1)} collective-permute-done((f32[8,32,128]{2,1,0:T(8,128)S(1)}, f32[8,32,128]{2,1,0:T(8,128)S(1)}, u32[]{:S(2)}, u32[]{:S(2)}) %collective-permute-start.15) | collective-permute-done | bytes 131104 | tf_op jit(solution)/shard_map/ppermute | solution.py:51
  65.8 1.3 %finish.1 = (f32[8,8192]{1,0:T(8,128)}, f32[8,8192]{1,0:T(8,128)}, f32[8,128]{1,0:T(8,128)S(1)}) custom-call(f32[8,32,128]{2,1,0:T(8,128)S(1)} %collective-permute-done.16.refs_0_, bf16[8,8,8192]{2,1,0:T(8,128)(2,1)S(1)} %get-tuple-element.27.refs_1_, bf16[8,8,8192]{2,1,0:T(8,128)(2,1)S(1)} %get-tuple-element.28.refs_2_, f32[4,8,8192]{2,1,0:T(8,128)S(1)} %bitcast.13, ...), custom_call_target="tpu_custom_call" | custom-call | flops 3200000 | tf_op jit(solution)/shard_map/finish/pallas_call | solution.py:374
  67.1 1.4 %collective-permute-start.21 = (f32[8,128]{1,0:T(8,128)S(1)}, f32[8,128]{1,0:T(8,128)S(1)}, u32[]{:S(2)}, u32[]{:S(2)}) collective-permute-start(f32[8,128]{1,0:T(8,128)S(1)} %get-tuple-element.48), channel_id=1, source_target_pairs={{0,1},{1,0},{2,3},{3,2},{4,5},{5,4},{6,7},{7,6},{8,9},{9,8},{10,11... | collective-permute-start | bytes 12296 | tf_op jit(solution)/shard_map/ppermute | solution.py:389
  68.5 2.2 %collective-permute-start.22 = (f32[8,128]{1,0:T(8,128)S(1)}, f32[8,128]{1,0:T(8,128)S(1)}, u32[]{:S(2)}, u32[]{:S(2)}) collective-permute-start(f32[8,128]{1,0:T(8,128)S(1)} %get-tuple-element.48), channel_id=1, source_target_pairs={{0,3},{1,2},{2,1},{3,0},{4,7},{5,6},{6,5},{7,4},{8,11},{9,10},{10,... | collective-permute-start | bytes 12296 | tf_op jit(solution)/shard_map/ppermute | solution.py:389
  71.4 1.9 %collective-permute-done.22 = f32[8,128]{1,0:T(8,128)S(1)} collective-permute-done((f32[8,128]{1,0:T(8,128)S(1)}, f32[8,128]{1,0:T(8,128)S(1)}, u32[]{:S(2)}, u32[]{:S(2)}) %collective-permute-start.22) | collective-permute-done | bytes 4128 | tf_op jit(solution)/shard_map/ppermute | solution.py:389
  73.3 2.5 %collective-permute-done.23 = f32[8,128]{1,0:T(8,128)S(1)} collective-permute-done((f32[8,128]{1,0:T(8,128)S(1)}, f32[8,128]{1,0:T(8,128)S(1)}, u32[]{:S(2)}, u32[]{:S(2)}) %collective-permute-start.23) | collective-permute-done | bytes 4128 | tf_op jit(solution)/shard_map/ppermute | solution.py:389
  (54 shorter events, 17.1 us)
Async XLA Ops:
  2.8 2.9 %collective-permute-start.2 = (f32[8,96,128]{2,1,0:T(8,128)S(1)}, f32[8,96,128]{2,1,0:T(8,128)S(1)}, u32[]{:S(2)}, u32[]{:S(2)}) collective-permute-start(f32[8,96,128]{2,1,0:T(8,128)S(1)} %get-tuple-element.31), channel_id=1, source_target_pairs={{0,4},{4,0},{1,5},{5,1},{2,6},{6,2},{3,7},{7,3},{8,12},{12,8},{9,1... | collective-permute-start | bytes 1179656 | tf_op jit(solution)/shard_map/ppermute | solution.py:55
  3.6 6.7 %collective-permute-start = (f32[8,96,128]{2,1,0:T(8,128)S(1)}, f32[8,96,128]{2,1,0:T(8,128)S(1)}, u32[]{:S(2)}, u32[]{:S(2)}) collective-permute-start(f32[8,96,128]{2,1,0:T(8,128)S(1)} %spectra.8), channel_id=1, source_target_pairs={{0,4},{4,0},{1,5},{5,1},{2,6},{6,2},{3,7},{7,3},{8,12},{12,8},{9,1... | collective-permute-start | bytes 1179656 | tf_op jit(solution)/shard_map/ppermute | solution.py:55
  4.8 6.8 %collective-permute-start.4 = (f32[8,96,128]{2,1,0:T(8,128)S(1)}, f32[8,96,128]{2,1,0:T(8,128)S(1)}, u32[]{:S(2)}, u32[]{:S(2)}) collective-permute-start(f32[8,96,128]{2,1,0:T(8,128)S(1)} %spectra.11), channel_id=1, source_target_pairs={{0,4},{4,0},{1,5},{5,1},{2,6},{6,2},{3,7},{7,3},{8,12},{12,8},{9,1... | collective-permute-start | bytes 1179656 | tf_op jit(solution)/shard_map/ppermute | solution.py:55
  5.7 8.1 %collective-permute-start.3 = (f32[8,96,128]{2,1,0:T(8,128)S(1)}, f32[8,96,128]{2,1,0:T(8,128)S(1)}, u32[]{:S(2)}, u32[]{:S(2)}) collective-permute-start(f32[8,96,128]{2,1,0:T(8,128)S(1)} %add.64), channel_id=1, source_target_pairs={{0,8},{4,28},{8,0},{12,20},{16,24},{20,12},{24,16},{28,4},{32,40},... | collective-permute-start | bytes 1179656 | tf_op jit(solution)/shard_map/ppermute | solution.py:51
  8.7 8.0 %collective-permute-start.6 = (f32[8,96,128]{2,1,0:T(8,128)S(1)}, f32[8,96,128]{2,1,0:T(8,128)S(1)}, u32[]{:S(2)}, u32[]{:S(2)}) collective-permute-start(f32[8,96,128]{2,1,0:T(8,128)S(1)} %spectra.13), channel_id=1, source_target_pairs={{0,4},{4,0},{1,5},{5,1},{2,6},{6,2},{3,7},{7,3},{8,12},{12,8},{9,1... | collective-permute-start | bytes 1179656 | tf_op jit(solution)/shard_map/ppermute | solution.py:55
  10.3 8.7 %collective-permute-start.1 = (f32[8,96,128]{2,1,0:T(8,128)S(1)}, f32[8,96,128]{2,1,0:T(8,128)S(1)}, u32[]{:S(2)}, u32[]{:S(2)}) collective-permute-start(f32[8,96,128]{2,1,0:T(8,128)S(1)} %add.63), channel_id=1, source_target_pairs={{0,8},{4,28},{8,0},{12,20},{16,24},{20,12},{24,16},{28,4},{32,40},... | collective-permute-start | bytes 1179656 | tf_op jit(solution)/shard_map/ppermute | solution.py:51
  13.9 5.9 %collective-permute-start.7 = (f32[4,96,128]{2,1,0:T(8,128)S(1)}, f32[4,96,128]{2,1,0:T(8,128)S(1)}, u32[]{:S(2)}, u32[]{:S(2)}) collective-permute-start(f32[4,96,128]{2,1,0:T(8,128)S(1)} %get-tuple-element.50), channel_id=1, source_target_pairs={{0,24},{4,12},{8,16},{12,4},{16,8},{20,28},{24,0},{28,20},{32,56},... | collective-permute-start | bytes 589832 | tf_op jit(solution)/shard_map/ppermute | solution.py:51
  15.9 6.0 %collective-permute-start.5 = (f32[4,96,128]{2,1,0:T(8,128)S(1)}, f32[4,96,128]{2,1,0:T(8,128)S(1)}, u32[]{:S(2)}, u32[]{:S(2)}) collective-permute-start(f32[4,96,128]{2,1,0:T(8,128)S(1)} %get-tuple-element.49), channel_id=1, source_target_pairs={{0,24},{4,12},{8,16},{12,4},{16,8},{20,28},{24,0},{28,20},{32,56},... | collective-permute-start | bytes 589832 | tf_op jit(solution)/shard_map/ppermute | solution.py:51
  19.8 5.8 %collective-permute-start.8 = (f32[4,96,128]{2,1,0:T(8,128)S(1)}, f32[4,96,128]{2,1,0:T(8,128)S(1)}, u32[]{:S(2)}, u32[]{:S(2)}) collective-permute-start(f32[4,96,128]{2,1,0:T(8,128)S(1)} %slice_add_fusion), channel_id=1, source_target_pairs={{0,32},{4,228},{8,40},{12,236},{16,48},{20,244},{24,56},{28,252},{... | collective-permute-start | bytes 589832 | tf_op jit(solution)/shard_map/ppermute | solution.py:51
  25.6 5.8 %collective-permute-start.9 = (f32[2,96,128]{2,1,0:T(8,128)S(1)}, f32[2,96,128]{2,1,0:T(8,128)S(1)}, u32[]{:S(2)}, u32[]{:S(2)}) collective-permute-start(f32[2,96,128]{2,1,0:T(8,128)S(1)} %slice_add_fusion.7), channel_id=1, source_target_pairs={{0,64},{4,68},{8,72},{12,76},{16,80},{20,84},{24,88},{28,92},{32,9... | collective-permute-start | bytes 294920 | tf_op jit(solution)/shard_map/ppermute | solution.py:51
  31.5 10.7 %collective-permute-start.10 = (f32[2,96,128]{2,1,0:T(8,128)S(1)}, f32[2,96,128]{2,1,0:T(8,128)S(1)}, u32[]{:S(2)}, u32[]{:S(2)}) collective-permute-start(f32[2,96,128]{2,1,0:T(8,128)S(1)} %fusion.a_ref), channel_id=1, source_target_pairs={{0,192},{4,196},{8,200},{12,204},{16,208},{20,212},{24,216},{28,22... | collective-permute-start | bytes 294920 | tf_op jit(solution)/shard_map/ppermute | solution.py:51
  42.4 5.0 %collective-permute-start.11 = (f32[2,32,128]{2,1,0:T(8,128)S(1)}, f32[2,32,128]{2,1,0:T(8,128)S(1)}, u32[]{:S(2)}, u32[]{:S(2)}) collective-permute-start(f32[2,32,128]{2,1,0:T(8,128)S(1)} %solve.1), channel_id=1, source_target_pairs={{0,64},{4,68},{8,72},{12,76},{16,80},{20,84},{24,88},{28,92},{32,9... | collective-permute-start | bytes 98312 | tf_op jit(solution)/shard_map/ppermute | solution.py:51
  44.4 3.9 %collective-permute-start.12 = (f32[2,32,128]{2,1,0:T(8,128)S(1)}, f32[2,32,128]{2,1,0:T(8,128)S(1)}, u32[]{:S(2)}, u32[]{:S(2)}) collective-permute-start(f32[2,32,128]{2,1,0:T(8,128)S(1)} %solve.1), channel_id=1, source_target_pairs={{0,32},{4,228},{8,40},{12,236},{16,48},{20,244},{24,56},{28,252},{... | collective-permute-start | bytes 98312 | tf_op jit(solution)/shard_map/ppermute | solution.py:51
  44.6 5.7 %collective-permute-start.13 = (f32[2,32,128]{2,1,0:T(8,128)S(1)}, f32[2,32,128]{2,1,0:T(8,128)S(1)}, u32[]{:S(2)}, u32[]{:S(2)}) collective-permute-start(f32[2,32,128]{2,1,0:T(8,128)S(1)} %solve.1), channel_id=1, source_target_pairs={{0,96},{4,36},{8,104},{12,44},{16,112},{20,52},{24,120},{28,60},{3... | collective-permute-start | bytes 98312 | tf_op jit(solution)/shard_map/ppermute | solution.py:51
  50.4 5.5 %collective-permute-start.14 = (f32[8,32,128]{2,1,0:T(8,128)S(1)}, f32[8,32,128]{2,1,0:T(8,128)S(1)}, u32[]{:S(2)}, u32[]{:S(2)}) collective-permute-start(f32[8,32,128]{2,1,0:T(8,128)S(1)} %pad_maximum_fusion.refs_0_), channel_id=1, source_target_pairs={{0,24},{4,12},{8,16},{12,4},{16,8},{20,28},{24,0},{28,20},{32,56},... | collective-permute-start | bytes 393224 | tf_op jit(solution)/shard_map/ppermute | solution.py:51
  52.0 7.2 %collective-permute-start.19 = (f32[8,32,128]{2,1,0:T(8,128)S(1)}, f32[8,32,128]{2,1,0:T(8,128)S(1)}, u32[]{:S(2)}, u32[]{:S(2)}) collective-permute-start(f32[8,32,128]{2,1,0:T(8,128)S(1)} %pad_maximum_fusion.refs_0_), channel_id=1, source_target_pairs={{0,8},{4,28},{8,0},{12,20},{16,24},{20,12},{24,16},{28,4},{32,40},... | collective-permute-start | bytes 393224 | tf_op jit(solution)/shard_map/ppermute | solution.py:51
  55.9 5.7 %collective-permute-start.15 = (f32[8,32,128]{2,1,0:T(8,128)S(1)}, f32[8,32,128]{2,1,0:T(8,128)S(1)}, u32[]{:S(2)}, u32[]{:S(2)}) collective-permute-start(f32[8,32,128]{2,1,0:T(8,128)S(1)} %collective-permute-done.14.refs_0_), channel_id=1, source_target_pairs={{0,8},{4,28},{8,0},{12,20},{16,24},{20,12},{24,16},{28,4},{32,40},... | collective-permute-start | bytes 393224 | tf_op jit(solution)/shard_map/ppermute | solution.py:51
  58.7 5.5 %collective-permute-start.17 = (f32[8,32,128]{2,1,0:T(8,128)S(1)}, f32[8,32,128]{2,1,0:T(8,128)S(1)}, u32[]{:S(2)}, u32[]{:S(2)}) collective-permute-start(f32[8,32,128]{2,1,0:T(8,128)S(1)} %pad_maximum_fusion.refs_0_), channel_id=1, source_target_pairs={{0,4},{4,0},{1,5},{5,1},{2,6},{6,2},{3,7},{7,3},{8,12},{12,8},{9,1... | collective-permute-start | bytes 393224 | tf_op jit(solution)/shard_map/ppermute | solution.py:55
  58.7 6.7 %collective-permute-start.18 = (f32[8,32,128]{2,1,0:T(8,128)S(1)}, f32[8,32,128]{2,1,0:T(8,128)S(1)}, u32[]{:S(2)}, u32[]{:S(2)}) collective-permute-start(f32[8,32,128]{2,1,0:T(8,128)S(1)} %collective-permute-done.14.refs_0_), channel_id=1, source_target_pairs={{0,4},{4,0},{1,5},{5,1},{2,6},{6,2},{3,7},{7,3},{8,12},{12,8},{9,1... | collective-permute-start | bytes 393224 | tf_op jit(solution)/shard_map/ppermute | solution.py:55
  59.2 5.8 %collective-permute-start.20 = (f32[8,32,128]{2,1,0:T(8,128)S(1)}, f32[8,32,128]{2,1,0:T(8,128)S(1)}, u32[]{:S(2)}, u32[]{:S(2)}) collective-permute-start(f32[8,32,128]{2,1,0:T(8,128)S(1)} %collective-permute-done.19.refs_0_), channel_id=1, source_target_pairs={{0,4},{4,0},{1,5},{5,1},{2,6},{6,2},{3,7},{7,3},{8,12},{12,8},{9,1... | collective-permute-start | bytes 393224 | tf_op jit(solution)/shard_map/ppermute | solution.py:55
  61.6 4.2 %collective-permute-start.16 = (f32[8,32,128]{2,1,0:T(8,128)S(1)}, f32[8,32,128]{2,1,0:T(8,128)S(1)}, u32[]{:S(2)}, u32[]{:S(2)}) collective-permute-start(f32[8,32,128]{2,1,0:T(8,128)S(1)} %collective-permute-done.15.refs_0_), channel_id=1, source_target_pairs={{0,4},{4,0},{1,5},{5,1},{2,6},{6,2},{3,7},{7,3},{8,12},{12,8},{9,1... | collective-permute-start | bytes 393224 | tf_op jit(solution)/shard_map/ppermute | solution.py:55
  67.1 4.3 %collective-permute-start.21 = (f32[8,128]{1,0:T(8,128)S(1)}, f32[8,128]{1,0:T(8,128)S(1)}, u32[]{:S(2)}, u32[]{:S(2)}) collective-permute-start(f32[8,128]{1,0:T(8,128)S(1)} %get-tuple-element.48), channel_id=1, source_target_pairs={{0,1},{1,0},{2,3},{3,2},{4,5},{5,4},{6,7},{7,6},{8,9},{9,8},{10,11... | collective-permute-start | bytes 12296 | tf_op jit(solution)/shard_map/ppermute | solution.py:389
  68.5 4.8 %collective-permute-start.22 = (f32[8,128]{1,0:T(8,128)S(1)}, f32[8,128]{1,0:T(8,128)S(1)}, u32[]{:S(2)}, u32[]{:S(2)}) collective-permute-start(f32[8,128]{1,0:T(8,128)S(1)} %get-tuple-element.48), channel_id=1, source_target_pairs={{0,3},{1,2},{2,1},{3,0},{4,7},{5,6},{6,5},{7,4},{8,11},{9,10},{10,... | collective-permute-start | bytes 12296 | tf_op jit(solution)/shard_map/ppermute | solution.py:389
  70.7 5.1 %collective-permute-start.23 = (f32[8,128]{1,0:T(8,128)S(1)}, f32[8,128]{1,0:T(8,128)S(1)}, u32[]{:S(2)}, u32[]{:S(2)}) collective-permute-start(f32[8,128]{1,0:T(8,128)S(1)} %get-tuple-element.48), channel_id=1, source_target_pairs={{0,2},{1,3},{2,0},{3,1},{4,6},{5,7},{6,4},{7,5},{8,10},{9,11},{10,... | collective-permute-start | bytes 12296 | tf_op jit(solution)/shard_map/ppermute | solution.py:389
  (1 other events, 0.8 us)

commit v4 on v3

--- a/solution.py
+++ b/solution.py
@@ -32,7 +32,7 @@
 
 STEPS = (
     (("x", 0, 0), ("x", 0, 1), ("z", 0, 0), ("z", 0, 1), ("z", 0, 2)),
-    (("x", 0, 1), ("x", 0, 0), ("z", 1, 0), ("z", 1, 2), ("z", 1, 1)),
+    (("x", 0, 1), ("x", 0, 0), ("z", 2, 0), ("z", 2, 1), ("z", 2, 2)),
 )
 SUB = 2
 
@@ -248,6 +248,28 @@
     return [cols_r[8] * inv, cols_i[8] * inv, cols_r[9] * inv, cols_i[9] * inv]
 
 
+def added_body(starts, count, *refs):
+    for u in range(count):
+        for r in range(ROWS // CH):
+            rows = pl.ds(CH * r, CH)
+            total = refs[0][starts[0] + u, rows, :]
+            for start, ref in zip(starts[1:], refs[1:-1]):
+                total = total + ref[start + u, rows, :]
+            refs[-1][u, rows, :] = total
+
+
+def added(arrays, starts, count):
+    return pl.pallas_call(
+        lambda *refs: added_body(starts, count, *refs),
+        out_shape=jax.ShapeDtypeStruct((count, ROWS, LANES), F32),
+        in_specs=[pl.BlockSpec(memory_space=VMEM)] * len(arrays),
+        out_specs=pl.BlockSpec(memory_space=VMEM),
+        compiler_params=params(),
+        cost_estimate=cost(count, 50000),
+        name="added",
+    )(*arrays)
+
+
 def solve_body(a_ref, b_ref, out_ref):
     for u in range(SUB):
         rows = [
@@ -308,8 +330,8 @@
     return [w_ref[p, CH * q : CH * (q + 1), :] for q in range(4)]
 
 
-def clean_body(sizes, half, which, first, count, w_ref, *refs):
-    data, (out_ref, num_ref) = refs[:4], refs[4:]
+def clean_body(sizes, half, which, first, count, last, w_ref, *refs):
+    data, sums, (out_ref, num_ref) = refs[:4], refs[4:-2], refs[-2:]
     codes = half_codes(sizes, half)
 
     def step(p, num):
@@ -319,68 +341,56 @@
         out_ref[p, CH : 2 * CH, :] = imag
         return num + part
 
-    num_ref[...] = lax.fori_loop(0, count, step, jnp.zeros((CH, LANES), F32))
-
-
-def clean(sizes, half, filters, rest, which, first):
+    num = lax.fori_loop(0, count, step, jnp.zeros((CH, LANES), F32))
+    for sum_ref in sums:
+        num = num + sum_ref[...]
+    if last:
+        weight = data[3][...]
+        square = jnp.sum(weight * weight)
+        lane = lax.broadcasted_iota(jnp.int32, (CH, LANES), 1)
+        total = jnp.broadcast_to(jnp.sum(num, axis=1, keepdims=True), (CH, LANES))
+        num = jnp.where(lane == 0, total, square)
+    num_ref[...] = num
+
+
+def clean(sizes, half, filters, rest, which, first, sums):
     count = filters.shape[0]
-    return pl.pallas_call(
-        lambda *refs: clean_body(sizes, half, which, first, count, *refs),
+    last = which == 1 and first + count == half
+    args = (filters, *rest, *sums)
+    return pl.pallas_call(
+        lambda *refs: clean_body(sizes, half, which, first, count, last, *refs),
         out_shape=[
             jax.ShapeDtypeStruct((count, 2 * CH, LANES), F32),
             jax.ShapeDtypeStruct((CH, LANES), F32),
         ],
-        in_specs=[pl.BlockSpec(memory_space=VMEM)] * 5,
+        in_specs=[pl.BlockSpec(memory_space=VMEM)] * len(args),
         out_specs=[pl.BlockSpec(memory_space=VMEM)] * 2,
         compiler_params=params(),
         cost_estimate=cost(count, 300000),
         name="clean",
-    )(filters, *rest)
-
-
-def finish_body(sizes, half, which, first, count, places, w_ref, *refs):
-    data, refs = refs[:4], refs[4:]
-    real_ref, imag_ref, num_ref = refs[-3:]
-    done = refs[: len(places)]
-    sums = refs[len(places) : 2 * len(places)]
+    )(*args)
+
+
+def merge_body(sizes, half, places, *refs):
+    real_ref, imag_ref = refs[-2:]
     codes = half_codes(sizes, half)
-
-    def step(p, num):
-        block = block_of(codes, which, first + p)
-        real, imag, part = clean_block(block, filter_tiles(w_ref, p), *data)
-        at = lanes_of(block)
-        real_ref[:, at] = real
-        imag_ref[:, at] = imag
-        return num + part
-
-    num = lax.fori_loop(0, count, step, jnp.zeros((CH, LANES), F32))
-    for (from_which, from_first), done_ref, sum_ref in zip(places, done, sums):
-        num = num + sum_ref[...]
+    for (which, first), done_ref in zip(places, refs):
         for p in range(done_ref.shape[0]):
-            at = lanes_of(block_of(codes, from_which, from_first + p))
+            at = lanes_of(block_of(codes, which, first + p))
             real_ref[:, at] = done_ref[p, 0:CH, :]
             imag_ref[:, at] = done_ref[p, CH : 2 * CH, :]
-    weight = data[3][...]
-    square = jnp.sum(weight * weight)
-    lane = lax.broadcasted_iota(jnp.int32, (CH, LANES), 1)
-    total = jnp.broadcast_to(jnp.sum(num, axis=1, keepdims=True), (CH, LANES))
-    num_ref[...] = jnp.where(lane == 0, total, square)
-
-
-def finish(sizes, half, filters, rest, which, first, places, pieces, sums):
-    count = filters.shape[0]
-    mr = rest[0]
-    args = (filters, *rest, *pieces, *sums)
-    return pl.pallas_call(
-        lambda *refs: finish_body(sizes, half, which, first, count, places, *refs),
-        out_shape=[jax.ShapeDtypeStruct((mr.shape[0], mr.shape[2]), F32)] * 2
-        + [jax.ShapeDtypeStruct((CH, LANES), F32)],
-        in_specs=[pl.BlockSpec(memory_space=VMEM)] * len(args),
-        out_specs=[pl.BlockSpec(memory_space=VMEM)] * 3,
-        compiler_params=params(),
-        cost_estimate=cost(count, 400000),
-        name="finish",
-    )(*args)
+
+
+def merge(sizes, half, places, pieces, bins):
+    return pl.pallas_call(
+        lambda *refs: merge_body(sizes, half, places, *refs),
+        out_shape=[jax.ShapeDtypeStruct((CH, bins), F32)] * 2,
+        in_specs=[pl.BlockSpec(memory_space=VMEM)] * len(pieces),
+        out_specs=[pl.BlockSpec(memory_space=VMEM)] * 2,
+        compiler_params=params(),
+        cost_estimate=cost(len(pieces), 300000),
+        name="merge",
+    )(*pieces)
 
 
 def summed_over_bin(value, sizes):
@@ -409,7 +419,10 @@
         own = spectra(sizes, half, keep, data, 0, first, count)
         received.extend([(first, first + count, own), (first, first + count, away)])
 
-    def summed(lo, hi):
+    def summed(lo, hi, alone=False):
+        if alone:
+            parts = [(a, lo - f) for f, t, a in received if f <= lo and hi <= t]
+            return added(*zip(*parts), hi - lo)
         parts = [a[lo - f : hi - f] for f, t, a in received if f <= lo and hi <= t]
         total = parts[0]
         for part in parts[1:]:
@@ -430,8 +443,11 @@
     local(0, q)
     h = jnp.stack([data[2], data[3]]).astype(F32)
     h = h.transpose(2, 0, 1, 3).reshape(2 * DET, CH, bins)
-    halve(2, e, 2 * e, 0)
-    halve(3, e // 2, e, 0)
+    direct = []
+    for n, steps in ((2, (2,)), (3, (2, 3)), (1, (3,))):
+        send = summed(n * SUB, (n + 1) * SUB, alone=n == 1)
+        direct.append((0, SUB, swap_steps(send, steps, sizes)))
+    received.extend(direct)
     last = summed(0, SUB)
     got = swap_steps(last, (4,), sizes)
     filters = solve(last, got)
@@ -442,22 +458,18 @@
         near.append(swap_steps(filters, steps, sizes))
     near = jnp.concatenate(near, axis=0)
     quarters = [near]
-    quarters.append(swap_steps(near, (1,), sizes))
-    quarters.append(swap_steps(near, (0,), sizes))
-    quarters.append(swap_steps(quarters[1], (0,), sizes))
+    for steps in ((1,), (0,), (0, 1)):
+        quarters.append(swap_steps(near, steps, sizes))
     pieces, sums, places = [], [], []
     for n, mine in enumerate(quarters):
         other = swap_core(mine)
         for which, filt in enumerate((mine, other)):
-            if (n, which) == (3, 1):
-                real, imag, num = finish(
-                    sizes, half, filt, rest, which, n * q, places, pieces, sums
-                )
-            else:
-                piece, num = clean(sizes, half, filt, rest, which, n * q)
-                pieces.append(piece)
-                sums.append(num)
-                places.append((which, n * q))
+            final = (n, which) == (3, 1)
+            piece, num = clean(sizes, half, filt, rest, which, n * q, sums if final else ())
+            pieces.append(piece)
+            sums.append(num)
+            places.append((which, n * q))
+    real, imag = merge(sizes, half, places, pieces, bins)
     totals = summed_over_bin(num, sizes)
     estimate = totals[:, 0] / jnp.sqrt(totals[:, 1])
     return (real, imag, estimate)

time: 78 us -> 73.2 us (0.938); the launches traced: 76.5 us -> 73.1 us
  starting transfers between devices: 34.6 us -> 30.8 us
    ppermute x13 -> x14, starting transfers between devices: 28.9 us -> 25.3 us  [swap_steps(): return lax.ppermute(value, SEG, pairs)]
    ppermute x13 -> x14, waiting for transfers between devices: 23.1 us -> 24.2 us  [swap_steps(): return lax.ppermute(value, SEG, pairs)]
    ppermute x3, waiting for transfers between devices: 4.39 us -> 3.46 us  [summed_over_bin(): got.append(lax.ppermute(value, 'y', flip_pairs('y', sizes['y'], 0, bits)))]
    pallas_call x7 -> x8, Pallas kernels: 2.7 us -> 3.22 us  [clean(): pl.pallas_call(lambda *refs: clean_body(sizes, half, which, first, count,...]
  transfers between devices with their start and end apart: 24 -> 25, of which waited for: 14 -> 14; matrix products, arithmetic and copies ran while one was open for 2% -> 2% of each run, Pallas kernels for 10% -> 12%
where the time goes in v4:
time: 73.2 us; the launch traced here: 73.1 us
  starting transfers between devices  30.8 us (42%)
  waiting for transfers between devices  27.7 us (38%)
  Pallas kernels  11.4 us (16%)
  other arithmetic  1.61 us (2%)
  between operations  0.85 us (1%)
  local copies, waits for them, and re-layouts  0.75 us (1%)
    ppermute x14, starting transfers between devices, swap_steps(): return lax.ppermute(value, SEG, pairs)  25.3 us
    ppermute x14, waiting for transfers between devices, swap_steps(): return lax.ppermute(value, SEG, pairs)  24.2 us
    pallas_call x7, Pallas kernels, spectra(): pl.pallas_call(lambda *refs: spectra_body(sizes, half, which, first, coun...  4.9 us
    ppermute x3, starting transfers between devices, summed_over_bin(): got.append(lax.ppermute(value, 'y', flip_pairs('y', sizes['y'], 0, bits)))  4.57 us
    ppermute x3, waiting for transfers between devices, summed_over_bin(): got.append(lax.ppermute(value, 'y', flip_pairs('y', sizes['y'], 0, bits)))  3.46 us
    pallas_call x8, Pallas kernels, clean(): pl.pallas_call(lambda *refs: clean_body(sizes, half, which, first, count,...  3.22 us
    pallas_call x1, Pallas kernels, front(): pl.pallas_call(lambda *refs: front_body(sizes, half, first, count, *refs)...  2.11 us
  transfers between devices with their start and end apart: 25, of which 14 were waited for; matrix products, arithmetic and copies ran while one was open for 2% of the time, Pallas kernels for 12%

profile of v4, /device:TPU:2, one launch (start us, length us, event | category | flops | bytes accessed | tf_op | source)
XLA Modules:
  0.0 73.1 jit_solution(2299009727436891859)
XLA Ops:
  0.6 2.1 %front.1 = (f32[8,96,128]{2,1,0:T(8,128)S(1)}, f32[8,8,128]{2,1,0:T(8,128)S(1)}, bf16[8,8,8192]{2,1,0:T(8,128)(2,1)S(1)}, bf16[8,8,8192]{2,1,0:T(8,128)(2,1)S(1)...) custom-call(s32[8]{0:T(128)} %refs_0_.1, bf16[8,8,8192]{2,1,0:T(8,128)(2,1)} %refs_1_.1, ...), custom_call_target="tpu_custom_call" | custom-call | flops 4000000 | tf_op jit(solution)/shard_map/front/pallas_call | solution.py:171
  5.7 2.3 %collective-permute-start.3 = (f32[8,96,128]{2,1,0:T(8,128)S(1)}, f32[8,96,128]{2,1,0:T(8,128)S(1)}, u32[]{:S(2)}, u32[]{:S(2)}) collective-permute-start(f32[8,96,128]{2,1,0:T(8,128)S(1)} %add.64), channel_id=1, source_target_pairs={{0,8},{4,28},{8,0},{12,20},{16,24},{20,12},{24,16},{28,4},{32,40},... | collective-permute-start | bytes 1179656 | tf_op jit(solution)/shard_map/ppermute | solution.py:51
  10.3 1.3 %collective-permute-start.1 = (f32[8,96,128]{2,1,0:T(8,128)S(1)}, f32[8,96,128]{2,1,0:T(8,128)S(1)}, u32[]{:S(2)}, u32[]{:S(2)}) collective-permute-start(f32[8,96,128]{2,1,0:T(8,128)S(1)} %add.63), channel_id=1, source_target_pairs={{0,8},{4,28},{8,0},{12,20},{16,24},{20,12},{24,16},{28,4},{32,40},... | collective-permute-start | bytes 1179656 | tf_op jit(solution)/shard_map/ppermute | solution.py:51
  11.6 2.2 %collective-permute-done.3 = f32[8,96,128]{2,1,0:T(8,128)S(1)} collective-permute-done((f32[8,96,128]{2,1,0:T(8,128)S(1)}, f32[8,96,128]{2,1,0:T(8,128)S(1)}, u32[]{:S(2)}, u32[]{:S(2)}) %collective-permute-start.3) | collective-permute-done | bytes 393248 | tf_op jit(solution)/shard_map/ppermute | solution.py:51
  13.9 1.4 %collective-permute-start.7 = (f32[4,96,128]{2,1,0:T(8,128)S(1)}, f32[4,96,128]{2,1,0:T(8,128)S(1)}, u32[]{:S(2)}, u32[]{:S(2)}) collective-permute-start(f32[4,96,128]{2,1,0:T(8,128)S(1)} %get-tuple-element.53), channel_id=1, source_target_pairs={{0,24},{4,12},{8,16},{12,4},{16,8},{20,28},{24,0},{28,20},{32,56},... | collective-permute-start | bytes 589832 | tf_op jit(solution)/shard_map/ppermute | solution.py:51
  16.8 2.3 %collective-permute-done.1.refs_0_ = f32[8,96,128]{2,1,0:T(8,128)S(1)} collective-permute-done((f32[8,96,128]{2,1,0:T(8,128)S(1)}, f32[8,96,128]{2,1,0:T(8,128)S(1)}, u32[]{:S(2)}, u32[]{:S(2)}) %collective-permute-start.1) | collective-permute-done | bytes 393248 | tf_op jit(solution)/shard_map/ppermute | solution.py:51
  19.8 1.8 %collective-permute-start.8 = (f32[2,96,128]{2,1,0:T(8,128)S(1)}, f32[2,96,128]{2,1,0:T(8,128)S(1)}, u32[]{:S(2)}, u32[]{:S(2)}) collective-permute-start(f32[2,96,128]{2,1,0:T(8,128)S(1)} %get-tuple-element.51), channel_id=1, source_target_pairs={{0,32},{4,36},{8,40},{12,44},{16,48},{20,52},{24,56},{28,60},{32,0... | collective-permute-start | bytes 294920 | tf_op jit(solution)/shard_map/ppermute | solution.py:51
  21.7 2.8 %collective-permute-start.9 = (f32[2,96,128]{2,1,0:T(8,128)S(1)}, f32[2,96,128]{2,1,0:T(8,128)S(1)}, u32[]{:S(2)}, u32[]{:S(2)}) collective-permute-start(f32[2,96,128]{2,1,0:T(8,128)S(1)} %get-tuple-element.52), channel_id=1, source_target_pairs={{0,96},{4,228},{8,104},{12,236},{16,112},{20,244},{24,120},{28,252... | collective-permute-start | bytes 294920 | tf_op jit(solution)/shard_map/ppermute | solution.py:51
  25.2 3.5 %collective-permute-done.9 = f32[2,96,128]{2,1,0:T(8,128)S(1)} collective-permute-done((f32[2,96,128]{2,1,0:T(8,128)S(1)}, f32[2,96,128]{2,1,0:T(8,128)S(1)}, u32[]{:S(2)}, u32[]{:S(2)}) %collective-permute-start.9) | collective-permute-done | bytes 98336 | tf_op jit(solution)/shard_map/ppermute | solution.py:51
  28.8 2.5 %collective-permute-done.10 = f32[2,96,128]{2,1,0:T(8,128)S(1)} collective-permute-done((f32[2,96,128]{2,1,0:T(8,128)S(1)}, f32[2,96,128]{2,1,0:T(8,128)S(1)}, u32[]{:S(2)}, u32[]{:S(2)}) %collective-permute-start.10) | collective-permute-done | bytes 98336 | tf_op jit(solution)/shard_map/ppermute | solution.py:51
  31.3 5.0 %collective-permute-start.11 = (f32[2,96,128]{2,1,0:T(8,128)S(1)}, f32[2,96,128]{2,1,0:T(8,128)S(1)}, u32[]{:S(2)}, u32[]{:S(2)}) collective-permute-start(f32[2,96,128]{2,1,0:T(8,128)S(1)} %fusion.2.a_ref), channel_id=1, source_target_pairs={{0,192},{4,68},{8,200},{12,76},{16,208},{20,84},{24,216},{28,92},{... | collective-permute-start | bytes 294920 | tf_op jit(solution)/shard_map/ppermute | solution.py:51
  36.3 3.6 %collective-permute-done.11.b_ref = f32[2,96,128]{2,1,0:T(8,128)S(1)} collective-permute-done((f32[2,96,128]{2,1,0:T(8,128)S(1)}, f32[2,96,128]{2,1,0:T(8,128)S(1)}, u32[]{:S(2)}, u32[]{:S(2)}) %collective-permute-start.11) | collective-permute-done | bytes 98336 | tf_op jit(solution)/shard_map/ppermute | solution.py:51
  40.2 1.7 %collective-permute-start.13 = (f32[2,32,128]{2,1,0:T(8,128)S(1)}, f32[2,32,128]{2,1,0:T(8,128)S(1)}, u32[]{:S(2)}, u32[]{:S(2)}) collective-permute-start(f32[2,32,128]{2,1,0:T(8,128)S(1)} %solve.1), channel_id=1, source_target_pairs={{0,32},{4,36},{8,40},{12,44},{16,48},{20,52},{24,56},{28,60},{32,0... | collective-permute-start | bytes 98312 | tf_op jit(solution)/shard_map/ppermute | solution.py:51
  41.9 2.7 %collective-permute-start.14 = (f32[2,32,128]{2,1,0:T(8,128)S(1)}, f32[2,32,128]{2,1,0:T(8,128)S(1)}, u32[]{:S(2)}, u32[]{:S(2)}) collective-permute-start(f32[2,32,128]{2,1,0:T(8,128)S(1)} %solve.1), channel_id=1, source_target_pairs={{0,96},{4,228},{8,104},{12,236},{16,112},{20,244},{24,120},{28,252... | collective-permute-start | bytes 98312 | tf_op jit(solution)/shard_map/ppermute | solution.py:51
  45.0 2.6 %collective-permute-done.14 = f32[2,32,128]{2,1,0:T(8,128)S(1)} collective-permute-done((f32[2,32,128]{2,1,0:T(8,128)S(1)}, f32[2,32,128]{2,1,0:T(8,128)S(1)}, u32[]{:S(2)}, u32[]{:S(2)}) %collective-permute-start.14) | collective-permute-done | bytes 32800 | tf_op jit(solution)/shard_map/ppermute | solution.py:51
  47.7 2.7 %collective-permute-start.18 = (f32[8,32,128]{2,1,0:T(8,128)S(1)}, f32[8,32,128]{2,1,0:T(8,128)S(1)}, u32[]{:S(2)}, u32[]{:S(2)}) collective-permute-start(f32[8,32,128]{2,1,0:T(8,128)S(1)} %pad_maximum_fusion.refs_0_), channel_id=1, source_target_pairs={{0,8},{4,28},{8,0},{12,20},{16,24},{20,12},{24,16},{28,4},{32,40},... | collective-permute-start | bytes 393224 | tf_op jit(solution)/shard_map/ppermute | solution.py:51
  50.4 1.8 %collective-permute-start.16 = (f32[8,32,128]{2,1,0:T(8,128)S(1)}, f32[8,32,128]{2,1,0:T(8,128)S(1)}, u32[]{:S(2)}, u32[]{:S(2)}) collective-permute-start(f32[8,32,128]{2,1,0:T(8,128)S(1)} %pad_maximum_fusion.refs_0_), channel_id=1, source_target_pairs={{0,24},{4,12},{8,16},{12,4},{16,8},{20,28},{24,0},{28,20},{32,56},... | collective-permute-start | bytes 393224 | tf_op jit(solution)/shard_map/ppermute | solution.py:51
  52.6 2.1 %collective-permute-done.18.refs_0_ = f32[8,32,128]{2,1,0:T(8,128)S(1)} collective-permute-done((f32[8,32,128]{2,1,0:T(8,128)S(1)}, f32[8,32,128]{2,1,0:T(8,128)S(1)}, u32[]{:S(2)}, u32[]{:S(2)}) %collective-permute-start.18) | collective-permute-done | bytes 131104 | tf_op jit(solution)/shard_map/ppermute | solution.py:51
  54.7 1.4 %collective-permute-done.16.refs_0_ = f32[8,32,128]{2,1,0:T(8,128)S(1)} collective-permute-done((f32[8,32,128]{2,1,0:T(8,128)S(1)}, f32[8,32,128]{2,1,0:T(8,128)S(1)}, u32[]{:S(2)}, u32[]{:S(2)}) %collective-permute-start.16) | collective-permute-done | bytes 131104 | tf_op jit(solution)/shard_map/ppermute | solution.py:51
  56.1 2.6 %collective-permute-done.20.refs_0_ = f32[8,32,128]{2,1,0:T(8,128)S(1)} collective-permute-done((f32[8,32,128]{2,1,0:T(8,128)S(1)}, f32[8,32,128]{2,1,0:T(8,128)S(1)}, u32[]{:S(2)}, u32[]{:S(2)}) %collective-permute-start.20) | collective-permute-done | bytes 131104 | tf_op jit(solution)/shard_map/ppermute | solution.py:51
  63.4 1.7 %collective-permute-start.22 = (f32[8,128]{1,0:T(8,128)S(1)}, f32[8,128]{1,0:T(8,128)S(1)}, u32[]{:S(2)}, u32[]{:S(2)}) collective-permute-start(f32[8,128]{1,0:T(8,128)S(1)} %get-tuple-element.50), channel_id=1, source_target_pairs={{0,1},{1,0},{2,3},{3,2},{4,5},{5,4},{6,7},{7,6},{8,9},{9,8},{10,11... | collective-permute-start | bytes 12296 | tf_op jit(solution)/shard_map/ppermute | solution.py:399
  65.1 2.2 %collective-permute-start.23 = (f32[8,128]{1,0:T(8,128)S(1)}, f32[8,128]{1,0:T(8,128)S(1)}, u32[]{:S(2)}, u32[]{:S(2)}) collective-permute-start(f32[8,128]{1,0:T(8,128)S(1)} %get-tuple-element.50), channel_id=1, source_target_pairs={{0,3},{1,2},{2,1},{3,0},{4,7},{5,6},{6,5},{7,4},{8,11},{9,10},{10,... | collective-permute-start | bytes 12296 | tf_op jit(solution)/shard_map/ppermute | solution.py:399
  68.9 1.0 %collective-permute-done.23 = f32[8,128]{1,0:T(8,128)S(1)} collective-permute-done((f32[8,128]{1,0:T(8,128)S(1)}, f32[8,128]{1,0:T(8,128)S(1)}, u32[]{:S(2)}, u32[]{:S(2)}) %collective-permute-start.23) | collective-permute-done | bytes 4128 | tf_op jit(solution)/shard_map/ppermute | solution.py:399
  69.9 2.5 %collective-permute-done.24 = f32[8,128]{1,0:T(8,128)S(1)} collective-permute-done((f32[8,128]{1,0:T(8,128)S(1)}, f32[8,128]{1,0:T(8,128)S(1)}, u32[]{:S(2)}, u32[]{:S(2)}) %collective-permute-start.24) | collective-permute-done | bytes 4128 | tf_op jit(solution)/shard_map/ppermute | solution.py:399
  (57 shorter events, 16.4 us)
Async XLA Ops:
  3.6 8.0 %collective-permute-start.4 = (f32[8,96,128]{2,1,0:T(8,128)S(1)}, f32[8,96,128]{2,1,0:T(8,128)S(1)}, u32[]{:S(2)}, u32[]{:S(2)}) collective-permute-start(f32[8,96,128]{2,1,0:T(8,128)S(1)} %spectra.11), channel_id=1, source_target_pairs={{0,4},{4,0},{1,5},{5,1},{2,6},{6,2},{3,7},{7,3},{8,12},{12,8},{9,1... | collective-permute-start | bytes 1179656 | tf_op jit(solution)/shard_map/ppermute | solution.py:55
  4.8 5.5 %collective-permute-start = (f32[8,96,128]{2,1,0:T(8,128)S(1)}, f32[8,96,128]{2,1,0:T(8,128)S(1)}, u32[]{:S(2)}, u32[]{:S(2)}) collective-permute-start(f32[8,96,128]{2,1,0:T(8,128)S(1)} %spectra.8), channel_id=1, source_target_pairs={{0,4},{4,0},{1,5},{5,1},{2,6},{6,2},{3,7},{7,3},{8,12},{12,8},{9,1... | collective-permute-start | bytes 1179656 | tf_op jit(solution)/shard_map/ppermute | solution.py:55
  5.7 8.1 %collective-permute-start.3 = (f32[8,96,128]{2,1,0:T(8,128)S(1)}, f32[8,96,128]{2,1,0:T(8,128)S(1)}, u32[]{:S(2)}, u32[]{:S(2)}) collective-permute-start(f32[8,96,128]{2,1,0:T(8,128)S(1)} %add.64), channel_id=1, source_target_pairs={{0,8},{4,28},{8,0},{12,20},{16,24},{20,12},{24,16},{28,4},{32,40},... | collective-permute-start | bytes 1179656 | tf_op jit(solution)/shard_map/ppermute | solution.py:51
  8.7 8.0 %collective-permute-start.6 = (f32[8,96,128]{2,1,0:T(8,128)S(1)}, f32[8,96,128]{2,1,0:T(8,128)S(1)}, u32[]{:S(2)}, u32[]{:S(2)}) collective-permute-start(f32[8,96,128]{2,1,0:T(8,128)S(1)} %spectra.13), channel_id=1, source_target_pairs={{0,4},{4,0},{1,5},{5,1},{2,6},{6,2},{3,7},{7,3},{8,12},{12,8},{9,1... | collective-permute-start | bytes 1179656 | tf_op jit(solution)/shard_map/ppermute | solution.py:55
  10.3 8.7 %collective-permute-start.1 = (f32[8,96,128]{2,1,0:T(8,128)S(1)}, f32[8,96,128]{2,1,0:T(8,128)S(1)}, u32[]{:S(2)}, u32[]{:S(2)}) collective-permute-start(f32[8,96,128]{2,1,0:T(8,128)S(1)} %add.63), channel_id=1, source_target_pairs={{0,8},{4,28},{8,0},{12,20},{16,24},{20,12},{24,16},{28,4},{32,40},... | collective-permute-start | bytes 1179656 | tf_op jit(solution)/shard_map/ppermute | solution.py:51
  13.9 5.9 %collective-permute-start.7 = (f32[4,96,128]{2,1,0:T(8,128)S(1)}, f32[4,96,128]{2,1,0:T(8,128)S(1)}, u32[]{:S(2)}, u32[]{:S(2)}) collective-permute-start(f32[4,96,128]{2,1,0:T(8,128)S(1)} %get-tuple-element.53), channel_id=1, source_target_pairs={{0,24},{4,12},{8,16},{12,4},{16,8},{20,28},{24,0},{28,20},{32,56},... | collective-permute-start | bytes 589832 | tf_op jit(solution)/shard_map/ppermute | solution.py:51
  15.9 8.6 %collective-permute-start.5 = (f32[4,96,128]{2,1,0:T(8,128)S(1)}, f32[4,96,128]{2,1,0:T(8,128)S(1)}, u32[]{:S(2)}, u32[]{:S(2)}) collective-permute-start(f32[4,96,128]{2,1,0:T(8,128)S(1)} %get-tuple-element.54), channel_id=1, source_target_pairs={{0,24},{4,12},{8,16},{12,4},{16,8},{20,28},{24,0},{28,20},{32,56},... | collective-permute-start | bytes 589832 | tf_op jit(solution)/shard_map/ppermute | solution.py:51
  19.8 5.4 %collective-permute-start.8 = (f32[2,96,128]{2,1,0:T(8,128)S(1)}, f32[2,96,128]{2,1,0:T(8,128)S(1)}, u32[]{:S(2)}, u32[]{:S(2)}) collective-permute-start(f32[2,96,128]{2,1,0:T(8,128)S(1)} %get-tuple-element.51), channel_id=1, source_target_pairs={{0,32},{4,36},{8,40},{12,44},{16,48},{20,52},{24,56},{28,60},{32,0... | collective-permute-start | bytes 294920 | tf_op jit(solution)/shard_map/ppermute | solution.py:51
  21.7 7.1 %collective-permute-start.9 = (f32[2,96,128]{2,1,0:T(8,128)S(1)}, f32[2,96,128]{2,1,0:T(8,128)S(1)}, u32[]{:S(2)}, u32[]{:S(2)}) collective-permute-start(f32[2,96,128]{2,1,0:T(8,128)S(1)} %get-tuple-element.52), channel_id=1, source_target_pairs={{0,96},{4,228},{8,104},{12,236},{16,112},{20,244},{24,120},{28,252... | collective-permute-start | bytes 294920 | tf_op jit(solution)/shard_map/ppermute | solution.py:51
  24.5 6.8 %collective-permute-start.10 = (f32[2,96,128]{2,1,0:T(8,128)S(1)}, f32[2,96,128]{2,1,0:T(8,128)S(1)}, u32[]{:S(2)}, u32[]{:S(2)}) collective-permute-start(f32[2,96,128]{2,1,0:T(8,128)S(1)} %added.1), channel_id=1, source_target_pairs={{0,64},{4,196},{8,72},{12,204},{16,80},{20,212},{24,88},{28,220},{... | collective-permute-start | bytes 294920 | tf_op jit(solution)/shard_map/ppermute | solution.py:51
  31.3 8.6 %collective-permute-start.11 = (f32[2,96,128]{2,1,0:T(8,128)S(1)}, f32[2,96,128]{2,1,0:T(8,128)S(1)}, u32[]{:S(2)}, u32[]{:S(2)}) collective-permute-start(f32[2,96,128]{2,1,0:T(8,128)S(1)} %fusion.2.a_ref), channel_id=1, source_target_pairs={{0,192},{4,68},{8,200},{12,76},{16,208},{20,84},{24,216},{28,92},{... | collective-permute-start | bytes 294920 | tf_op jit(solution)/shard_map/ppermute | solution.py:51
  40.1 4.9 %collective-permute-start.12 = (f32[2,32,128]{2,1,0:T(8,128)S(1)}, f32[2,32,128]{2,1,0:T(8,128)S(1)}, u32[]{:S(2)}, u32[]{:S(2)}) collective-permute-start(f32[2,32,128]{2,1,0:T(8,128)S(1)} %solve.1), channel_id=1, source_target_pairs={{0,64},{4,196},{8,72},{12,204},{16,80},{20,212},{24,88},{28,220},{... | collective-permute-start | bytes 98312 | tf_op jit(solution)/shard_map/ppermute | solution.py:51
  40.2 4.8 %collective-permute-start.13 = (f32[2,32,128]{2,1,0:T(8,128)S(1)}, f32[2,32,128]{2,1,0:T(8,128)S(1)}, u32[]{:S(2)}, u32[]{:S(2)}) collective-permute-start(f32[2,32,128]{2,1,0:T(8,128)S(1)} %solve.1), channel_id=1, source_target_pairs={{0,32},{4,36},{8,40},{12,44},{16,48},{20,52},{24,56},{28,60},{32,0... | collective-permute-start | bytes 98312 | tf_op jit(solution)/shard_map/ppermute | solution.py:51
  41.9 5.7 %collective-permute-start.14 = (f32[2,32,128]{2,1,0:T(8,128)S(1)}, f32[2,32,128]{2,1,0:T(8,128)S(1)}, u32[]{:S(2)}, u32[]{:S(2)}) collective-permute-start(f32[2,32,128]{2,1,0:T(8,128)S(1)} %solve.1), channel_id=1, source_target_pairs={{0,96},{4,228},{8,104},{12,236},{16,112},{20,244},{24,120},{28,252... | collective-permute-start | bytes 98312 | tf_op jit(solution)/shard_map/ppermute | solution.py:51
  47.7 7.0 %collective-permute-start.18 = (f32[8,32,128]{2,1,0:T(8,128)S(1)}, f32[8,32,128]{2,1,0:T(8,128)S(1)}, u32[]{:S(2)}, u32[]{:S(2)}) collective-permute-start(f32[8,32,128]{2,1,0:T(8,128)S(1)} %pad_maximum_fusion.refs_0_), channel_id=1, source_target_pairs={{0,8},{4,28},{8,0},{12,20},{16,24},{20,12},{24,16},{28,4},{32,40},... | collective-permute-start | bytes 393224 | tf_op jit(solution)/shard_map/ppermute | solution.py:51
  50.4 5.7 %collective-permute-start.16 = (f32[8,32,128]{2,1,0:T(8,128)S(1)}, f32[8,32,128]{2,1,0:T(8,128)S(1)}, u32[]{:S(2)}, u32[]{:S(2)}) collective-permute-start(f32[8,32,128]{2,1,0:T(8,128)S(1)} %pad_maximum_fusion.refs_0_), channel_id=1, source_target_pairs={{0,24},{4,12},{8,16},{12,4},{16,8},{20,28},{24,0},{28,20},{32,56},... | collective-permute-start | bytes 393224 | tf_op jit(solution)/shard_map/ppermute | solution.py:51
  52.2 6.5 %collective-permute-start.20 = (f32[8,32,128]{2,1,0:T(8,128)S(1)}, f32[8,32,128]{2,1,0:T(8,128)S(1)}, u32[]{:S(2)}, u32[]{:S(2)}) collective-permute-start(f32[8,32,128]{2,1,0:T(8,128)S(1)} %pad_maximum_fusion.refs_0_), channel_id=1, source_target_pairs={{0,16},{4,20},{8,24},{12,28},{16,0},{20,4},{24,8},{28,12},{32,48},... | collective-permute-start | bytes 393224 | tf_op jit(solution)/shard_map/ppermute | solution.py:51
  52.6 9.1 %collective-permute-start.15 = (f32[8,32,128]{2,1,0:T(8,128)S(1)}, f32[8,32,128]{2,1,0:T(8,128)S(1)}, u32[]{:S(2)}, u32[]{:S(2)}) collective-permute-start(f32[8,32,128]{2,1,0:T(8,128)S(1)} %pad_maximum_fusion.refs_0_), channel_id=1, source_target_pairs={{0,4},{4,0},{1,5},{5,1},{2,6},{6,2},{3,7},{7,3},{8,12},{12,8},{9,1... | collective-permute-start | bytes 393224 | tf_op jit(solution)/shard_map/ppermute | solution.py:55
  54.7 7.4 %collective-permute-start.19 = (f32[8,32,128]{2,1,0:T(8,128)S(1)}, f32[8,32,128]{2,1,0:T(8,128)S(1)}, u32[]{:S(2)}, u32[]{:S(2)}) collective-permute-start(f32[8,32,128]{2,1,0:T(8,128)S(1)} %collective-permute-done.18.refs_0_), channel_id=1, source_target_pairs={{0,4},{4,0},{1,5},{5,1},{2,6},{6,2},{3,7},{7,3},{8,12},{12,8},{9,1... | collective-permute-start | bytes 393224 | tf_op jit(solution)/shard_map/ppermute | solution.py:55
  56.0 6.4 %collective-permute-start.17 = (f32[8,32,128]{2,1,0:T(8,128)S(1)}, f32[8,32,128]{2,1,0:T(8,128)S(1)}, u32[]{:S(2)}, u32[]{:S(2)}) collective-permute-start(f32[8,32,128]{2,1,0:T(8,128)S(1)} %collective-permute-done.16.refs_0_), channel_id=1, source_target_pairs={{0,4},{4,0},{1,5},{5,1},{2,6},{6,2},{3,7},{7,3},{8,12},{12,8},{9,1... | collective-permute-start | bytes 393224 | tf_op jit(solution)/shard_map/ppermute | solution.py:55
  58.7 4.2 %collective-permute-start.21 = (f32[8,32,128]{2,1,0:T(8,128)S(1)}, f32[8,32,128]{2,1,0:T(8,128)S(1)}, u32[]{:S(2)}, u32[]{:S(2)}) collective-permute-start(f32[8,32,128]{2,1,0:T(8,128)S(1)} %collective-permute-done.20.refs_0_), channel_id=1, source_target_pairs={{0,4},{4,0},{1,5},{5,1},{2,6},{6,2},{3,7},{7,3},{8,12},{12,8},{9,1... | collective-permute-start | bytes 393224 | tf_op jit(solution)/shard_map/ppermute | solution.py:55
  63.4 5.5 %collective-permute-start.22 = (f32[8,128]{1,0:T(8,128)S(1)}, f32[8,128]{1,0:T(8,128)S(1)}, u32[]{:S(2)}, u32[]{:S(2)}) collective-permute-start(f32[8,128]{1,0:T(8,128)S(1)} %get-tuple-element.50), channel_id=1, source_target_pairs={{0,1},{1,0},{2,3},{3,2},{4,5},{5,4},{6,7},{7,6},{8,9},{9,8},{10,11... | collective-permute-start | bytes 12296 | tf_op jit(solution)/shard_map/ppermute | solution.py:399
  65.1 4.8 %collective-permute-start.23 = (f32[8,128]{1,0:T(8,128)S(1)}, f32[8,128]{1,0:T(8,128)S(1)}, u32[]{:S(2)}, u32[]{:S(2)}) collective-permute-start(f32[8,128]{1,0:T(8,128)S(1)} %get-tuple-element.50), channel_id=1, source_target_pairs={{0,3},{1,2},{2,1},{3,0},{4,7},{5,6},{6,5},{7,4},{8,11},{9,10},{10,... | collective-permute-start | bytes 12296 | tf_op jit(solution)/shard_map/ppermute | solution.py:399
  67.2 5.1 %collective-permute-start.24 = (f32[8,128]{1,0:T(8,128)S(1)}, f32[8,128]{1,0:T(8,128)S(1)}, u32[]{:S(2)}, u32[]{:S(2)}) collective-permute-start(f32[8,128]{1,0:T(8,128)S(1)} %get-tuple-element.50), channel_id=1, source_target_pairs={{0,2},{1,3},{2,0},{3,1},{4,6},{5,7},{6,4},{7,5},{8,10},{9,11},{10,... | collective-permute-start | bytes 12296 | tf_op jit(solution)/shard_map/ppermute | solution.py:399
  (2 other events, 3.7 us)

commit v5 on v4

--- a/solution.py
+++ b/solution.py
@@ -349,7 +349,8 @@
         square = jnp.sum(weight * weight)
         lane = lax.broadcasted_iota(jnp.int32, (CH, LANES), 1)
         total = jnp.broadcast_to(jnp.sum(num, axis=1, keepdims=True), (CH, LANES))
-        num = jnp.where(lane == 0, total, square)
+        total = jnp.sum(jnp.where(lane == sublane(), total, 0.0), axis=0, keepdims=True)
+        num = jnp.where(sublane() == 0, jnp.broadcast_to(total, (CH, LANES)), square)
     num_ref[...] = num
 
 
@@ -471,7 +472,7 @@
             places.append((which, n * q))
     real, imag = merge(sizes, half, places, pieces, bins)
     totals = summed_over_bin(num, sizes)
-    estimate = totals[:, 0] / jnp.sqrt(totals[:, 1])
+    estimate = (totals[0] / jnp.sqrt(totals[1]))[:CH]
     return (real, imag, estimate)
 
 

time: 73.2 us -> 73.1 us (level)
  no operation moved by 1% of the time
where the time goes in v5:
time: 73.1 us; the launch traced here: 72.9 us
  starting transfers between devices  30.8 us (42%)
  waiting for transfers between devices  27.7 us (38%)
  Pallas kernels  11.4 us (16%)
  local copies, waits for them, and re-layouts  1.27 us (2%)
  other arithmetic  0.92 us (1%)
  between operations  0.85 us (1%)
    ppermute x14, starting transfers between devices, swap_steps(): return lax.ppermute(value, SEG, pairs)  25.3 us
    ppermute x14, waiting for transfers between devices, swap_steps(): return lax.ppermute(value, SEG, pairs)  24.2 us
    pallas_call x7, Pallas kernels, spectra(): pl.pallas_call(lambda *refs: spectra_body(sizes, half, which, first, coun...  4.9 us
    ppermute x3, starting transfers between devices, summed_over_bin(): got.append(lax.ppermute(value, 'y', flip_pairs('y', sizes['y'], 0, bits)))  4.57 us
    ppermute x3, waiting for transfers between devices, summed_over_bin(): got.append(lax.ppermute(value, 'y', flip_pairs('y', sizes['y'], 0, bits)))  3.46 us
    pallas_call x8, Pallas kernels, clean(): pl.pallas_call(lambda *refs: clean_body(sizes, half, which, first, count,...  3.22 us
    pallas_call x1, Pallas kernels, front(): pl.pallas_call(lambda *refs: front_body(sizes, half, first, count, *refs)...  2.11 us
  transfers between devices with their start and end apart: 25, of which 14 were waited for; matrix products, arithmetic and copies ran while one was open for 2% of the time, Pallas kernels for 12%

profile of v5, /device:TPU:2, one launch (start us, length us, event | category | flops | bytes accessed | tf_op | source)
XLA Modules:
  0.0 72.9 jit_solution(6637891758015262199)
XLA Ops:
  0.6 2.1 %front.1 = (f32[8,96,128]{2,1,0:T(8,128)S(1)}, f32[8,8,128]{2,1,0:T(8,128)S(1)}, bf16[8,8,8192]{2,1,0:T(8,128)(2,1)S(1)}, bf16[8,8,8192]{2,1,0:T(8,128)(2,1)S(1)...) custom-call(s32[8]{0:T(128)} %refs_0_.1, bf16[8,8,8192]{2,1,0:T(8,128)(2,1)} %refs_1_.1, ...), custom_call_target="tpu_custom_call" | custom-call | flops 4000000 | tf_op jit(solution)/shard_map/front/pallas_call | solution.py:171
  5.7 2.3 %collective-permute-start.3 = (f32[8,96,128]{2,1,0:T(8,128)S(1)}, f32[8,96,128]{2,1,0:T(8,128)S(1)}, u32[]{:S(2)}, u32[]{:S(2)}) collective-permute-start(f32[8,96,128]{2,1,0:T(8,128)S(1)} %add.64), channel_id=1, source_target_pairs={{0,8},{4,28},{8,0},{12,20},{16,24},{20,12},{24,16},{28,4},{32,40},... | collective-permute-start | bytes 1179656 | tf_op jit(solution)/shard_map/ppermute | solution.py:51
  10.3 1.3 %collective-permute-start.1 = (f32[8,96,128]{2,1,0:T(8,128)S(1)}, f32[8,96,128]{2,1,0:T(8,128)S(1)}, u32[]{:S(2)}, u32[]{:S(2)}) collective-permute-start(f32[8,96,128]{2,1,0:T(8,128)S(1)} %add.63), channel_id=1, source_target_pairs={{0,8},{4,28},{8,0},{12,20},{16,24},{20,12},{24,16},{28,4},{32,40},... | collective-permute-start | bytes 1179656 | tf_op jit(solution)/shard_map/ppermute | solution.py:51
  11.6 2.2 %collective-permute-done.3 = f32[8,96,128]{2,1,0:T(8,128)S(1)} collective-permute-done((f32[8,96,128]{2,1,0:T(8,128)S(1)}, f32[8,96,128]{2,1,0:T(8,128)S(1)}, u32[]{:S(2)}, u32[]{:S(2)}) %collective-permute-start.3) | collective-permute-done | bytes 393248 | tf_op jit(solution)/shard_map/ppermute | solution.py:51
  13.9 1.4 %collective-permute-start.7 = (f32[4,96,128]{2,1,0:T(8,128)S(1)}, f32[4,96,128]{2,1,0:T(8,128)S(1)}, u32[]{:S(2)}, u32[]{:S(2)}) collective-permute-start(f32[4,96,128]{2,1,0:T(8,128)S(1)} %get-tuple-element.53), channel_id=1, source_target_pairs={{0,24},{4,12},{8,16},{12,4},{16,8},{20,28},{24,0},{28,20},{32,56},... | collective-permute-start | bytes 589832 | tf_op jit(solution)/shard_map/ppermute | solution.py:51
  16.8 2.3 %collective-permute-done.1.refs_0_ = f32[8,96,128]{2,1,0:T(8,128)S(1)} collective-permute-done((f32[8,96,128]{2,1,0:T(8,128)S(1)}, f32[8,96,128]{2,1,0:T(8,128)S(1)}, u32[]{:S(2)}, u32[]{:S(2)}) %collective-permute-start.1) | collective-permute-done | bytes 393248 | tf_op jit(solution)/shard_map/ppermute | solution.py:51
  19.8 1.8 %collective-permute-start.8 = (f32[2,96,128]{2,1,0:T(8,128)S(1)}, f32[2,96,128]{2,1,0:T(8,128)S(1)}, u32[]{:S(2)}, u32[]{:S(2)}) collective-permute-start(f32[2,96,128]{2,1,0:T(8,128)S(1)} %get-tuple-element.51), channel_id=1, source_target_pairs={{0,32},{4,36},{8,40},{12,44},{16,48},{20,52},{24,56},{28,60},{32,0... | collective-permute-start | bytes 294920 | tf_op jit(solution)/shard_map/ppermute | solution.py:51
  21.7 2.8 %collective-permute-start.9 = (f32[2,96,128]{2,1,0:T(8,128)S(1)}, f32[2,96,128]{2,1,0:T(8,128)S(1)}, u32[]{:S(2)}, u32[]{:S(2)}) collective-permute-start(f32[2,96,128]{2,1,0:T(8,128)S(1)} %get-tuple-element.52), channel_id=1, source_target_pairs={{0,96},{4,228},{8,104},{12,236},{16,112},{20,244},{24,120},{28,252... | collective-permute-start | bytes 294920 | tf_op jit(solution)/shard_map/ppermute | solution.py:51
  25.2 3.5 %collective-permute-done.9 = f32[2,96,128]{2,1,0:T(8,128)S(1)} collective-permute-done((f32[2,96,128]{2,1,0:T(8,128)S(1)}, f32[2,96,128]{2,1,0:T(8,128)S(1)}, u32[]{:S(2)}, u32[]{:S(2)}) %collective-permute-start.9) | collective-permute-done | bytes 98336 | tf_op jit(solution)/shard_map/ppermute | solution.py:51
  28.8 2.5 %collective-permute-done.10 = f32[2,96,128]{2,1,0:T(8,128)S(1)} collective-permute-done((f32[2,96,128]{2,1,0:T(8,128)S(1)}, f32[2,96,128]{2,1,0:T(8,128)S(1)}, u32[]{:S(2)}, u32[]{:S(2)}) %collective-permute-start.10) | collective-permute-done | bytes 98336 | tf_op jit(solution)/shard_map/ppermute | solution.py:51
  31.3 5.0 %collective-permute-start.11 = (f32[2,96,128]{2,1,0:T(8,128)S(1)}, f32[2,96,128]{2,1,0:T(8,128)S(1)}, u32[]{:S(2)}, u32[]{:S(2)}) collective-permute-start(f32[2,96,128]{2,1,0:T(8,128)S(1)} %fusion.2.a_ref), channel_id=1, source_target_pairs={{0,192},{4,68},{8,200},{12,76},{16,208},{20,84},{24,216},{28,92},{... | collective-permute-start | bytes 294920 | tf_op jit(solution)/shard_map/ppermute | solution.py:51
  36.3 3.6 %collective-permute-done.11.b_ref = f32[2,96,128]{2,1,0:T(8,128)S(1)} collective-permute-done((f32[2,96,128]{2,1,0:T(8,128)S(1)}, f32[2,96,128]{2,1,0:T(8,128)S(1)}, u32[]{:S(2)}, u32[]{:S(2)}) %collective-permute-start.11) | collective-permute-done | bytes 98336 | tf_op jit(solution)/shard_map/ppermute | solution.py:51
  40.2 1.7 %collective-permute-start.13 = (f32[2,32,128]{2,1,0:T(8,128)S(1)}, f32[2,32,128]{2,1,0:T(8,128)S(1)}, u32[]{:S(2)}, u32[]{:S(2)}) collective-permute-start(f32[2,32,128]{2,1,0:T(8,128)S(1)} %solve.1), channel_id=1, source_target_pairs={{0,32},{4,36},{8,40},{12,44},{16,48},{20,52},{24,56},{28,60},{32,0... | collective-permute-start | bytes 98312 | tf_op jit(solution)/shard_map/ppermute | solution.py:51
  41.9 2.7 %collective-permute-start.14 = (f32[2,32,128]{2,1,0:T(8,128)S(1)}, f32[2,32,128]{2,1,0:T(8,128)S(1)}, u32[]{:S(2)}, u32[]{:S(2)}) collective-permute-start(f32[2,32,128]{2,1,0:T(8,128)S(1)} %solve.1), channel_id=1, source_target_pairs={{0,96},{4,228},{8,104},{12,236},{16,112},{20,244},{24,120},{28,252... | collective-permute-start | bytes 98312 | tf_op jit(solution)/shard_map/ppermute | solution.py:51
  45.0 2.6 %collective-permute-done.14 = f32[2,32,128]{2,1,0:T(8,128)S(1)} collective-permute-done((f32[2,32,128]{2,1,0:T(8,128)S(1)}, f32[2,32,128]{2,1,0:T(8,128)S(1)}, u32[]{:S(2)}, u32[]{:S(2)}) %collective-permute-start.14) | collective-permute-done | bytes 32800 | tf_op jit(solution)/shard_map/ppermute | solution.py:51
  47.7 2.7 %collective-permute-start.18 = (f32[8,32,128]{2,1,0:T(8,128)S(1)}, f32[8,32,128]{2,1,0:T(8,128)S(1)}, u32[]{:S(2)}, u32[]{:S(2)}) collective-permute-start(f32[8,32,128]{2,1,0:T(8,128)S(1)} %pad_maximum_fusion.refs_0_), channel_id=1, source_target_pairs={{0,8},{4,28},{8,0},{12,20},{16,24},{20,12},{24,16},{28,4},{32,40},... | collective-permute-start | bytes 393224 | tf_op jit(solution)/shard_map/ppermute | solution.py:51
  50.4 1.8 %collective-permute-start.16 = (f32[8,32,128]{2,1,0:T(8,128)S(1)}, f32[8,32,128]{2,1,0:T(8,128)S(1)}, u32[]{:S(2)}, u32[]{:S(2)}) collective-permute-start(f32[8,32,128]{2,1,0:T(8,128)S(1)} %pad_maximum_fusion.refs_0_), channel_id=1, source_target_pairs={{0,24},{4,12},{8,16},{12,4},{16,8},{20,28},{24,0},{28,20},{32,56},... | collective-permute-start | bytes 393224 | tf_op jit(solution)/shard_map/ppermute | solution.py:51
  52.6 2.1 %collective-permute-done.18.refs_0_ = f32[8,32,128]{2,1,0:T(8,128)S(1)} collective-permute-done((f32[8,32,128]{2,1,0:T(8,128)S(1)}, f32[8,32,128]{2,1,0:T(8,128)S(1)}, u32[]{:S(2)}, u32[]{:S(2)}) %collective-permute-start.18) | collective-permute-done | bytes 131104 | tf_op jit(solution)/shard_map/ppermute | solution.py:51
  54.7 1.4 %collective-permute-done.16.refs_0_ = f32[8,32,128]{2,1,0:T(8,128)S(1)} collective-permute-done((f32[8,32,128]{2,1,0:T(8,128)S(1)}, f32[8,32,128]{2,1,0:T(8,128)S(1)}, u32[]{:S(2)}, u32[]{:S(2)}) %collective-permute-start.16) | collective-permute-done | bytes 131104 | tf_op jit(solution)/shard_map/ppermute | solution.py:51
  56.1 2.6 %collective-permute-done.20.refs_0_ = f32[8,32,128]{2,1,0:T(8,128)S(1)} collective-permute-done((f32[8,32,128]{2,1,0:T(8,128)S(1)}, f32[8,32,128]{2,1,0:T(8,128)S(1)}, u32[]{:S(2)}, u32[]{:S(2)}) %collective-permute-start.20) | collective-permute-done | bytes 131104 | tf_op jit(solution)/shard_map/ppermute | solution.py:51
  63.4 1.7 %collective-permute-start.22 = (f32[8,128]{1,0:T(8,128)S(1)}, f32[8,128]{1,0:T(8,128)S(1)}, u32[]{:S(2)}, u32[]{:S(2)}) collective-permute-start(f32[8,128]{1,0:T(8,128)S(1)} %get-tuple-element.50), channel_id=1, source_target_pairs={{0,1},{1,0},{2,3},{3,2},{4,5},{5,4},{6,7},{7,6},{8,9},{9,8},{10,11... | collective-permute-start | bytes 12296 | tf_op jit(solution)/shard_map/ppermute | solution.py:400
  65.1 2.2 %collective-permute-start.23 = (f32[8,128]{1,0:T(8,128)S(1)}, f32[8,128]{1,0:T(8,128)S(1)}, u32[]{:S(2)}, u32[]{:S(2)}) collective-permute-start(f32[8,128]{1,0:T(8,128)S(1)} %get-tuple-element.50), channel_id=1, source_target_pairs={{0,3},{1,2},{2,1},{3,0},{4,7},{5,6},{6,5},{7,4},{8,11},{9,10},{10,... | collective-permute-start | bytes 12296 | tf_op jit(solution)/shard_map/ppermute | solution.py:400
  68.9 1.0 %collective-permute-done.23 = f32[8,128]{1,0:T(8,128)S(1)} collective-permute-done((f32[8,128]{1,0:T(8,128)S(1)}, f32[8,128]{1,0:T(8,128)S(1)}, u32[]{:S(2)}, u32[]{:S(2)}) %collective-permute-start.23) | collective-permute-done | bytes 4128 | tf_op jit(solution)/shard_map/ppermute | solution.py:400
  69.9 2.5 %collective-permute-done.24 = f32[8,128]{1,0:T(8,128)S(1)} collective-permute-done((f32[8,128]{1,0:T(8,128)S(1)}, f32[8,128]{1,0:T(8,128)S(1)}, u32[]{:S(2)}, u32[]{:S(2)}) %collective-permute-start.24) | collective-permute-done | bytes 4128 | tf_op jit(solution)/shard_map/ppermute | solution.py:400
  (58 shorter events, 16.2 us)
Async XLA Ops:
  3.6 8.0 %collective-permute-start.4 = (f32[8,96,128]{2,1,0:T(8,128)S(1)}, f32[8,96,128]{2,1,0:T(8,128)S(1)}, u32[]{:S(2)}, u32[]{:S(2)}) collective-permute-start(f32[8,96,128]{2,1,0:T(8,128)S(1)} %spectra.11), channel_id=1, source_target_pairs={{0,4},{4,0},{1,5},{5,1},{2,6},{6,2},{3,7},{7,3},{8,12},{12,8},{9,1... | collective-permute-start | bytes 1179656 | tf_op jit(solution)/shard_map/ppermute | solution.py:55
  4.8 5.5 %collective-permute-start = (f32[8,96,128]{2,1,0:T(8,128)S(1)}, f32[8,96,128]{2,1,0:T(8,128)S(1)}, u32[]{:S(2)}, u32[]{:S(2)}) collective-permute-start(f32[8,96,128]{2,1,0:T(8,128)S(1)} %spectra.8), channel_id=1, source_target_pairs={{0,4},{4,0},{1,5},{5,1},{2,6},{6,2},{3,7},{7,3},{8,12},{12,8},{9,1... | collective-permute-start | bytes 1179656 | tf_op jit(solution)/shard_map/ppermute | solution.py:55
  5.7 8.1 %collective-permute-start.3 = (f32[8,96,128]{2,1,0:T(8,128)S(1)}, f32[8,96,128]{2,1,0:T(8,128)S(1)}, u32[]{:S(2)}, u32[]{:S(2)}) collective-permute-start(f32[8,96,128]{2,1,0:T(8,128)S(1)} %add.64), channel_id=1, source_target_pairs={{0,8},{4,28},{8,0},{12,20},{16,24},{20,12},{24,16},{28,4},{32,40},... | collective-permute-start | bytes 1179656 | tf_op jit(solution)/shard_map/ppermute | solution.py:51
  8.7 8.0 %collective-permute-start.6 = (f32[8,96,128]{2,1,0:T(8,128)S(1)}, f32[8,96,128]{2,1,0:T(8,128)S(1)}, u32[]{:S(2)}, u32[]{:S(2)}) collective-permute-start(f32[8,96,128]{2,1,0:T(8,128)S(1)} %spectra.13), channel_id=1, source_target_pairs={{0,4},{4,0},{1,5},{5,1},{2,6},{6,2},{3,7},{7,3},{8,12},{12,8},{9,1... | collective-permute-start | bytes 1179656 | tf_op jit(solution)/shard_map/ppermute | solution.py:55
  10.3 8.7 %collective-permute-start.1 = (f32[8,96,128]{2,1,0:T(8,128)S(1)}, f32[8,96,128]{2,1,0:T(8,128)S(1)}, u32[]{:S(2)}, u32[]{:S(2)}) collective-permute-start(f32[8,96,128]{2,1,0:T(8,128)S(1)} %add.63), channel_id=1, source_target_pairs={{0,8},{4,28},{8,0},{12,20},{16,24},{20,12},{24,16},{28,4},{32,40},... | collective-permute-start | bytes 1179656 | tf_op jit(solution)/shard_map/ppermute | solution.py:51
  13.9 5.9 %collective-permute-start.7 = (f32[4,96,128]{2,1,0:T(8,128)S(1)}, f32[4,96,128]{2,1,0:T(8,128)S(1)}, u32[]{:S(2)}, u32[]{:S(2)}) collective-permute-start(f32[4,96,128]{2,1,0:T(8,128)S(1)} %get-tuple-element.53), channel_id=1, source_target_pairs={{0,24},{4,12},{8,16},{12,4},{16,8},{20,28},{24,0},{28,20},{32,56},... | collective-permute-start | bytes 589832 | tf_op jit(solution)/shard_map/ppermute | solution.py:51
  15.9 8.6 %collective-permute-start.5 = (f32[4,96,128]{2,1,0:T(8,128)S(1)}, f32[4,96,128]{2,1,0:T(8,128)S(1)}, u32[]{:S(2)}, u32[]{:S(2)}) collective-permute-start(f32[4,96,128]{2,1,0:T(8,128)S(1)} %get-tuple-element.54), channel_id=1, source_target_pairs={{0,24},{4,12},{8,16},{12,4},{16,8},{20,28},{24,0},{28,20},{32,56},... | collective-permute-start | bytes 589832 | tf_op jit(solution)/shard_map/ppermute | solution.py:51
  19.8 5.4 %collective-permute-start.8 = (f32[2,96,128]{2,1,0:T(8,128)S(1)}, f32[2,96,128]{2,1,0:T(8,128)S(1)}, u32[]{:S(2)}, u32[]{:S(2)}) collective-permute-start(f32[2,96,128]{2,1,0:T(8,128)S(1)} %get-tuple-element.51), channel_id=1, source_target_pairs={{0,32},{4,36},{8,40},{12,44},{16,48},{20,52},{24,56},{28,60},{32,0... | collective-permute-start | bytes 294920 | tf_op jit(solution)/shard_map/ppermute | solution.py:51
  21.7 7.1 %collective-permute-start.9 = (f32[2,96,128]{2,1,0:T(8,128)S(1)}, f32[2,96,128]{2,1,0:T(8,128)S(1)}, u32[]{:S(2)}, u32[]{:S(2)}) collective-permute-start(f32[2,96,128]{2,1,0:T(8,128)S(1)} %get-tuple-element.52), channel_id=1, source_target_pairs={{0,96},{4,228},{8,104},{12,236},{16,112},{20,244},{24,120},{28,252... | collective-permute-start | bytes 294920 | tf_op jit(solution)/shard_map/ppermute | solution.py:51
  24.5 6.8 %collective-permute-start.10 = (f32[2,96,128]{2,1,0:T(8,128)S(1)}, f32[2,96,128]{2,1,0:T(8,128)S(1)}, u32[]{:S(2)}, u32[]{:S(2)}) collective-permute-start(f32[2,96,128]{2,1,0:T(8,128)S(1)} %added.1), channel_id=1, source_target_pairs={{0,64},{4,196},{8,72},{12,204},{16,80},{20,212},{24,88},{28,220},{... | collective-permute-start | bytes 294920 | tf_op jit(solution)/shard_map/ppermute | solution.py:51
  31.3 8.6 %collective-permute-start.11 = (f32[2,96,128]{2,1,0:T(8,128)S(1)}, f32[2,96,128]{2,1,0:T(8,128)S(1)}, u32[]{:S(2)}, u32[]{:S(2)}) collective-permute-start(f32[2,96,128]{2,1,0:T(8,128)S(1)} %fusion.2.a_ref), channel_id=1, source_target_pairs={{0,192},{4,68},{8,200},{12,76},{16,208},{20,84},{24,216},{28,92},{... | collective-permute-start | bytes 294920 | tf_op jit(solution)/shard_map/ppermute | solution.py:51
  40.1 4.9 %collective-permute-start.12 = (f32[2,32,128]{2,1,0:T(8,128)S(1)}, f32[2,32,128]{2,1,0:T(8,128)S(1)}, u32[]{:S(2)}, u32[]{:S(2)}) collective-permute-start(f32[2,32,128]{2,1,0:T(8,128)S(1)} %solve.1), channel_id=1, source_target_pairs={{0,64},{4,196},{8,72},{12,204},{16,80},{20,212},{24,88},{28,220},{... | collective-permute-start | bytes 98312 | tf_op jit(solution)/shard_map/ppermute | solution.py:51
  40.2 4.8 %collective-permute-start.13 = (f32[2,32,128]{2,1,0:T(8,128)S(1)}, f32[2,32,128]{2,1,0:T(8,128)S(1)}, u32[]{:S(2)}, u32[]{:S(2)}) collective-permute-start(f32[2,32,128]{2,1,0:T(8,128)S(1)} %solve.1), channel_id=1, source_target_pairs={{0,32},{4,36},{8,40},{12,44},{16,48},{20,52},{24,56},{28,60},{32,0... | collective-permute-start | bytes 98312 | tf_op jit(solution)/shard_map/ppermute | solution.py:51
  41.9 5.7 %collective-permute-start.14 = (f32[2,32,128]{2,1,0:T(8,128)S(1)}, f32[2,32,128]{2,1,0:T(8,128)S(1)}, u32[]{:S(2)}, u32[]{:S(2)}) collective-permute-start(f32[2,32,128]{2,1,0:T(8,128)S(1)} %solve.1), channel_id=1, source_target_pairs={{0,96},{4,228},{8,104},{12,236},{16,112},{20,244},{24,120},{28,252... | collective-permute-start | bytes 98312 | tf_op jit(solution)/shard_map/ppermute | solution.py:51
  47.7 7.0 %collective-permute-start.18 = (f32[8,32,128]{2,1,0:T(8,128)S(1)}, f32[8,32,128]{2,1,0:T(8,128)S(1)}, u32[]{:S(2)}, u32[]{:S(2)}) collective-permute-start(f32[8,32,128]{2,1,0:T(8,128)S(1)} %pad_maximum_fusion.refs_0_), channel_id=1, source_target_pairs={{0,8},{4,28},{8,0},{12,20},{16,24},{20,12},{24,16},{28,4},{32,40},... | collective-permute-start | bytes 393224 | tf_op jit(solution)/shard_map/ppermute | solution.py:51
  50.4 5.7 %collective-permute-start.16 = (f32[8,32,128]{2,1,0:T(8,128)S(1)}, f32[8,32,128]{2,1,0:T(8,128)S(1)}, u32[]{:S(2)}, u32[]{:S(2)}) collective-permute-start(f32[8,32,128]{2,1,0:T(8,128)S(1)} %pad_maximum_fusion.refs_0_), channel_id=1, source_target_pairs={{0,24},{4,12},{8,16},{12,4},{16,8},{20,28},{24,0},{28,20},{32,56},... | collective-permute-start | bytes 393224 | tf_op jit(solution)/shard_map/ppermute | solution.py:51
  52.2 6.5 %collective-permute-start.20 = (f32[8,32,128]{2,1,0:T(8,128)S(1)}, f32[8,32,128]{2,1,0:T(8,128)S(1)}, u32[]{:S(2)}, u32[]{:S(2)}) collective-permute-start(f32[8,32,128]{2,1,0:T(8,128)S(1)} %pad_maximum_fusion.refs_0_), channel_id=1, source_target_pairs={{0,16},{4,20},{8,24},{12,28},{16,0},{20,4},{24,8},{28,12},{32,48},... | collective-permute-start | bytes 393224 | tf_op jit(solution)/shard_map/ppermute | solution.py:51
  52.6 9.1 %collective-permute-start.15 = (f32[8,32,128]{2,1,0:T(8,128)S(1)}, f32[8,32,128]{2,1,0:T(8,128)S(1)}, u32[]{:S(2)}, u32[]{:S(2)}) collective-permute-start(f32[8,32,128]{2,1,0:T(8,128)S(1)} %pad_maximum_fusion.refs_0_), channel_id=1, source_target_pairs={{0,4},{4,0},{1,5},{5,1},{2,6},{6,2},{3,7},{7,3},{8,12},{12,8},{9,1... | collective-permute-start | bytes 393224 | tf_op jit(solution)/shard_map/ppermute | solution.py:55
  54.7 7.4 %collective-permute-start.19 = (f32[8,32,128]{2,1,0:T(8,128)S(1)}, f32[8,32,128]{2,1,0:T(8,128)S(1)}, u32[]{:S(2)}, u32[]{:S(2)}) collective-permute-start(f32[8,32,128]{2,1,0:T(8,128)S(1)} %collective-permute-done.18.refs_0_), channel_id=1, source_target_pairs={{0,4},{4,0},{1,5},{5,1},{2,6},{6,2},{3,7},{7,3},{8,12},{12,8},{9,1... | collective-permute-start | bytes 393224 | tf_op jit(solution)/shard_map/ppermute | solution.py:55
  56.0 6.4 %collective-permute-start.17 = (f32[8,32,128]{2,1,0:T(8,128)S(1)}, f32[8,32,128]{2,1,0:T(8,128)S(1)}, u32[]{:S(2)}, u32[]{:S(2)}) collective-permute-start(f32[8,32,128]{2,1,0:T(8,128)S(1)} %collective-permute-done.16.refs_0_), channel_id=1, source_target_pairs={{0,4},{4,0},{1,5},{5,1},{2,6},{6,2},{3,7},{7,3},{8,12},{12,8},{9,1... | collective-permute-start | bytes 393224 | tf_op jit(solution)/shard_map/ppermute | solution.py:55
  58.7 4.2 %collective-permute-start.21 = (f32[8,32,128]{2,1,0:T(8,128)S(1)}, f32[8,32,128]{2,1,0:T(8,128)S(1)}, u32[]{:S(2)}, u32[]{:S(2)}) collective-permute-start(f32[8,32,128]{2,1,0:T(8,128)S(1)} %collective-permute-done.20.refs_0_), channel_id=1, source_target_pairs={{0,4},{4,0},{1,5},{5,1},{2,6},{6,2},{3,7},{7,3},{8,12},{12,8},{9,1... | collective-permute-start | bytes 393224 | tf_op jit(solution)/shard_map/ppermute | solution.py:55
  63.4 5.5 %collective-permute-start.22 = (f32[8,128]{1,0:T(8,128)S(1)}, f32[8,128]{1,0:T(8,128)S(1)}, u32[]{:S(2)}, u32[]{:S(2)}) collective-permute-start(f32[8,128]{1,0:T(8,128)S(1)} %get-tuple-element.50), channel_id=1, source_target_pairs={{0,1},{1,0},{2,3},{3,2},{4,5},{5,4},{6,7},{7,6},{8,9},{9,8},{10,11... | collective-permute-start | bytes 12296 | tf_op jit(solution)/shard_map/ppermute | solution.py:400
  65.1 4.8 %collective-permute-start.23 = (f32[8,128]{1,0:T(8,128)S(1)}, f32[8,128]{1,0:T(8,128)S(1)}, u32[]{:S(2)}, u32[]{:S(2)}) collective-permute-start(f32[8,128]{1,0:T(8,128)S(1)} %get-tuple-element.50), channel_id=1, source_target_pairs={{0,3},{1,2},{2,1},{3,0},{4,7},{5,6},{6,5},{7,4},{8,11},{9,10},{10,... | collective-permute-start | bytes 12296 | tf_op jit(solution)/shard_map/ppermute | solution.py:400
  67.2 5.1 %collective-permute-start.24 = (f32[8,128]{1,0:T(8,128)S(1)}, f32[8,128]{1,0:T(8,128)S(1)}, u32[]{:S(2)}, u32[]{:S(2)}) collective-permute-start(f32[8,128]{1,0:T(8,128)S(1)} %get-tuple-element.50), channel_id=1, source_target_pairs={{0,2},{1,3},{2,0},{3,1},{4,6},{5,7},{6,4},{7,5},{8,10},{9,11},{10,... | collective-permute-start | bytes 12296 | tf_op jit(solution)/shard_map/ppermute | solution.py:400
  (2 other events, 3.7 us)

commit v6 on v5

--- a/solution.py
+++ b/solution.py
@@ -341,7 +341,7 @@
         out_ref[p, CH : 2 * CH, :] = imag
         return num + part
 
-    num = lax.fori_loop(0, count, step, jnp.zeros((CH, LANES), F32))
+    num = lax.fori_loop(0, count, step, jnp.zeros((CH, LANES), F32), unroll=2)
     for sum_ref in sums:
         num = num + sum_ref[...]
     if last:
@@ -350,8 +350,10 @@
         lane = lax.broadcasted_iota(jnp.int32, (CH, LANES), 1)
         total = jnp.broadcast_to(jnp.sum(num, axis=1, keepdims=True), (CH, LANES))
         total = jnp.sum(jnp.where(lane == sublane(), total, 0.0), axis=0, keepdims=True)
-        num = jnp.where(sublane() == 0, jnp.broadcast_to(total, (CH, LANES)), square)
-    num_ref[...] = num
+        num_ref[0:1, :] = total
+        num_ref[1:2, :] = jnp.full((1, LANES), square)
+    else:
+        num_ref[...] = num
 
 
 def clean(sizes, half, filters, rest, which, first, sums):
@@ -362,7 +364,7 @@
         lambda *refs: clean_body(sizes, half, which, first, count, last, *refs),
         out_shape=[
             jax.ShapeDtypeStruct((count, 2 * CH, LANES), F32),
-            jax.ShapeDtypeStruct((CH, LANES), F32),
+            jax.ShapeDtypeStruct((2 if last else CH, LANES), F32),
         ],
         in_specs=[pl.BlockSpec(memory_space=VMEM)] * len(args),
         out_specs=[pl.BlockSpec(memory_space=VMEM)] * 2,

time: 73.1 us -> 72.7 us (level)
  transfers between devices with their start and end apart: 25 -> 25, of which waited for: 14 -> 14; matrix products, arithmetic and copies ran while one was open for 2% -> 2% of each run, Pallas kernels for 12% -> 11%
where the time goes in v6:
time: 72.7 us; the launch traced here: 72.5 us
  starting transfers between devices  30.8 us (42%)
  waiting for transfers between devices  27.7 us (38%)
  Pallas kernels  11 us (15%)
  local copies, waits for them, and re-layouts  1.27 us (2%)
  other arithmetic  0.92 us (1%)
  between operations  0.85 us (1%)
    ppermute x14, starting transfers between devices, swap_steps(): return lax.ppermute(value, SEG, pairs)  25.3 us
    ppermute x14, waiting for transfers between devices, swap_steps(): return lax.ppermute(value, SEG, pairs)  24.2 us
    pallas_call x7, Pallas kernels, spectra(): pl.pallas_call(lambda *refs: spectra_body(sizes, half, which, first, coun...  4.9 us
    ppermute x3, starting transfers between devices, summed_over_bin(): got.append(lax.ppermute(value, 'y', flip_pairs('y', sizes['y'], 0, bits)))  4.57 us
    ppermute x3, waiting for transfers between devices, summed_over_bin(): got.append(lax.ppermute(value, 'y', flip_pairs('y', sizes['y'], 0, bits)))  3.43 us
    pallas_call x8, Pallas kernels, clean(): pl.pallas_call(lambda *refs: clean_body(sizes, half, which, first, count,...  2.85 us
    pallas_call x1, Pallas kernels, front(): pl.pallas_call(lambda *refs: front_body(sizes, half, first, count, *refs)...  2.11 us
  transfers between devices with their start and end apart: 25, of which 14 were waited for; matrix products, arithmetic and copies ran while one was open for 2% of the time, Pallas kernels for 11%

profile of v6, /device:TPU:2, one launch (start us, length us, event | category | flops | bytes accessed | tf_op | source)
XLA Modules:
  0.0 72.5 jit_solution(1910929633207414039)
XLA Ops:
  0.6 2.1 %front.1 = (f32[8,96,128]{2,1,0:T(8,128)S(1)}, f32[8,8,128]{2,1,0:T(8,128)S(1)}, bf16[8,8,8192]{2,1,0:T(8,128)(2,1)S(1)}, bf16[8,8,8192]{2,1,0:T(8,128)(2,1)S(1)...) custom-call(s32[8]{0:T(128)} %refs_0_.1, bf16[8,8,8192]{2,1,0:T(8,128)(2,1)} %refs_1_.1, ...), custom_call_target="tpu_custom_call" | custom-call | flops 4000000 | tf_op jit(solution)/shard_map/front/pallas_call | solution.py:171
  5.7 2.3 %collective-permute-start.3 = (f32[8,96,128]{2,1,0:T(8,128)S(1)}, f32[8,96,128]{2,1,0:T(8,128)S(1)}, u32[]{:S(2)}, u32[]{:S(2)}) collective-permute-start(f32[8,96,128]{2,1,0:T(8,128)S(1)} %add.64), channel_id=1, source_target_pairs={{0,8},{4,28},{8,0},{12,20},{16,24},{20,12},{24,16},{28,4},{32,40},... | collective-permute-start | bytes 1179656 | tf_op jit(solution)/shard_map/ppermute | solution.py:51
  10.3 1.3 %collective-permute-start.1 = (f32[8,96,128]{2,1,0:T(8,128)S(1)}, f32[8,96,128]{2,1,0:T(8,128)S(1)}, u32[]{:S(2)}, u32[]{:S(2)}) collective-permute-start(f32[8,96,128]{2,1,0:T(8,128)S(1)} %add.63), channel_id=1, source_target_pairs={{0,8},{4,28},{8,0},{12,20},{16,24},{20,12},{24,16},{28,4},{32,40},... | collective-permute-start | bytes 1179656 | tf_op jit(solution)/shard_map/ppermute | solution.py:51
  11.6 2.2 %collective-permute-done.3 = f32[8,96,128]{2,1,0:T(8,128)S(1)} collective-permute-done((f32[8,96,128]{2,1,0:T(8,128)S(1)}, f32[8,96,128]{2,1,0:T(8,128)S(1)}, u32[]{:S(2)}, u32[]{:S(2)}) %collective-permute-start.3) | collective-permute-done | bytes 393248 | tf_op jit(solution)/shard_map/ppermute | solution.py:51
  13.9 1.4 %collective-permute-start.7 = (f32[4,96,128]{2,1,0:T(8,128)S(1)}, f32[4,96,128]{2,1,0:T(8,128)S(1)}, u32[]{:S(2)}, u32[]{:S(2)}) collective-permute-start(f32[4,96,128]{2,1,0:T(8,128)S(1)} %get-tuple-element.53), channel_id=1, source_target_pairs={{0,24},{4,12},{8,16},{12,4},{16,8},{20,28},{24,0},{28,20},{32,56},... | collective-permute-start | bytes 589832 | tf_op jit(solution)/shard_map/ppermute | solution.py:51
  16.8 2.3 %collective-permute-done.1.refs_0_ = f32[8,96,128]{2,1,0:T(8,128)S(1)} collective-permute-done((f32[8,96,128]{2,1,0:T(8,128)S(1)}, f32[8,96,128]{2,1,0:T(8,128)S(1)}, u32[]{:S(2)}, u32[]{:S(2)}) %collective-permute-start.1) | collective-permute-done | bytes 393248 | tf_op jit(solution)/shard_map/ppermute | solution.py:51
  19.8 1.8 %collective-permute-start.8 = (f32[2,96,128]{2,1,0:T(8,128)S(1)}, f32[2,96,128]{2,1,0:T(8,128)S(1)}, u32[]{:S(2)}, u32[]{:S(2)}) collective-permute-start(f32[2,96,128]{2,1,0:T(8,128)S(1)} %get-tuple-element.51), channel_id=1, source_target_pairs={{0,32},{4,36},{8,40},{12,44},{16,48},{20,52},{24,56},{28,60},{32,0... | collective-permute-start | bytes 294920 | tf_op jit(solution)/shard_map/ppermute | solution.py:51
  21.7 2.8 %collective-permute-start.9 = (f32[2,96,128]{2,1,0:T(8,128)S(1)}, f32[2,96,128]{2,1,0:T(8,128)S(1)}, u32[]{:S(2)}, u32[]{:S(2)}) collective-permute-start(f32[2,96,128]{2,1,0:T(8,128)S(1)} %get-tuple-element.52), channel_id=1, source_target_pairs={{0,96},{4,228},{8,104},{12,236},{16,112},{20,244},{24,120},{28,252... | collective-permute-start | bytes 294920 | tf_op jit(solution)/shard_map/ppermute | solution.py:51
  25.2 3.5 %collective-permute-done.9 = f32[2,96,128]{2,1,0:T(8,128)S(1)} collective-permute-done((f32[2,96,128]{2,1,0:T(8,128)S(1)}, f32[2,96,128]{2,1,0:T(8,128)S(1)}, u32[]{:S(2)}, u32[]{:S(2)}) %collective-permute-start.9) | collective-permute-done | bytes 98336 | tf_op jit(solution)/shard_map/ppermute | solution.py:51
  28.8 2.5 %collective-permute-done.10 = f32[2,96,128]{2,1,0:T(8,128)S(1)} collective-permute-done((f32[2,96,128]{2,1,0:T(8,128)S(1)}, f32[2,96,128]{2,1,0:T(8,128)S(1)}, u32[]{:S(2)}, u32[]{:S(2)}) %collective-permute-start.10) | collective-permute-done | bytes 98336 | tf_op jit(solution)/shard_map/ppermute | solution.py:51
  31.3 5.0 %collective-permute-start.11 = (f32[2,96,128]{2,1,0:T(8,128)S(1)}, f32[2,96,128]{2,1,0:T(8,128)S(1)}, u32[]{:S(2)}, u32[]{:S(2)}) collective-permute-start(f32[2,96,128]{2,1,0:T(8,128)S(1)} %fusion.2.a_ref), channel_id=1, source_target_pairs={{0,192},{4,68},{8,200},{12,76},{16,208},{20,84},{24,216},{28,92},{... | collective-permute-start | bytes 294920 | tf_op jit(solution)/shard_map/ppermute | solution.py:51
  36.3 3.6 %collective-permute-done.11.b_ref = f32[2,96,128]{2,1,0:T(8,128)S(1)} collective-permute-done((f32[2,96,128]{2,1,0:T(8,128)S(1)}, f32[2,96,128]{2,1,0:T(8,128)S(1)}, u32[]{:S(2)}, u32[]{:S(2)}) %collective-permute-start.11) | collective-permute-done | bytes 98336 | tf_op jit(solution)/shard_map/ppermute | solution.py:51
  40.2 1.7 %collective-permute-start.13 = (f32[2,32,128]{2,1,0:T(8,128)S(1)}, f32[2,32,128]{2,1,0:T(8,128)S(1)}, u32[]{:S(2)}, u32[]{:S(2)}) collective-permute-start(f32[2,32,128]{2,1,0:T(8,128)S(1)} %solve.1), channel_id=1, source_target_pairs={{0,32},{4,36},{8,40},{12,44},{16,48},{20,52},{24,56},{28,60},{32,0... | collective-permute-start | bytes 98312 | tf_op jit(solution)/shard_map/ppermute | solution.py:51
  41.9 2.7 %collective-permute-start.14 = (f32[2,32,128]{2,1,0:T(8,128)S(1)}, f32[2,32,128]{2,1,0:T(8,128)S(1)}, u32[]{:S(2)}, u32[]{:S(2)}) collective-permute-start(f32[2,32,128]{2,1,0:T(8,128)S(1)} %solve.1), channel_id=1, source_target_pairs={{0,96},{4,228},{8,104},{12,236},{16,112},{20,244},{24,120},{28,252... | collective-permute-start | bytes 98312 | tf_op jit(solution)/shard_map/ppermute | solution.py:51
  45.0 2.6 %collective-permute-done.14 = f32[2,32,128]{2,1,0:T(8,128)S(1)} collective-permute-done((f32[2,32,128]{2,1,0:T(8,128)S(1)}, f32[2,32,128]{2,1,0:T(8,128)S(1)}, u32[]{:S(2)}, u32[]{:S(2)}) %collective-permute-start.14) | collective-permute-done | bytes 32800 | tf_op jit(solution)/shard_map/ppermute | solution.py:51
  47.7 2.7 %collective-permute-start.18 = (f32[8,32,128]{2,1,0:T(8,128)S(1)}, f32[8,32,128]{2,1,0:T(8,128)S(1)}, u32[]{:S(2)}, u32[]{:S(2)}) collective-permute-start(f32[8,32,128]{2,1,0:T(8,128)S(1)} %pad_maximum_fusion.refs_0_), channel_id=1, source_target_pairs={{0,8},{4,28},{8,0},{12,20},{16,24},{20,12},{24,16},{28,4},{32,40},... | collective-permute-start | bytes 393224 | tf_op jit(solution)/shard_map/ppermute | solution.py:51
  50.4 1.8 %collective-permute-start.16 = (f32[8,32,128]{2,1,0:T(8,128)S(1)}, f32[8,32,128]{2,1,0:T(8,128)S(1)}, u32[]{:S(2)}, u32[]{:S(2)}) collective-permute-start(f32[8,32,128]{2,1,0:T(8,128)S(1)} %pad_maximum_fusion.refs_0_), channel_id=1, source_target_pairs={{0,24},{4,12},{8,16},{12,4},{16,8},{20,28},{24,0},{28,20},{32,56},... | collective-permute-start | bytes 393224 | tf_op jit(solution)/shard_map/ppermute | solution.py:51
  52.6 2.1 %collective-permute-done.18.refs_0_ = f32[8,32,128]{2,1,0:T(8,128)S(1)} collective-permute-done((f32[8,32,128]{2,1,0:T(8,128)S(1)}, f32[8,32,128]{2,1,0:T(8,128)S(1)}, u32[]{:S(2)}, u32[]{:S(2)}) %collective-permute-start.18) | collective-permute-done | bytes 131104 | tf_op jit(solution)/shard_map/ppermute | solution.py:51
  54.7 1.4 %collective-permute-done.16.refs_0_ = f32[8,32,128]{2,1,0:T(8,128)S(1)} collective-permute-done((f32[8,32,128]{2,1,0:T(8,128)S(1)}, f32[8,32,128]{2,1,0:T(8,128)S(1)}, u32[]{:S(2)}, u32[]{:S(2)}) %collective-permute-start.16) | collective-permute-done | bytes 131104 | tf_op jit(solution)/shard_map/ppermute | solution.py:51
  56.1 2.6 %collective-permute-done.20.refs_0_ = f32[8,32,128]{2,1,0:T(8,128)S(1)} collective-permute-done((f32[8,32,128]{2,1,0:T(8,128)S(1)}, f32[8,32,128]{2,1,0:T(8,128)S(1)}, u32[]{:S(2)}, u32[]{:S(2)}) %collective-permute-start.20) | collective-permute-done | bytes 131104 | tf_op jit(solution)/shard_map/ppermute | solution.py:51
  63.0 1.7 %collective-permute-start.22 = (f32[2,128]{1,0:T(2,128)S(1)}, f32[2,128]{1,0:T(2,128)S(1)}, u32[]{:S(2)}, u32[]{:S(2)}) collective-permute-start(f32[2,128]{1,0:T(2,128)S(1)} %get-tuple-element.50), channel_id=1, source_target_pairs={{0,1},{1,0},{2,3},{3,2},{4,5},{5,4},{6,7},{7,6},{8,9},{9,8},{10,11... | collective-permute-start | bytes 3080 | tf_op jit(solution)/shard_map/ppermute | solution.py:402
  64.7 2.2 %collective-permute-start.23 = (f32[2,128]{1,0:T(2,128)S(1)}, f32[2,128]{1,0:T(2,128)S(1)}, u32[]{:S(2)}, u32[]{:S(2)}) collective-permute-start(f32[2,128]{1,0:T(2,128)S(1)} %get-tuple-element.50), channel_id=1, source_target_pairs={{0,3},{1,2},{2,1},{3,0},{4,7},{5,6},{6,5},{7,4},{8,11},{9,10},{10,... | collective-permute-start | bytes 3080 | tf_op jit(solution)/shard_map/ppermute | solution.py:402
  68.5 1.0 %collective-permute-done.23 = f32[2,128]{1,0:T(2,128)S(1)} collective-permute-done((f32[2,128]{1,0:T(2,128)S(1)}, f32[2,128]{1,0:T(2,128)S(1)}, u32[]{:S(2)}, u32[]{:S(2)}) %collective-permute-start.23) | collective-permute-done | bytes 1056 | tf_op jit(solution)/shard_map/ppermute | solution.py:402
  69.5 2.5 %collective-permute-done.24 = f32[2,128]{1,0:T(2,128)S(1)} collective-permute-done((f32[2,128]{1,0:T(2,128)S(1)}, f32[2,128]{1,0:T(2,128)S(1)}, u32[]{:S(2)}, u32[]{:S(2)}) %collective-permute-start.24) | collective-permute-done | bytes 1056 | tf_op jit(solution)/shard_map/ppermute | solution.py:402
  (58 shorter events, 15.9 us)
Async XLA Ops:
  3.6 8.0 %collective-permute-start.4 = (f32[8,96,128]{2,1,0:T(8,128)S(1)}, f32[8,96,128]{2,1,0:T(8,128)S(1)}, u32[]{:S(2)}, u32[]{:S(2)}) collective-permute-start(f32[8,96,128]{2,1,0:T(8,128)S(1)} %spectra.11), channel_id=1, source_target_pairs={{0,4},{4,0},{1,5},{5,1},{2,6},{6,2},{3,7},{7,3},{8,12},{12,8},{9,1... | collective-permute-start | bytes 1179656 | tf_op jit(solution)/shard_map/ppermute | solution.py:55
  4.8 5.5 %collective-permute-start = (f32[8,96,128]{2,1,0:T(8,128)S(1)}, f32[8,96,128]{2,1,0:T(8,128)S(1)}, u32[]{:S(2)}, u32[]{:S(2)}) collective-permute-start(f32[8,96,128]{2,1,0:T(8,128)S(1)} %spectra.8), channel_id=1, source_target_pairs={{0,4},{4,0},{1,5},{5,1},{2,6},{6,2},{3,7},{7,3},{8,12},{12,8},{9,1... | collective-permute-start | bytes 1179656 | tf_op jit(solution)/shard_map/ppermute | solution.py:55
  5.7 8.1 %collective-permute-start.3 = (f32[8,96,128]{2,1,0:T(8,128)S(1)}, f32[8,96,128]{2,1,0:T(8,128)S(1)}, u32[]{:S(2)}, u32[]{:S(2)}) collective-permute-start(f32[8,96,128]{2,1,0:T(8,128)S(1)} %add.64), channel_id=1, source_target_pairs={{0,8},{4,28},{8,0},{12,20},{16,24},{20,12},{24,16},{28,4},{32,40},... | collective-permute-start | bytes 1179656 | tf_op jit(solution)/shard_map/ppermute | solution.py:51
  8.7 8.0 %collective-permute-start.6 = (f32[8,96,128]{2,1,0:T(8,128)S(1)}, f32[8,96,128]{2,1,0:T(8,128)S(1)}, u32[]{:S(2)}, u32[]{:S(2)}) collective-permute-start(f32[8,96,128]{2,1,0:T(8,128)S(1)} %spectra.13), channel_id=1, source_target_pairs={{0,4},{4,0},{1,5},{5,1},{2,6},{6,2},{3,7},{7,3},{8,12},{12,8},{9,1... | collective-permute-start | bytes 1179656 | tf_op jit(solution)/shard_map/ppermute | solution.py:55
  10.3 8.7 %collective-permute-start.1 = (f32[8,96,128]{2,1,0:T(8,128)S(1)}, f32[8,96,128]{2,1,0:T(8,128)S(1)}, u32[]{:S(2)}, u32[]{:S(2)}) collective-permute-start(f32[8,96,128]{2,1,0:T(8,128)S(1)} %add.63), channel_id=1, source_target_pairs={{0,8},{4,28},{8,0},{12,20},{16,24},{20,12},{24,16},{28,4},{32,40},... | collective-permute-start | bytes 1179656 | tf_op jit(solution)/shard_map/ppermute | solution.py:51
  13.9 5.9 %collective-permute-start.7 = (f32[4,96,128]{2,1,0:T(8,128)S(1)}, f32[4,96,128]{2,1,0:T(8,128)S(1)}, u32[]{:S(2)}, u32[]{:S(2)}) collective-permute-start(f32[4,96,128]{2,1,0:T(8,128)S(1)} %get-tuple-element.53), channel_id=1, source_target_pairs={{0,24},{4,12},{8,16},{12,4},{16,8},{20,28},{24,0},{28,20},{32,56},... | collective-permute-start | bytes 589832 | tf_op jit(solution)/shard_map/ppermute | solution.py:51
  15.9 8.6 %collective-permute-start.5 = (f32[4,96,128]{2,1,0:T(8,128)S(1)}, f32[4,96,128]{2,1,0:T(8,128)S(1)}, u32[]{:S(2)}, u32[]{:S(2)}) collective-permute-start(f32[4,96,128]{2,1,0:T(8,128)S(1)} %get-tuple-element.54), channel_id=1, source_target_pairs={{0,24},{4,12},{8,16},{12,4},{16,8},{20,28},{24,0},{28,20},{32,56},... | collective-permute-start | bytes 589832 | tf_op jit(solution)/shard_map/ppermute | solution.py:51
  19.8 5.4 %collective-permute-start.8 = (f32[2,96,128]{2,1,0:T(8,128)S(1)}, f32[2,96,128]{2,1,0:T(8,128)S(1)}, u32[]{:S(2)}, u32[]{:S(2)}) collective-permute-start(f32[2,96,128]{2,1,0:T(8,128)S(1)} %get-tuple-element.51), channel_id=1, source_target_pairs={{0,32},{4,36},{8,40},{12,44},{16,48},{20,52},{24,56},{28,60},{32,0... | collective-permute-start | bytes 294920 | tf_op jit(solution)/shard_map/ppermute | solution.py:51
  21.7 7.1 %collective-permute-start.9 = (f32[2,96,128]{2,1,0:T(8,128)S(1)}, f32[2,96,128]{2,1,0:T(8,128)S(1)}, u32[]{:S(2)}, u32[]{:S(2)}) collective-permute-start(f32[2,96,128]{2,1,0:T(8,128)S(1)} %get-tuple-element.52), channel_id=1, source_target_pairs={{0,96},{4,228},{8,104},{12,236},{16,112},{20,244},{24,120},{28,252... | collective-permute-start | bytes 294920 | tf_op jit(solution)/shard_map/ppermute | solution.py:51
  24.5 6.8 %collective-permute-start.10 = (f32[2,96,128]{2,1,0:T(8,128)S(1)}, f32[2,96,128]{2,1,0:T(8,128)S(1)}, u32[]{:S(2)}, u32[]{:S(2)}) collective-permute-start(f32[2,96,128]{2,1,0:T(8,128)S(1)} %added.1), channel_id=1, source_target_pairs={{0,64},{4,196},{8,72},{12,204},{16,80},{20,212},{24,88},{28,220},{... | collective-permute-start | bytes 294920 | tf_op jit(solution)/shard_map/ppermute | solution.py:51
  31.3 8.6 %collective-permute-start.11 = (f32[2,96,128]{2,1,0:T(8,128)S(1)}, f32[2,96,128]{2,1,0:T(8,128)S(1)}, u32[]{:S(2)}, u32[]{:S(2)}) collective-permute-start(f32[2,96,128]{2,1,0:T(8,128)S(1)} %fusion.2.a_ref), channel_id=1, source_target_pairs={{0,192},{4,68},{8,200},{12,76},{16,208},{20,84},{24,216},{28,92},{... | collective-permute-start | bytes 294920 | tf_op jit(solution)/shard_map/ppermute | solution.py:51
  40.1 4.9 %collective-permute-start.12 = (f32[2,32,128]{2,1,0:T(8,128)S(1)}, f32[2,32,128]{2,1,0:T(8,128)S(1)}, u32[]{:S(2)}, u32[]{:S(2)}) collective-permute-start(f32[2,32,128]{2,1,0:T(8,128)S(1)} %solve.1), channel_id=1, source_target_pairs={{0,64},{4,196},{8,72},{12,204},{16,80},{20,212},{24,88},{28,220},{... | collective-permute-start | bytes 98312 | tf_op jit(solution)/shard_map/ppermute | solution.py:51
  40.2 4.8 %collective-permute-start.13 = (f32[2,32,128]{2,1,0:T(8,128)S(1)}, f32[2,32,128]{2,1,0:T(8,128)S(1)}, u32[]{:S(2)}, u32[]{:S(2)}) collective-permute-start(f32[2,32,128]{2,1,0:T(8,128)S(1)} %solve.1), channel_id=1, source_target_pairs={{0,32},{4,36},{8,40},{12,44},{16,48},{20,52},{24,56},{28,60},{32,0... | collective-permute-start | bytes 98312 | tf_op jit(solution)/shard_map/ppermute | solution.py:51
  41.9 5.7 %collective-permute-start.14 = (f32[2,32,128]{2,1,0:T(8,128)S(1)}, f32[2,32,128]{2,1,0:T(8,128)S(1)}, u32[]{:S(2)}, u32[]{:S(2)}) collective-permute-start(f32[2,32,128]{2,1,0:T(8,128)S(1)} %solve.1), channel_id=1, source_target_pairs={{0,96},{4,228},{8,104},{12,236},{16,112},{20,244},{24,120},{28,252... | collective-permute-start | bytes 98312 | tf_op jit(solution)/shard_map/ppermute | solution.py:51
  47.7 7.0 %collective-permute-start.18 = (f32[8,32,128]{2,1,0:T(8,128)S(1)}, f32[8,32,128]{2,1,0:T(8,128)S(1)}, u32[]{:S(2)}, u32[]{:S(2)}) collective-permute-start(f32[8,32,128]{2,1,0:T(8,128)S(1)} %pad_maximum_fusion.refs_0_), channel_id=1, source_target_pairs={{0,8},{4,28},{8,0},{12,20},{16,24},{20,12},{24,16},{28,4},{32,40},... | collective-permute-start | bytes 393224 | tf_op jit(solution)/shard_map/ppermute | solution.py:51
  50.4 5.7 %collective-permute-start.16 = (f32[8,32,128]{2,1,0:T(8,128)S(1)}, f32[8,32,128]{2,1,0:T(8,128)S(1)}, u32[]{:S(2)}, u32[]{:S(2)}) collective-permute-start(f32[8,32,128]{2,1,0:T(8,128)S(1)} %pad_maximum_fusion.refs_0_), channel_id=1, source_target_pairs={{0,24},{4,12},{8,16},{12,4},{16,8},{20,28},{24,0},{28,20},{32,56},... | collective-permute-start | bytes 393224 | tf_op jit(solution)/shard_map/ppermute | solution.py:51
  52.2 6.5 %collective-permute-start.20 = (f32[8,32,128]{2,1,0:T(8,128)S(1)}, f32[8,32,128]{2,1,0:T(8,128)S(1)}, u32[]{:S(2)}, u32[]{:S(2)}) collective-permute-start(f32[8,32,128]{2,1,0:T(8,128)S(1)} %pad_maximum_fusion.refs_0_), channel_id=1, source_target_pairs={{0,16},{4,20},{8,24},{12,28},{16,0},{20,4},{24,8},{28,12},{32,48},... | collective-permute-start | bytes 393224 | tf_op jit(solution)/shard_map/ppermute | solution.py:51
  52.6 8.9 %collective-permute-start.15 = (f32[8,32,128]{2,1,0:T(8,128)S(1)}, f32[8,32,128]{2,1,0:T(8,128)S(1)}, u32[]{:S(2)}, u32[]{:S(2)}) collective-permute-start(f32[8,32,128]{2,1,0:T(8,128)S(1)} %pad_maximum_fusion.refs_0_), channel_id=1, source_target_pairs={{0,4},{4,0},{1,5},{5,1},{2,6},{6,2},{3,7},{7,3},{8,12},{12,8},{9,1... | collective-permute-start | bytes 393224 | tf_op jit(solution)/shard_map/ppermute | solution.py:55
  54.7 7.1 %collective-permute-start.19 = (f32[8,32,128]{2,1,0:T(8,128)S(1)}, f32[8,32,128]{2,1,0:T(8,128)S(1)}, u32[]{:S(2)}, u32[]{:S(2)}) collective-permute-start(f32[8,32,128]{2,1,0:T(8,128)S(1)} %collective-permute-done.18.refs_0_), channel_id=1, source_target_pairs={{0,4},{4,0},{1,5},{5,1},{2,6},{6,2},{3,7},{7,3},{8,12},{12,8},{9,1... | collective-permute-start | bytes 393224 | tf_op jit(solution)/shard_map/ppermute | solution.py:55
  56.0 6.1 %collective-permute-start.17 = (f32[8,32,128]{2,1,0:T(8,128)S(1)}, f32[8,32,128]{2,1,0:T(8,128)S(1)}, u32[]{:S(2)}, u32[]{:S(2)}) collective-permute-start(f32[8,32,128]{2,1,0:T(8,128)S(1)} %collective-permute-done.16.refs_0_), channel_id=1, source_target_pairs={{0,4},{4,0},{1,5},{5,1},{2,6},{6,2},{3,7},{7,3},{8,12},{12,8},{9,1... | collective-permute-start | bytes 393224 | tf_op jit(solution)/shard_map/ppermute | solution.py:55
  58.7 3.9 %collective-permute-start.21 = (f32[8,32,128]{2,1,0:T(8,128)S(1)}, f32[8,32,128]{2,1,0:T(8,128)S(1)}, u32[]{:S(2)}, u32[]{:S(2)}) collective-permute-start(f32[8,32,128]{2,1,0:T(8,128)S(1)} %collective-permute-done.20.refs_0_), channel_id=1, source_target_pairs={{0,4},{4,0},{1,5},{5,1},{2,6},{6,2},{3,7},{7,3},{8,12},{12,8},{9,1... | collective-permute-start | bytes 393224 | tf_op jit(solution)/shard_map/ppermute | solution.py:55
  63.0 5.5 %collective-permute-start.22 = (f32[2,128]{1,0:T(2,128)S(1)}, f32[2,128]{1,0:T(2,128)S(1)}, u32[]{:S(2)}, u32[]{:S(2)}) collective-permute-start(f32[2,128]{1,0:T(2,128)S(1)} %get-tuple-element.50), channel_id=1, source_target_pairs={{0,1},{1,0},{2,3},{3,2},{4,5},{5,4},{6,7},{7,6},{8,9},{9,8},{10,11... | collective-permute-start | bytes 3080 | tf_op jit(solution)/shard_map/ppermute | solution.py:402
  64.7 4.8 %collective-permute-start.23 = (f32[2,128]{1,0:T(2,128)S(1)}, f32[2,128]{1,0:T(2,128)S(1)}, u32[]{:S(2)}, u32[]{:S(2)}) collective-permute-start(f32[2,128]{1,0:T(2,128)S(1)} %get-tuple-element.50), channel_id=1, source_target_pairs={{0,3},{1,2},{2,1},{3,0},{4,7},{5,6},{6,5},{7,4},{8,11},{9,10},{10,... | collective-permute-start | bytes 3080 | tf_op jit(solution)/shard_map/ppermute | solution.py:402
  66.9 5.1 %collective-permute-start.24 = (f32[2,128]{1,0:T(2,128)S(1)}, f32[2,128]{1,0:T(2,128)S(1)}, u32[]{:S(2)}, u32[]{:S(2)}) collective-permute-start(f32[2,128]{1,0:T(2,128)S(1)} %get-tuple-element.50), channel_id=1, source_target_pairs={{0,2},{1,3},{2,0},{3,1},{4,6},{5,7},{6,4},{7,5},{8,10},{9,11},{10,... | collective-permute-start | bytes 3080 | tf_op jit(solution)/shard_map/ppermute | solution.py:402
  (2 other events, 3.7 us)
